TPU v7x, 128 devices: a whole 4x4x4 slice. The times are simulated.
128 devices in a mesh: blk: 16 (over z, x_hi, core), uly: 8 (over y, x_lo).
Axes of the slice: x: 4 (x_hi: 2, x_lo: 2; x = x_hi * 2 + x_lo), y: 4, z: 4, core: 2. Of those that a mesh axis runs over, the one named last changes fastest.
Arguments:
- queries: bfloat16 [2048, 128, 128], P(('blk', 'uly')), may hold values from -8 to 8
- query_tangents: bfloat16 [2048, 128, 4, 128], P(('blk', 'uly')), may hold values from -6 to 6
- keys: bfloat16 [2048, 8, 128], P(('blk', 'uly')), may hold values from -8 to 8
- key_tangents: bfloat16 [2048, 8, 4, 128], P(('blk', 'uly')), may hold values from -6 to 6
- values: bfloat16 [2048, 8, 128], P(('blk', 'uly')), may hold values from -6 to 6
- value_tangents: bfloat16 [2048, 8, 4, 128], P(('blk', 'uly')), may hold values from -6 to 6
- span_order: int32 [32], replicated, may hold values from 0 to 31, as said below
Outputs:
- attention_out: bfloat16 [2048, 128, 128], P(('blk', 'uly'))
- tangent_out: bfloat16 [2048, 128, 4, 128], P(('blk', 'uly'))
Inputs may be any that keep to these rules, and one draw needn't show every extreme that they name: span_order is a permutation of the span positions; for every b the stored spans 2 * b and 2 * b + 1 hold positions c and 31 - c for some c.
All inputs are finite; a program needn't handle non-finite values.
Results may differ from a plain program's by a relative error of at most 0.0055.
Values may be sent and summed in bfloat16 or wider, within the bound.
No kernel may reach another device: no remote copies, remote signals or barrier semaphores. Data moves between devices by JAX's collectives and lax.ppermute only.
A program may use at most 64 MiB of HBM per device.

v0:
```python
import math

import jax
import jax.numpy as jnp
from jax import lax
from jax.sharding import PartitionSpec as P

HQ = 128
KVH = 8


def in_one_piece(arrays, axis, split_dim, concat_dim, along):
    widths = [math.prod(a.shape[along:]) for a in arrays]
    both = jnp.concatenate(
        [a.reshape(*a.shape[:along], w) for a, w in zip(arrays, widths)], axis=along
    )
    out = lax.all_to_all(both, axis, split_axis=split_dim, concat_axis=concat_dim, tiled=True)
    parts = jnp.split(out, [sum(widths[:k]) for k in range(1, len(widths))], axis=along)
    return tuple((b.reshape(*out.shape[:along], *a.shape[along:]) for a, b in zip(arrays, parts)))


def sent_together(arrays, axis, dim, along):
    columns = [a.reshape(*a.shape[:along], -1) for a in arrays]
    both = jnp.concatenate(columns, axis=along)
    out, at, finished = (lax.all_gather(both, axis, axis=dim, tiled=True), 0, [])
    for a, column in zip(arrays, columns):
        slab = out[..., at : at + column.shape[along]]
        finished.append(slab.reshape(*slab.shape[:along], *a.shape[along:]))
        at += column.shape[along]
    return tuple(finished)


def positions(stored, span_order, span_rows):
    span_ids = stored // span_rows
    table_ids = jnp.arange(span_order.shape[0], dtype=jnp.int32)
    looked_up = jnp.sum(
        jnp.where(span_ids[:, None] == table_ids[None, :], span_order[None, :], 0), axis=1
    )
    return looked_up * span_rows + stored % span_rows


def per_device(queries, query_tangents, keys, key_tangents, values, value_tangents, span_order):
    local_queries, local_tangents = (
        lax.all_to_all(queries, "uly", split_axis=1, concat_axis=0, tiled=True),
        lax.all_to_all(query_tangents, "uly", split_axis=1, concat_axis=0, tiled=True),
    )
    query_rows = local_queries.shape[0]
    span_rows = query_rows // 2
    head_size = local_queries.shape[2]
    group = HQ // KVH
    kv_local = local_queries.shape[1] // group
    probes = local_tangents.shape[2]
    scaling = head_size ** (-0.5)
    stored = lax.axis_index("blk") * query_rows + jnp.arange(query_rows, dtype=jnp.int32)
    query_places = positions(stored, span_order, span_rows)
    latest = jnp.max(query_places)
    query_heads = jnp.transpose(
        local_queries.reshape(query_rows, kv_local, group, head_size), (1, 2, 0, 3)
    )
    tangent_heads = jnp.transpose(
        local_tangents.reshape(query_rows, kv_local, group, probes, head_size), (1, 2, 3, 0, 4)
    )

    def update(carry, block):
        key_block, key_tan, value_block, value_tan, key_places = block
        running_max, totals, primal_sums, tangent_sums, shifts = carry
        visible = key_places[None, :] <= query_places[:, None]
        scores = (
            jnp.einsum("grqd,kgd->grqk", query_heads, key_block, preferred_element_type=jnp.float32)
            * scaling
        )
        scores = jnp.where(visible[None, None], scores, -1e30)
        new_max = jnp.maximum(running_max, jnp.max(scores, axis=-1))
        rescale = jnp.exp(running_max - new_max)
        weights_full = jnp.where(visible[None, None], jnp.exp(scores - new_max[..., None]), 0.0)
        weights_half = weights_full.astype(jnp.bfloat16)
        score_tan = jnp.einsum(
            "grpqd,kgd->grpqk", tangent_heads, key_block, preferred_element_type=jnp.float32
        )
        score_tan = score_tan + jnp.einsum(
            "grqd,kgpd->grpqk", query_heads, key_tan, preferred_element_type=jnp.float32
        )
        weighted = weights_full[:, :, None] * (score_tan * scaling)
        totals = totals * rescale + jnp.sum(weights_full, axis=-1)
        primal_sums = primal_sums * rescale[..., None] + jnp.einsum(
            "grqk,kgd->grqd", weights_half, value_block, preferred_element_type=jnp.float32
        )
        shifts = shifts * rescale[:, :, None] + jnp.sum(weighted, axis=-1)
        tangent_sums = tangent_sums * rescale[:, :, None, :, None]
        tangent_sums = tangent_sums + jnp.einsum(
            "grpqk,kgd->grpqd",
            weighted.astype(jnp.bfloat16),
            value_block,
            preferred_element_type=jnp.float32,
        )
        tangent_sums = tangent_sums + jnp.einsum(
            "grqk,kgpd->grpqd", weights_half, value_tan, preferred_element_type=jnp.float32
        )
        return (new_max, totals, primal_sums, tangent_sums, shifts)

    def keep_state(carry, block):
        return carry

    def visit(carry, block):
        reachable = jnp.min(block[4]) <= latest
        return (lax.cond(reachable, update, keep_state, carry, block), None)

    initial = (
        jnp.full((kv_local, group, query_rows), -1e30, jnp.float32),
        jnp.zeros((kv_local, group, query_rows), jnp.float32),
        jnp.zeros((kv_local, group, query_rows, head_size), jnp.float32),
        jnp.zeros((kv_local, group, probes, query_rows, head_size), jnp.float32),
        jnp.zeros((kv_local, group, probes, query_rows), jnp.float32),
    )
    head_keys, head_key_tan, head_values, head_value_tan = in_one_piece(
        (keys, key_tangents, values, value_tangents), "uly", 1, 0, 2
    )
    carry = initial
    key_piece, key_tan_piece, value_piece, value_tan_piece = sent_together(
        (head_keys, head_key_tan, head_values, head_value_tan), "blk", 0, 2
    )
    piece_rows = key_piece.shape[0]
    block_rows = 256
    block_total = piece_rows // block_rows
    places = positions(jnp.arange(piece_rows, dtype=jnp.int32), span_order, span_rows)
    stacked = (
        key_piece.reshape(block_total, block_rows, kv_local, head_size),
        key_tan_piece.reshape(block_total, block_rows, kv_local, probes, head_size),
        value_piece.reshape(block_total, block_rows, kv_local, head_size),
        value_tan_piece.reshape(block_total, block_rows, kv_local, probes, head_size),
        places.reshape(block_total, block_rows),
    )
    carry, unused = lax.scan(visit, carry, stacked)
    running_max, totals, primal_sums, tangent_sums, shifts = carry
    primal = primal_sums / totals[..., None]
    tangent = (
        tangent_sums / totals[:, :, None, :, None]
        - primal[:, :, None] * (shifts / totals[:, :, None])[..., None]
    )
    output_rows = jnp.transpose(primal.astype(jnp.bfloat16), (2, 0, 1, 3)).reshape(
        query_rows, kv_local * group, head_size
    )
    tangent_rows = jnp.transpose(tangent.astype(jnp.bfloat16), (3, 0, 1, 2, 4)).reshape(
        query_rows, kv_local * group, probes, head_size
    )
    attention_out, tangent_out = (
        lax.all_to_all(output_rows, "uly", split_axis=0, concat_axis=1, tiled=True),
        lax.all_to_all(tangent_rows, "uly", split_axis=0, concat_axis=1, tiled=True),
    )
    return (attention_out, tangent_out)


def solution(mesh):
    placed = (
        P(("blk", "uly"), None, None),
        P(("blk", "uly"), None, None, None),
        P(("blk", "uly"), None, None),
        P(("blk", "uly"), None, None, None),
        P(("blk", "uly"), None, None),
        P(("blk", "uly"), None, None, None),
        P(),
    )
    return jax.shard_map(
        per_device,
        mesh=mesh,
        in_specs=placed,
        out_specs=(P(("blk", "uly"), None, None), P(("blk", "uly"), None, None, None)),
        check_vma=False,
    )
```

profile of v0, /device:TPU:0, one launch (start us, length us, event | category | flops | bytes accessed | tf_op | source)
XLA Modules:
  0.0 317.2 jit_solution(10333332695281003336)
XLA Ops:
  11.0 13.5 %all_to_all.84 = bf16[16,8,1280]{2,0,1:T(8,128)(2,1)} all-to-all(bf16[16,8,1280]{2,0,1:T(8,128)(2,1)S(1)} %pad_maximum_fusion), channel_id=1, replica_groups=mesh['blk'=16,'uly'=8] {'uly'}, dimensions={1} | all-to-all | bytes 655360 | tf_op jit(solution)/shard_map/all_to_all | solution.py:17
  25.7 3.5 %all-to-all-start.1 = ((bf16[16,128,128]{2,0,1:T(8,128)(2,1)}), bf16[16,128,128]{2,0,1:T(8,128)(2,1)S(1)}, u32[]{:S(2)}, u32[]{:S(2)}) async-start(bf16[16,128,128]{2,0,1:T(8,128)(2,1)} %copy.87), calls=%async_computation.1 | async-start | bytes 1048576 | tf_op jit(solution)/shard_map/all_to_all | solution.py:44
  29.2 2.5 copy.89
  31.7 6.5 %all-to-all-done.1 = bf16[16,128,128]{2,0,1:T(8,128)(2,1)S(1)} async-done(((bf16[16,128,128]{2,0,1:T(8,128)(2,1)}), bf16[16,128,128]{2,0,1:T(8,128)(2,1)S(1)}, u32[]{:S(2)}, u32[]{:S(2)}) %all-to-all-start.1) | async-done | bytes 524320 | tf_op jit(solution)/shard_map/all_to_all | solution.py:44
  38.2 3.6 %all-to-all-start.2 = ((bf16[16,128,4,128]{3,2,0,1:T(4,128)(2,1)}), bf16[16,128,4,128]{3,2,0,1:T(4,128)(2,1)S(1)}, u32[]{:S(2)}, u32[]{:S(2)}) async-start(bf16[16,128,4,128]{3,2,0,1:T(4,128)(2,1)} %copy.89), calls=%async_computation.2 | async-start | bytes 4194304 | tf_op jit(solution)/shard_map/all_to_all | solution.py:45
  42.9 32.5 %all-to-all-done.2 = bf16[16,128,4,128]{3,2,0,1:T(4,128)(2,1)S(1)} async-done(((bf16[16,128,4,128]{3,2,0,1:T(4,128)(2,1)}), bf16[16,128,4,128]{3,2,0,1:T(4,128)(2,1)S(1)}, u32[]{:S(2)}, u32[]{:S(2)}) %all-to-all-start.2) | async-done | bytes 2097184 | tf_op jit(solution)/shard_map/all_to_all | solution.py:45
  78.9 11.5 %all-gather.2.cloned.1.call-done = bf16[2048,1,1280]{2,0,1:T(8,128)(2,1)} async-done(((bf16[128,1,1280]{2,0,1:T(8,128)(2,1)}), bf16[2048,1,1280]{2,0,1:T(8,128)(2,1)}) %all-gather.2.cloned.1.call-update) | async-done | bytes 5242896 | tf_op jit(solution)/shard_map/all_gather | solution.py:25
  90.5 4.6 %fusion.48 = (bf16[2048,1,512]{2,0,1:T(8,128)(2,1)}, bf16[2048,1,512]{2,0,1:T(8,128)(2,1)}) fusion(bf16[2048,1,1280]{2,0,1:T(8,128)(2,1)} %all-gather.2.cloned.1.call-done), kind=kLoop, calls=%fused_computation.81 | loop fusion | bytes 8388608 | tf_op jit(solution)/shard_map/slice | solution.py:27
  95.1 4.0 %reshape.242 = bf16[8,256,1,4,128]{4,3,1,0,2:T(4,128)(2,1)} reshape(bf16[2048,1,512]{2,0,1:T(8,128)(2,1)} %get-tuple-element.325) | data formatting | bytes 4194304 | tf_op jit(solution)/shard_map/reshape;reshape | solution.py:130
  99.0 4.2 %copy.96 = bf16[8,256,1,4,128]{1,4,3,2,0:T(8,128)(2,1)} copy(bf16[8,256,1,4,128]{4,3,1,0,2:T(4,128)(2,1)} %reshape.242) | data formatting | bytes 4194304 | tf_op jit(solution)/shard_map/while | solution.py:133
  103.2 4.0 %reshape.241 = bf16[8,256,1,4,128]{4,3,1,0,2:T(4,128)(2,1)} reshape(bf16[2048,1,512]{2,0,1:T(8,128)(2,1)} %get-tuple-element.326) | data formatting | bytes 4194304 | tf_op jit(solution)/shard_map/reshape;reshape | solution.py:128
  107.2 3.5 %copy.95 = bf16[8,256,1,4,128]{4,1,3,2,0:T(8,128)(2,1)} copy(bf16[8,256,1,4,128]{4,3,1,0,2:T(4,128)(2,1)} %reshape.241) | data formatting | bytes 4194304 | tf_op jit(solution)/shard_map/while | solution.py:133
  113.9 2.5 broadcast_in_dim.80
  116.3 142.2 %while.18 = (s32[]{:T(128)}, f32[1,16,128]{2,1,0:T(8,128)S(1)}, f32[1,16,128]{2,1,0:T(8,128)S(1)}, f32[1,16,128,128]{3,2,1,0:T(8,128)}, f32[1,16,4,128,128]{4,3,...) while((s32[]{:T(128)}, f32[1,16,128]{2,1,0:T(8,128)S(1)}, ...), condition=%wide.region_10.11_spmd, body=%wide.region_3.10_spmd.sunk | while | flops 2437986560 | bytes 102954992 | solution.py:133
  118.4 15.7 %conditional.2 = ((f32[1,16,128]{2,1,0:T(8,128)S(1)}, f32[1,16,128]{2,1,0:T(8,128)S(1)}, f32[1,16,128,128]{3,2,1,0:T(8,128)}, f32[1,16,4,128,128]{4,3,2,1,0:T(8,128)}, f32[1,16,4,128]{3,2,1,0:T(4,128)S(1)})) conditional(s32[]{:T(128)} %convert_element_type.36, (f32[1,16,128]{2,1,0:T(8,128)S(1)}, f32[1,16,128]{2,1,0:T(8,128)S(1)}, ...), branch_computations={%region_5.5_spmd, %region_6.9_spmd} | conditional | flops 2437986304 | bytes 102952616 | solution.py:106
  123.9 2.6 fusion.47
  126.5 2.3 fusion.1
  128.8 3.3 %bitcast_add_fusion.1 = f32[1,16,4,128,128]{4,3,2,1,0:T(8,128)S(1)} fusion(f32[16,4,128,128]{3,2,1,0:T(8,128)S(1)} %fusion.1, f32[1,16,4,128,128]{4,3,2,1,0:T(8,128)S(1)} %copy-done, f32[16,128]{1,0:T(8,128)S(1)} %get-tuple-element.313, bf16[8,256,1,4,128]{1,4,3,2,0:T(8,128)(2,1)} %get-tuple-element.190, s32[]{:T(128)} %get-tuple-element.182, ...), kind=kOutput, calls=%fused_computation.2 | convolution fusion | flops 542638080 | bytes 14991872 | tf_op jit(solution)/shard_map/while/body/eval_jaxpr/cond/branch_1_fun/grqk,kgpd->grpqd/dot_general | solution.py:96
  136.2 15.7 %conditional.2 = ((f32[1,16,128]{2,1,0:T(8,128)S(1)}, f32[1,16,128]{2,1,0:T(8,128)S(1)}, f32[1,16,128,128]{3,2,1,0:T(8,128)}, f32[1,16,4,128,128]{4,3,2,1,0:T(8,128)}, f32[1,16,4,128]{3,2,1,0:T(4,128)S(1)})) conditional(s32[]{:T(128)} %convert_element_type.36, (f32[1,16,128]{2,1,0:T(8,128)S(1)}, f32[1,16,128]{2,1,0:T(8,128)S(1)}, ...), branch_computations={%region_5.5_spmd, %region_6.9_spmd} | conditional | flops 2437986304 | bytes 102952616 | solution.py:106
  141.6 2.6 fusion.47
  144.3 2.3 fusion.1
  146.6 3.3 %bitcast_add_fusion.1 = f32[1,16,4,128,128]{4,3,2,1,0:T(8,128)S(1)} fusion(f32[16,4,128,128]{3,2,1,0:T(8,128)S(1)} %fusion.1, f32[1,16,4,128,128]{4,3,2,1,0:T(8,128)S(1)} %copy-done, f32[16,128]{1,0:T(8,128)S(1)} %get-tuple-element.313, bf16[8,256,1,4,128]{1,4,3,2,0:T(8,128)(2,1)} %get-tuple-element.190, s32[]{:T(128)} %get-tuple-element.182, ...), kind=kOutput, calls=%fused_computation.2 | convolution fusion | flops 542638080 | bytes 14991872 | tf_op jit(solution)/shard_map/while/body/eval_jaxpr/cond/branch_1_fun/grqk,kgpd->grpqd/dot_general | solution.py:96
  154.0 15.7 %conditional.2 = ((f32[1,16,128]{2,1,0:T(8,128)S(1)}, f32[1,16,128]{2,1,0:T(8,128)S(1)}, f32[1,16,128,128]{3,2,1,0:T(8,128)}, f32[1,16,4,128,128]{4,3,2,1,0:T(8,128)}, f32[1,16,4,128]{3,2,1,0:T(4,128)S(1)})) conditional(s32[]{:T(128)} %convert_element_type.36, (f32[1,16,128]{2,1,0:T(8,128)S(1)}, f32[1,16,128]{2,1,0:T(8,128)S(1)}, ...), branch_computations={%region_5.5_spmd, %region_6.9_spmd} | conditional | flops 2437986304 | bytes 102952616 | solution.py:106
  159.4 2.6 fusion.47
  162.0 2.3 fusion.1
  164.3 3.3 %bitcast_add_fusion.1 = f32[1,16,4,128,128]{4,3,2,1,0:T(8,128)S(1)} fusion(f32[16,4,128,128]{3,2,1,0:T(8,128)S(1)} %fusion.1, f32[1,16,4,128,128]{4,3,2,1,0:T(8,128)S(1)} %copy-done, f32[16,128]{1,0:T(8,128)S(1)} %get-tuple-element.313, bf16[8,256,1,4,128]{1,4,3,2,0:T(8,128)(2,1)} %get-tuple-element.190, s32[]{:T(128)} %get-tuple-element.182, ...), kind=kOutput, calls=%fused_computation.2 | convolution fusion | flops 542638080 | bytes 14991872 | tf_op jit(solution)/shard_map/while/body/eval_jaxpr/cond/branch_1_fun/grqk,kgpd->grpqd/dot_general | solution.py:96
  171.8 15.7 %conditional.2 = ((f32[1,16,128]{2,1,0:T(8,128)S(1)}, f32[1,16,128]{2,1,0:T(8,128)S(1)}, f32[1,16,128,128]{3,2,1,0:T(8,128)}, f32[1,16,4,128,128]{4,3,2,1,0:T(8,128)}, f32[1,16,4,128]{3,2,1,0:T(4,128)S(1)})) conditional(s32[]{:T(128)} %convert_element_type.36, (f32[1,16,128]{2,1,0:T(8,128)S(1)}, f32[1,16,128]{2,1,0:T(8,128)S(1)}, ...), branch_computations={%region_5.5_spmd, %region_6.9_spmd} | conditional | flops 2437986304 | bytes 102952616 | solution.py:106
  177.2 2.6 fusion.47
  179.8 2.3 fusion.1
  182.1 3.3 %bitcast_add_fusion.1 = f32[1,16,4,128,128]{4,3,2,1,0:T(8,128)S(1)} fusion(f32[16,4,128,128]{3,2,1,0:T(8,128)S(1)} %fusion.1, f32[1,16,4,128,128]{4,3,2,1,0:T(8,128)S(1)} %copy-done, f32[16,128]{1,0:T(8,128)S(1)} %get-tuple-element.313, bf16[8,256,1,4,128]{1,4,3,2,0:T(8,128)(2,1)} %get-tuple-element.190, s32[]{:T(128)} %get-tuple-element.182, ...), kind=kOutput, calls=%fused_computation.2 | convolution fusion | flops 542638080 | bytes 14991872 | tf_op jit(solution)/shard_map/while/body/eval_jaxpr/cond/branch_1_fun/grqk,kgpd->grpqd/dot_general | solution.py:96
  189.5 15.7 %conditional.2 = ((f32[1,16,128]{2,1,0:T(8,128)S(1)}, f32[1,16,128]{2,1,0:T(8,128)S(1)}, f32[1,16,128,128]{3,2,1,0:T(8,128)}, f32[1,16,4,128,128]{4,3,2,1,0:T(8,128)}, f32[1,16,4,128]{3,2,1,0:T(4,128)S(1)})) conditional(s32[]{:T(128)} %convert_element_type.36, (f32[1,16,128]{2,1,0:T(8,128)S(1)}, f32[1,16,128]{2,1,0:T(8,128)S(1)}, ...), branch_computations={%region_5.5_spmd, %region_6.9_spmd} | conditional | flops 2437986304 | bytes 102952616 | solution.py:106
  195.0 2.6 fusion.47
  199.9 3.3 %bitcast_add_fusion.1 = f32[1,16,4,128,128]{4,3,2,1,0:T(8,128)S(1)} fusion(f32[16,4,128,128]{3,2,1,0:T(8,128)S(1)} %fusion.1, f32[1,16,4,128,128]{4,3,2,1,0:T(8,128)S(1)} %copy-done, f32[16,128]{1,0:T(8,128)S(1)} %get-tuple-element.313, bf16[8,256,1,4,128]{1,4,3,2,0:T(8,128)(2,1)} %get-tuple-element.190, s32[]{:T(128)} %get-tuple-element.182, ...), kind=kOutput, calls=%fused_computation.2 | convolution fusion | flops 542638080 | bytes 14991872 | tf_op jit(solution)/shard_map/while/body/eval_jaxpr/cond/branch_1_fun/grqk,kgpd->grpqd/dot_general | solution.py:96
  207.3 15.7 %conditional.2 = ((f32[1,16,128]{2,1,0:T(8,128)S(1)}, f32[1,16,128]{2,1,0:T(8,128)S(1)}, f32[1,16,128,128]{3,2,1,0:T(8,128)}, f32[1,16,4,128,128]{4,3,2,1,0:T(8,128)}, f32[1,16,4,128]{3,2,1,0:T(4,128)S(1)})) conditional(s32[]{:T(128)} %convert_element_type.36, (f32[1,16,128]{2,1,0:T(8,128)S(1)}, f32[1,16,128]{2,1,0:T(8,128)S(1)}, ...), branch_computations={%region_5.5_spmd, %region_6.9_spmd} | conditional | flops 2437986304 | bytes 102952616 | solution.py:106
  212.7 2.6 fusion.47
  217.7 3.3 %bitcast_add_fusion.1 = f32[1,16,4,128,128]{4,3,2,1,0:T(8,128)S(1)} fusion(f32[16,4,128,128]{3,2,1,0:T(8,128)S(1)} %fusion.1, f32[1,16,4,128,128]{4,3,2,1,0:T(8,128)S(1)} %copy-done, f32[16,128]{1,0:T(8,128)S(1)} %get-tuple-element.313, bf16[8,256,1,4,128]{1,4,3,2,0:T(8,128)(2,1)} %get-tuple-element.190, s32[]{:T(128)} %get-tuple-element.182, ...), kind=kOutput, calls=%fused_computation.2 | convolution fusion | flops 542638080 | bytes 14991872 | tf_op jit(solution)/shard_map/while/body/eval_jaxpr/cond/branch_1_fun/grqk,kgpd->grpqd/dot_general | solution.py:96
  225.1 15.7 %conditional.2 = ((f32[1,16,128]{2,1,0:T(8,128)S(1)}, f32[1,16,128]{2,1,0:T(8,128)S(1)}, f32[1,16,128,128]{3,2,1,0:T(8,128)}, f32[1,16,4,128,128]{4,3,2,1,0:T(8,128)}, f32[1,16,4,128]{3,2,1,0:T(4,128)S(1)})) conditional(s32[]{:T(128)} %convert_element_type.36, (f32[1,16,128]{2,1,0:T(8,128)S(1)}, f32[1,16,128]{2,1,0:T(8,128)S(1)}, ...), branch_computations={%region_5.5_spmd, %region_6.9_spmd} | conditional | flops 2437986304 | bytes 102952616 | solution.py:106
  230.5 2.6 fusion.47
  235.5 3.3 %bitcast_add_fusion.1 = f32[1,16,4,128,128]{4,3,2,1,0:T(8,128)S(1)} fusion(f32[16,4,128,128]{3,2,1,0:T(8,128)S(1)} %fusion.1, f32[1,16,4,128,128]{4,3,2,1,0:T(8,128)S(1)} %copy-done, f32[16,128]{1,0:T(8,128)S(1)} %get-tuple-element.313, bf16[8,256,1,4,128]{1,4,3,2,0:T(8,128)(2,1)} %get-tuple-element.190, s32[]{:T(128)} %get-tuple-element.182, ...), kind=kOutput, calls=%fused_computation.2 | convolution fusion | flops 542638080 | bytes 14991872 | tf_op jit(solution)/shard_map/while/body/eval_jaxpr/cond/branch_1_fun/grqk,kgpd->grpqd/dot_general | solution.py:96
  242.9 15.7 %conditional.2 = ((f32[1,16,128]{2,1,0:T(8,128)S(1)}, f32[1,16,128]{2,1,0:T(8,128)S(1)}, f32[1,16,128,128]{3,2,1,0:T(8,128)}, f32[1,16,4,128,128]{4,3,2,1,0:T(8,128)}, f32[1,16,4,128]{3,2,1,0:T(4,128)S(1)})) conditional(s32[]{:T(128)} %convert_element_type.36, (f32[1,16,128]{2,1,0:T(8,128)S(1)}, f32[1,16,128]{2,1,0:T(8,128)S(1)}, ...), branch_computations={%region_5.5_spmd, %region_6.9_spmd} | conditional | flops 2437986304 | bytes 102952616 | solution.py:106
  248.3 2.6 fusion.47
  253.2 3.3 %bitcast_add_fusion.1 = f32[1,16,4,128,128]{4,3,2,1,0:T(8,128)S(1)} fusion(f32[16,4,128,128]{3,2,1,0:T(8,128)S(1)} %fusion.1, f32[1,16,4,128,128]{4,3,2,1,0:T(8,128)S(1)} %copy-done, f32[16,128]{1,0:T(8,128)S(1)} %get-tuple-element.313, bf16[8,256,1,4,128]{1,4,3,2,0:T(8,128)(2,1)} %get-tuple-element.190, s32[]{:T(128)} %get-tuple-element.182, ...), kind=kOutput, calls=%fused_computation.2 | convolution fusion | flops 542638080 | bytes 14991872 | tf_op jit(solution)/shard_map/while/body/eval_jaxpr/cond/branch_1_fun/grqk,kgpd->grpqd/dot_general | solution.py:96
  258.7 2.8 fusion.37
  261.4 4.7 %all-to-all-start.3 = ((bf16[128,16,128]{2,1,0:T(8,128)(2,1)}), bf16[128,16,128]{2,1,0:T(8,128)(2,1)S(1)}, u32[]{:S(2)}, u32[]{:S(2)}) async-start(bf16[128,16,128]{2,1,0:T(8,128)(2,1)} %get-tuple-element.330), calls=%async_computation.3 | async-start | bytes 1048576 | tf_op jit(solution)/shard_map/all_to_all | solution.py:147
  266.7 8.4 %fusion.36 = bf16[128,16,4,128]{3,2,1,0:T(4,128)(2,1)} fusion(f32[16,4,128]{1,0,2:T(8,128)S(1)} %copy.102, f32[16,128,128]{2,0,1:T(8,128)S(1)} %get-tuple-element.329, f32[16,128]{0,1:T(8,128)S(1)} %copy.97, f32[1,16,4,128,128]{4,3,2,1,0:T(8,128)} %get-tuple-element.221), kind=kLoop, calls=%fused_computation.48 | loop fusion | flops 4194304 | bytes 7380992 | tf_op jit(solution)/shard_map/reshape | solution.py:143
  276.7 4.2 %all-to-all-start.4 = ((bf16[128,16,4,128]{3,2,1,0:T(4,128)(2,1)}), bf16[128,16,4,128]{3,2,1,0:T(4,128)(2,1)S(1)}, u32[]{:S(2)}, u32[]{:S(2)}) async-start(bf16[128,16,4,128]{3,2,1,0:T(4,128)(2,1)} %fusion.36), calls=%async_computation.4 | async-start | bytes 4194304 | tf_op jit(solution)/shard_map/all_to_all | solution.py:148
  281.7 26.0 %all-to-all-done.4 = bf16[128,16,4,128]{3,2,1,0:T(4,128)(2,1)S(1)} async-done(((bf16[128,16,4,128]{3,2,1,0:T(4,128)(2,1)}), bf16[128,16,4,128]{3,2,1,0:T(4,128)(2,1)S(1)}, u32[]{:S(2)}, u32[]{:S(2)}) %all-to-all-start.4) | async-done | bytes 2097184 | tf_op jit(solution)/shard_map/all_to_all | solution.py:148
  307.7 2.7 copy.103
  (186 shorter events, 89.2 us)
Async XLA Ops:
  7.2 17.4 %copy-start.6 = (bf16[16,128,128]{2,1,0:T(8,128)(2,1)S(1)}, bf16[16,128,128]{2,1,0:T(8,128)(2,1)}, u32[]{:S(2)}) copy-start(bf16[16,128,128]{2,1,0:T(8,128)(2,1)} %param.11) | copy-start | bytes 1572868
  7.2 83.3 %all-gather.2.cloned.1.call-start = ((), (), s32[]{:S(2)}) async-start(), calls=%async_computation.5 | async-start | bytes 5570560 | tf_op jit(solution)/shard_map/all_gather | solution.py:25
  9.8 19.4 %copy-start.5 = (bf16[16,128,4,128]{3,2,1,0:T(4,128)(2,1)S(1)}, bf16[16,128,4,128]{3,2,1,0:T(4,128)(2,1)}, u32[]{:S(2)}) copy-start(bf16[16,128,4,128]{3,2,1,0:T(4,128)(2,1)} %param.12) | copy-start | bytes 6291460
  25.7 12.5 %all-to-all-start.1 = ((bf16[16,128,128]{2,0,1:T(8,128)(2,1)}), bf16[16,128,128]{2,0,1:T(8,128)(2,1)S(1)}, u32[]{:S(2)}, u32[]{:S(2)}) async-start(bf16[16,128,128]{2,0,1:T(8,128)(2,1)} %copy.87), calls=%async_computation.1 | async-start | bytes 1048576 | tf_op jit(solution)/shard_map/all_to_all | solution.py:44
  31.7 10.2 %copy-start.7 = (s32[32]{0:T(128)S(1)}, s32[32]{0:T(128)}, u32[]{:S(2)}) copy-start(s32[32]{0:T(128)} %param.17) | copy-start | bytes 388
  38.2 37.2 %all-to-all-start.2 = ((bf16[16,128,4,128]{3,2,0,1:T(4,128)(2,1)}), bf16[16,128,4,128]{3,2,0,1:T(4,128)(2,1)S(1)}, u32[]{:S(2)}, u32[]{:S(2)}) async-start(bf16[16,128,4,128]{3,2,0,1:T(4,128)(2,1)} %copy.89), calls=%async_computation.2 | async-start | bytes 4194304 | tf_op jit(solution)/shard_map/all_to_all | solution.py:45
  75.4 1.3 copy-start.2
  118.4 1.2 copy-start.3
  121.6 1.0 copy-start.4
  126.5 2.3 copy-start
  132.1 2.0 copy-start.1
  136.2 1.2 copy-start.3
  139.4 1.0 copy-start.4
  144.2 2.3 copy-start
  149.9 2.0 copy-start.1
  154.0 1.2 copy-start.3
  157.1 1.0 copy-start.4
  162.0 2.3 copy-start
  167.7 2.0 copy-start.1
  171.8 1.2 copy-start.3
  174.9 1.0 copy-start.4
  179.8 2.3 copy-start
  185.5 2.0 copy-start.1
  189.5 1.2 copy-start.3
  192.7 1.0 copy-start.4
  197.6 2.3 copy-start
  203.2 2.0 copy-start.1
  207.3 1.2 copy-start.3
  210.5 1.0 copy-start.4
  215.3 2.3 copy-start
  221.0 2.0 copy-start.1
  225.1 1.2 copy-start.3
  228.3 1.0 copy-start.4
  233.1 2.3 copy-start
  238.8 2.0 copy-start.1
  242.9 1.2 copy-start.3
  246.0 1.0 copy-start.4
  250.9 2.3 copy-start
  256.6 2.0 copy-start.1
  261.4 15.3 %all-to-all-start.3 = ((bf16[128,16,128]{2,1,0:T(8,128)(2,1)}), bf16[128,16,128]{2,1,0:T(8,128)(2,1)S(1)}, u32[]{:S(2)}, u32[]{:S(2)}) async-start(bf16[128,16,128]{2,1,0:T(8,128)(2,1)} %get-tuple-element.330), calls=%async_computation.3 | async-start | bytes 1048576 | tf_op jit(solution)/shard_map/all_to_all | solution.py:147
  276.7 31.0 %all-to-all-start.4 = ((bf16[128,16,4,128]{3,2,1,0:T(4,128)(2,1)}), bf16[128,16,4,128]{3,2,1,0:T(4,128)(2,1)S(1)}, u32[]{:S(2)}, u32[]{:S(2)}) async-start(bf16[128,16,4,128]{3,2,1,0:T(4,128)(2,1)} %fusion.36), calls=%async_computation.4 | async-start | bytes 4194304 | tf_op jit(solution)/shard_map/all_to_all | solution.py:148
Sparse Core Ops, SparseCore 0:
  24.7 65.7 all-gather.1
where the time goes:
time: 320 us; the launch traced here: 317 us
  matrix products  94.8 us (30%)
  waiting for transfers between devices  78.1 us (24%)
  local copies, waits for them, and re-layouts  64.5 us (20%)
  other arithmetic  23.9 us (7%)
  starting transfers between devices  16.1 us (5%)
  between operations  14.2 us (4%)
  blocking collectives  13.5 us (4%)
  loops' own time  12.1 us (4%)
    all_to_all x1, waiting for transfers between devices, per_device(): lax.all_to_all(query_tangents, 'uly', split_axis=1, concat_axis=0, tiled=...  32.5 us
    dot_general x8, matrix products, update(): jnp.einsum('grqk,kgpd->grpqd', weights_half, value_tan, preferred_element...  26.7 us
    all_to_all x1, waiting for transfers between devices, per_device(): lax.all_to_all(tangent_rows, 'uly', split_axis=0, concat_axis=1, tiled=True)  26 us
    cond x72, local copies, waits for them, and re-layouts  23.5 us
    dot_general x8, matrix products, update(): jnp.einsum('grqd,kgpd->grpqk', query_heads, key_tan, preferred_element_ty...  20.7 us
    dot_general x8, matrix products, update(): jnp.einsum('grpqk,kgd->grpqd', weighted.astype(jnp.bfloat16), value_block...  18.4 us
    dot_general x8, matrix products, update(): jnp.einsum('grqk,kgd->grqd', weights_half, value_block, preferred_element...  15.3 us
    all_to_all x1, blocking collectives, in_one_piece(): lax.all_to_all(both, axis, split_axis=split_dim, concat_axis=concat_dim,...  13.5 us
  transfers between devices with their start and end apart: 5, of which 5 were waited for; matrix products, arithmetic and copies ran while one was open for 5% of the time, Pallas kernels for 0%

commit v1 on v0

v1 whole, which is shorter than its diff:
```python
import functools
import math

import jax
import jax.numpy as jnp
from jax import lax
from jax.experimental import pallas as pl
from jax.experimental.pallas import tpu as pltpu
from jax.sharding import PartitionSpec as P

HD = 128
HQ = 128
KVH = 8
P_SIZE = 4
GROUP = HQ // KVH
SPAN = 64
SPANS = 32
ULY = 8
ROWS = 16
KB = 256
PER_BLOCK = KB // SPAN
BLOCKS = SPANS // PER_BLOCK
TILE = 512
HALF = SPAN * GROUP
WIDTH = HD * (2 + 2 * P_SIZE)
SCALE = HD**-0.5
LOG2E = math.log2(math.e)
F32 = jnp.float32
BF16 = jnp.bfloat16


def over_last(a, b):
    return lax.dot_general(a, b, (((1,), (1,)), ((), ())), preferred_element_type=F32)


def attend(meta, x_ref, kv_hbm, out_ref, kv, scores, top, acc, sems):
    first = 2 * meta[SPANS]
    limit = jnp.maximum(meta[first], meta[first + 1])

    def copy_of(j):
        at = pl.multiple_of(meta[j] * SPAN, SPAN)
        return pltpu.make_async_copy(
            kv_hbm.at[pl.ds(j * SPAN, SPAN), :], kv.at[pl.ds(at, SPAN), :], sems.at[j]
        )

    for j in range(SPANS):
        copy_of(j).start()
    for j in range(SPANS):
        copy_of(j).wait()

    ones = jnp.ones((KB, HD), BF16)

    def tile(index, unused):
        half = index // (HALF // TILE)
        part = index % (HALF // TILE)
        pos = meta[first + half]
        blocks = pos // PER_BLOCK + 1
        sources = TILE // 256
        source = half * 4 + part * sources

        def rows_of(k):
            return x_ref[pl.ds(source, sources), k].reshape(TILE, HD)

        def score(b):
            at = pl.multiple_of(b * KB, KB)
            return over_last(rows_of(0), kv[pl.ds(at, KB), 0:HD])

        def keep(b, s):
            scores[b] = s
            top[...] = jnp.maximum(top[...], jnp.maximum(s[:, :HD], s[:, HD:]))

        top[...] = jnp.full((TILE, HD), -1e30, F32)

        def first_pass(b, carry):
            keep(b, score(b))
            return carry

        lax.fori_loop(0, blocks - 1, first_pass, 0)
        last = blocks - 1
        token = part * (TILE // GROUP) + lax.broadcasted_iota(jnp.int32, (TILE, KB), 0) // GROUP
        key = lax.broadcasted_iota(jnp.int32, (TILE, KB), 1)
        visible = key <= (pos - last * PER_BLOCK) * SPAN + token
        keep(last, jnp.where(visible, score(last), -1e30))
        top[...] = jnp.broadcast_to(jnp.max(top[...], axis=1, keepdims=True), (TILE, HD))
        acc[...] = jnp.zeros_like(acc)

        def second_pass(b, carry):
            at = pl.multiple_of(b * KB, KB)
            rows = pl.ds(at, KB)
            peak = top[...]
            s = scores[b]
            s = jnp.concatenate([s[:, :HD] - peak, s[:, HD:] - peak], axis=1)
            weights = jnp.exp2(s * (SCALE * LOG2E))
            half_weights = weights.astype(BF16)
            scaled = weights * SCALE
            v = kv[rows, 5 * HD : 6 * HD]
            from_v = jnp.dot(
                half_weights,
                jnp.concatenate([kv[rows, 5 * HD : 10 * HD], ones], axis=1),
                preferred_element_type=F32,
            )
            v_ones = jnp.concatenate([v, ones], axis=1)
            q = rows_of(0)
            k = kv[rows, 0:HD]
            acc[:, 0:HD] += from_v[:, 0:HD]
            acc[:, HD : 2 * HD] += from_v[:, 5 * HD : 6 * HD]
            for t in range(P_SIZE):
                lhs = jnp.concatenate([rows_of(1 + t), q], axis=1)
                rhs = jnp.concatenate([k, kv[rows, (1 + t) * HD : (2 + t) * HD]], axis=1)
                weighted = (scaled * over_last(lhs, rhs)).astype(BF16)
                part_sum = jnp.dot(weighted, v_ones, preferred_element_type=F32)
                c = 2 * (1 + t) * HD
                acc[:, c : c + HD] += part_sum[:, :HD] + from_v[:, (1 + t) * HD : (2 + t) * HD]
                acc[:, c + HD : c + 2 * HD] += part_sum[:, HD:]
            return carry

        lax.fori_loop(0, blocks, second_pass, 0)
        inverse = 1.0 / acc[:, HD : 2 * HD]
        primal = acc[:, 0:HD] * inverse

        def put(k, value):
            out_ref[pl.ds(source, sources), k] = value.astype(BF16).reshape(sources, 256, HD)

        put(0, primal)
        for t in range(P_SIZE):
            c = 2 * (1 + t) * HD
            put(1 + t, (acc[:, c : c + HD] - primal * acc[:, c + HD : c + 2 * HD]) * inverse)
        return unused

    lax.fori_loop(0, 2 * HALF // TILE, tile, 0)


def attention(meta, x, kv, interpret=False):
    return pl.pallas_call(
        attend,
        out_shape=jax.ShapeDtypeStruct(x.shape, BF16),
        in_specs=[
            pl.BlockSpec(memory_space=pltpu.SMEM),
            pl.BlockSpec(memory_space=pltpu.VMEM),
            pl.BlockSpec(memory_space=pl.ANY),
        ],
        out_specs=pl.BlockSpec(memory_space=pltpu.VMEM),
        scratch_shapes=[
            pltpu.VMEM((SPANS * SPAN, WIDTH), BF16),
            pltpu.VMEM((BLOCKS, TILE, KB), F32),
            pltpu.VMEM((TILE, HD), F32),
            pltpu.VMEM((TILE, 10 * HD), F32),
            pltpu.SemaphoreType.DMA((SPANS,)),
        ],
        compiler_params=pltpu.CompilerParams(vmem_limit_bytes=40 * 2**20),
        interpret=interpret,
        name="attend",
    )(meta, x, kv)


def per_device(queries, query_tangents, keys, key_tangents, values, value_tangents, span_order):
    packed = jnp.concatenate(
        [
            keys.reshape(ROWS, KVH, HD),
            key_tangents.reshape(ROWS, KVH, P_SIZE * HD),
            values.reshape(ROWS, KVH, HD),
            value_tangents.reshape(ROWS, KVH, P_SIZE * HD),
        ],
        axis=2,
    )
    head_kv = lax.all_to_all(packed.transpose(1, 0, 2), "uly", 0, 0, tiled=True)
    kv = lax.all_gather(head_kv.reshape(ULY * ROWS, WIDTH), "blk", axis=0, tiled=True)

    q = queries.reshape(ROWS, ULY, GROUP, HD).transpose(1, 0, 2, 3).reshape(ULY, 1, 256, HD)
    qt = query_tangents.reshape(ROWS, ULY, GROUP, P_SIZE, HD).transpose(1, 3, 0, 2, 4)
    x = jnp.concatenate([q, qt.reshape(ULY, P_SIZE, 256, HD)], axis=1)
    x = lax.all_to_all(x, "uly", 0, 0, tiled=True)

    blk = lax.axis_index("blk").astype(jnp.int32)
    meta = jnp.concatenate([span_order, blk[None]])
    out = attention(meta, x, kv)
    out = lax.all_to_all(out, "uly", 0, 0, tiled=True).reshape(ULY, 1 + P_SIZE, ROWS, GROUP, HD)
    attention_out = out[:, 0].transpose(1, 0, 2, 3).reshape(ROWS, HQ, HD)
    tangent_out = out[:, 1:].transpose(2, 0, 3, 1, 4).reshape(ROWS, HQ, P_SIZE, HD)
    return attention_out, tangent_out


def solution(mesh):
    placed = (
        P(("blk", "uly"), None, None),
        P(("blk", "uly"), None, None, None),
        P(("blk", "uly"), None, None),
        P(("blk", "uly"), None, None, None),
        P(("blk", "uly"), None, None),
        P(("blk", "uly"), None, None, None),
        P(),
    )
    return jax.shard_map(
        per_device,
        mesh=mesh,
        in_specs=placed,
        out_specs=(P(("blk", "uly"), None, None), P(("blk", "uly"), None, None, None)),
        check_vma=False,
    )
```

time: 320 us -> 175 us (0.55)
  matrix products: 94.8 us -> 0 us
  local copies, waits for them, and re-layouts: 64.5 us -> 12 us
  blocking collectives: 13.5 us -> 51.7 us
  Pallas kernels: 0 us -> 32.1 us
  other arithmetic: 23.9 us -> 1.82 us
  waiting for transfers between devices: 78.1 us -> 58.6 us
  starting transfers between devices: 16.1 us -> 3.79 us
  loops' own time: 12.1 us -> 0 us
    dot_general x48 -> x0, matrix products: 94.8 us -> none  [the longest x8 26.7 us: update(): jnp.einsum('grqk,kgpd->grpqd', weights_half, value_tan, preferred_element...]
    all_to_all x1 -> x2, blocking collectives: 13.5 us -> 51.7 us  [the longest x1 38 us: per_device(): lax.all_to_all(out, 'uly', 0, 0, tiled=True)]
    pallas_call x0 -> x1, Pallas kernels: none -> 32.1 us  [attention(): pl.pallas_call(attend, out_shape=jax.ShapeDtypeStruct(x.shape, BF16), in_...]
    all_to_all x4 -> x1, waiting for transfers between devices: 66.5 us -> 35.6 us  [per_device(): x = lax.all_to_all(x, 'uly', 0, 0, tiled=True)]
    cond x72 -> x0, local copies, waits for them, and re-layouts: 23.5 us -> none
    all_to_all x4 -> x1, starting transfers between devices: 16 us -> 3.76 us  [per_device(): x = lax.all_to_all(x, 'uly', 0, 0, tiled=True)]
    another operation x9 -> x0, loops' own time: 12.1 us -> none  [the longest x1 11.1 us: per_device(): carry, unused = lax.scan(visit, carry, stacked)]
    all_gather x1, waiting for transfers between devices: 11.5 us -> 23 us  [per_device(): lax.all_gather(head_kv.reshape(ULY * ROWS, WIDTH), 'blk', axis=0, tiled=T...]
  transfers between devices with their start and end apart: 5 -> 2, of which waited for: 5 -> 2; matrix products, arithmetic and copies ran while one was open for 5% -> 1% of each run, Pallas kernels for 0% -> 0%
where the time goes in v1:
time: 175 us; the launch traced here: 174 us
  waiting for transfers between devices  58.6 us (33%)
  blocking collectives  51.7 us (30%)
  Pallas kernels  32.1 us (18%)
  between operations  14.1 us (8%)
  local copies, waits for them, and re-layouts  12 us (7%)
  starting transfers between devices  3.79 us (2%)
  other arithmetic  1.82 us (1%)
    all_to_all x1, blocking collectives, per_device(): lax.all_to_all(out, 'uly', 0, 0, tiled=True)  38 us
    all_to_all x1, waiting for transfers between devices, per_device(): x = lax.all_to_all(x, 'uly', 0, 0, tiled=True)  35.6 us
    pallas_call x1, Pallas kernels, attention(): pl.pallas_call(attend, out_shape=jax.ShapeDtypeStruct(x.shape, BF16), in_...  32.1 us
    all_gather x1, waiting for transfers between devices, per_device(): lax.all_gather(head_kv.reshape(ULY * ROWS, WIDTH), 'blk', axis=0, tiled=T...  23 us
    all_to_all x1, blocking collectives, per_device(): head_kv = lax.all_to_all(packed.transpose(1, 0, 2), 'uly', 0, 0, tiled=True)  13.6 us
    transpose x2, local copies, waits for them, and re-layouts, per_device(): out[:, 1:].transpose(2, 0, 3, 1, 4).reshape(ROWS, HQ, P_SIZE, HD)  4.38 us
    unnamed x10, local copies, waits for them, and re-layouts  4.03 us
    all_to_all x1, starting transfers between devices, per_device(): x = lax.all_to_all(x, 'uly', 0, 0, tiled=True)  3.76 us
  transfers between devices with their start and end apart: 2, of which 2 were waited for; matrix products, arithmetic and copies ran while one was open for 1% of the time, Pallas kernels for 0%

profile of v1, /device:TPU:0, one launch (start us, length us, event | category | flops | bytes accessed | tf_op | source)
XLA Modules:
  0.0 174.1 jit_solution(11554153832401929458)
XLA Ops:
  7.2 0.0 copy-start.1
  7.2 0.0 all-gather.2.cloned.1.call-start
  7.2 1.1 reshape.38
  8.4 1.0 reshape.39
  9.4 0.8 copy.11
  10.2 0.8 copy.13
  11.0 0.0 copy-start.2
  11.0 13.6 %all_to_all.15 = bf16[8,16,1280]{2,1,0:T(8,128)(2,1)} all-to-all(bf16[8,16,1280]{2,1,0:T(8,128)(2,1)S(1)} %maximum_bitcast_fusion), channel_id=1, replica_groups=mesh['blk'=16,'uly'=8] {'uly'}, dimensions={0} | all-to-all | bytes 655360 | tf_op jit(solution)/shard_map/all_to_all | solution.py:166
  24.6 0.0 all-gather.2.cloned.1.call-update
  24.6 0.0 copy-done.1
  24.6 0.5 copy.10
  25.1 0.0 copy-done.2
  25.2 1.7 pad_maximum_fusion
  26.9 0.0 copy-start.3
  26.9 3.8 %all-to-all-start = ((bf16[8,5,256,128]{3,2,1,0:T(8,128)(2,1)}), bf16[8,5,256,128]{3,2,1,0:T(8,128)(2,1)S(1)}, u32[]{:S(2)}, u32[]{:S(2)}) async-start(bf16[8,5,256,128]{3,2,1,0:T(8,128)(2,1)} %pad_maximum_fusion), calls=%async_computation | async-start | bytes 5242880 | tf_op jit(solution)/shard_map/all_to_all | solution.py:172
  30.7 0.0 copy-done.3
  30.7 0.1 pad_add_fusion.meta
  30.8 35.6 %all-to-all-done.x_ref = bf16[8,5,256,128]{3,2,1,0:T(8,128)(2,1)S(1)} async-done(((bf16[8,5,256,128]{3,2,1,0:T(8,128)(2,1)}), bf16[8,5,256,128]{3,2,1,0:T(8,128)(2,1)S(1)}, u32[]{:S(2)}, u32[]{:S(2)}) %all-to-all-start) | async-done | bytes 2621472 | tf_op jit(solution)/shard_map/all_to_all | solution.py:172
  66.3 23.0 %all-gather.2.cloned.1.call-done.kv_hbm = bf16[2048,1280]{1,0:T(8,128)(2,1)} async-done(((bf16[128,1280]{1,0:T(8,128)(2,1)}), bf16[2048,1280]{1,0:T(8,128)(2,1)}) %all-gather.2.cloned.1.call-update) | async-done | bytes 5242896 | tf_op jit(solution)/shard_map/all_gather | solution.py:167
  89.4 0.0 copy-start
  89.4 2.5 %copy-done = bf16[2048,1280]{1,0:T(8,128)(2,1)S(1)} copy-done((bf16[2048,1280]{1,0:T(8,128)(2,1)S(1)}, bf16[2048,1280]{1,0:T(8,128)(2,1)}, u32[]{:S(2)}) %copy-start) | copy-done | bytes 5242904
  91.9 32.1 %attend.1 = bf16[8,5,256,128]{3,2,1,0:T(8,128)(2,1)S(1)} custom-call(s32[33]{0:T(128)S(1)} %pad_add_fusion.meta, bf16[8,5,256,128]{3,2,1,0:T(8,128)(2,1)S(1)} %all-to-all-done.x_ref, bf16[2048,1280]{1,0:T(8,128)(2,1)S(1)} %copy-done), custom_call_target="tpu_custom_call" | custom-call | tf_op jit(solution)/shard_map/attend/pallas_call | solution.py:134
  124.0 38.0 %all_to_all.16 = bf16[8,5,256,128]{3,2,1,0:T(8,128)(2,1)S(1)} all-to-all(bf16[8,5,256,128]{3,2,1,0:T(8,128)(2,1)S(1)} %attend.1), channel_id=1, replica_groups=mesh['blk'=16,'uly'=8] {'uly'}, dimensions={0} | all-to-all | bytes 5242880 | tf_op jit(solution)/shard_map/all_to_all | solution.py:177
  162.0 0.4 slice_bitcast_fusion
  162.4 4.0 %copy.16 = bf16[16,8,16,4,128]{4,3,2,1,0:T(4,128)(2,1)} copy(bf16[16,8,16,4,128]{4,2,0,3,1:T(8,128)(2,1)S(1)} %slice_bitcast_fusion) | data formatting | bytes 4194304 | tf_op jit(solution)/shard_map/transpose | solution.py:179
  166.5 0.8 copy.15
  (5 shorter events, 0.2 us)
Async XLA Ops:
  7.2 17.5 %copy-start.1 = (bf16[16,128,4,128]{3,2,1,0:T(4,128)(2,1)S(1)}, bf16[16,128,4,128]{3,2,1,0:T(4,128)(2,1)}, u32[]{:S(2)}) copy-start(bf16[16,128,4,128]{3,2,1,0:T(4,128)(2,1)} %param.8) | copy-start | bytes 6291460
  7.2 82.2 %all-gather.2.cloned.1.call-start = ((), (), s32[]{:S(2)}) async-start(), calls=%async_computation.3 | async-start | bytes 5570560 | tf_op jit(solution)/shard_map/all_gather | solution.py:167
  11.0 14.2 %copy-start.2 = (bf16[16,128,128]{2,1,0:T(8,128)(2,1)S(1)}, bf16[16,128,128]{2,1,0:T(8,128)(2,1)}, u32[]{:S(2)}) copy-start(bf16[16,128,128]{2,1,0:T(8,128)(2,1)} %param.7) | copy-start | bytes 1572868
  26.9 3.8 %copy-start.3 = (s32[32]{0:T(128)S(1)}, s32[32]{0:T(128)}, u32[]{:S(2)}) copy-start(s32[32]{0:T(128)} %param.13) | copy-start | bytes 388
  26.9 39.4 %all-to-all-start = ((bf16[8,5,256,128]{3,2,1,0:T(8,128)(2,1)}), bf16[8,5,256,128]{3,2,1,0:T(8,128)(2,1)S(1)}, u32[]{:S(2)}, u32[]{:S(2)}) async-start(bf16[8,5,256,128]{3,2,1,0:T(8,128)(2,1)} %pad_maximum_fusion), calls=%async_computation | async-start | bytes 5242880 | tf_op jit(solution)/shard_map/all_to_all | solution.py:172
  89.4 2.5 %copy-start = (bf16[2048,1280]{1,0:T(8,128)(2,1)S(1)}, bf16[2048,1280]{1,0:T(8,128)(2,1)}, u32[]{:S(2)}) copy-start(bf16[2048,1280]{1,0:T(8,128)(2,1)} %all-gather.2.cloned.1.call-done.kv_hbm) | copy-start | bytes 15728644
Sparse Core Ops, SparseCore 0:
  24.7 64.5 all-gather.1

commit v2 on v1

v2 whole, which is shorter than its diff:
```python
import math

import jax
import jax.numpy as jnp
from jax import lax
from jax.experimental import pallas as pl
from jax.experimental.pallas import tpu as pltpu
from jax.sharding import Mesh
from jax.sharding import PartitionSpec as P

HD = 128
HQ = 128
KVH = 8
P_SIZE = 4
GROUP = HQ // KVH
SPAN = 64
SPANS = 32
ULY = 8
ROWS = 16
KB = 256
PER_BLOCK = KB // SPAN
BLOCKS = SPANS // PER_BLOCK
PARTS = 2
HEADS = GROUP // PARTS
CHUNK = ROWS * HEADS
TILE = SPAN * HEADS
WIDTH = HD * (2 + 2 * P_SIZE)
SCALE = HD**-0.5
LOG2E = math.log2(math.e)
F32 = jnp.float32
BF16 = jnp.bfloat16
AXES = ("z", "xh", "core", "y", "xl")


def over_last(a, b):
    return lax.dot_general(a, b, (((1,), (1,)), ((), ())), preferred_element_type=F32)


def pieces_of(z, xh, core):
    found = []
    for other_core in range(2):
        at = 5 * other_core
        c = core ^ other_core
        for operand, step, halves in ((0, 0, (0, 1)), (1, 3, (0, 1)), (2, 1, (0, 1)), (3, 2, (0,)), (4, 2, (1,))):
            for place, h in enumerate(halves):
                block = (((z + step) % 4) * 2 + (xh ^ h)) * 2 + c
                for s in range(2):
                    found.append((at + operand, place * 2 * SPAN + s * SPAN, 2 * block + s))
    return found


def attend(meta, x_ref, *rest):
    pieces, (out_ref, kv, scores, top, acc, sems) = rest[:10], rest[10:]
    blk = meta[SPANS]
    first = 2 * blk

    for n, (operand, row, stored) in enumerate(pieces_of(blk // 4, (blk // 2) % 2, blk % 2)):
        at = pl.multiple_of(meta[stored] * SPAN, SPAN)
        pltpu.make_async_copy(
            pieces[operand].at[pl.ds(row, SPAN), :], kv.at[pl.ds(at, SPAN), :], sems.at[n]
        ).start()
    for n in range(SPANS):
        pltpu.make_async_copy(
            pieces[0].at[pl.ds(0, SPAN), :], kv.at[pl.ds(0, SPAN), :], sems.at[n]
        ).wait()

    ones = jnp.ones((KB, HD), BF16)

    def tile(half, unused):
        pos = meta[first + half]
        blocks = pos // PER_BLOCK + 1
        source = half * 4

        def rows_of(k):
            return x_ref[pl.ds(source, 4), k].reshape(TILE, HD)

        def score(b):
            at = pl.multiple_of(b * KB, KB)
            return over_last(rows_of(0), kv[pl.ds(at, KB), 0:HD])

        def keep(b, s):
            scores[b] = s
            top[...] = jnp.maximum(top[...], jnp.maximum(s[:, :HD], s[:, HD:]))

        top[...] = jnp.full((TILE, HD), -1e30, F32)

        def first_pass(b, carry):
            keep(b, score(b))
            return carry

        lax.fori_loop(0, blocks - 1, first_pass, 0)
        last = blocks - 1
        token = lax.broadcasted_iota(jnp.int32, (TILE, KB), 0) // HEADS
        key = lax.broadcasted_iota(jnp.int32, (TILE, KB), 1)
        visible = key <= (pos - last * PER_BLOCK) * SPAN + token
        keep(last, jnp.where(visible, score(last), -1e30))
        top[...] = jnp.broadcast_to(jnp.max(top[...], axis=1, keepdims=True), (TILE, HD))
        acc[...] = jnp.zeros_like(acc)

        def second_pass(b, carry):
            at = pl.multiple_of(b * KB, KB)
            rows = pl.ds(at, KB)
            peak = top[...]
            s = scores[b]
            s = jnp.concatenate([s[:, :HD] - peak, s[:, HD:] - peak], axis=1)
            weights = jnp.exp2(s * (SCALE * LOG2E))
            half_weights = weights.astype(BF16)
            scaled = weights * SCALE
            v = kv[rows, 5 * HD : 6 * HD]
            from_v = jnp.dot(
                half_weights,
                jnp.concatenate([kv[rows, 5 * HD : 10 * HD], ones], axis=1),
                preferred_element_type=F32,
            )
            v_ones = jnp.concatenate([v, ones], axis=1)
            q = rows_of(0)
            k = kv[rows, 0:HD]
            acc[:, 0:HD] += from_v[:, 0:HD]
            acc[:, HD : 2 * HD] += from_v[:, 5 * HD : 6 * HD]
            for t in range(P_SIZE):
                lhs = jnp.concatenate([rows_of(1 + t), q], axis=1)
                rhs = jnp.concatenate([k, kv[rows, (1 + t) * HD : (2 + t) * HD]], axis=1)
                weighted = (scaled * over_last(lhs, rhs)).astype(BF16)
                part_sum = jnp.dot(weighted, v_ones, preferred_element_type=F32)
                c = 2 * (1 + t) * HD
                acc[:, c : c + HD] += part_sum[:, :HD] + from_v[:, (1 + t) * HD : (2 + t) * HD]
                acc[:, c + HD : c + 2 * HD] += part_sum[:, HD:]
            return carry

        lax.fori_loop(0, blocks, second_pass, 0)
        inverse = 1.0 / acc[:, HD : 2 * HD]
        primal = acc[:, 0:HD] * inverse

        def put(k, value):
            out_ref[pl.ds(source, 4), k] = value.astype(BF16).reshape(4, CHUNK, HD)

        put(0, primal)
        for t in range(P_SIZE):
            c = 2 * (1 + t) * HD
            put(1 + t, (acc[:, c : c + HD] - primal * acc[:, c + HD : c + 2 * HD]) * inverse)
        return unused

    lax.fori_loop(0, 2, tile, 0)


def attention(meta, x, pieces):
    flops = 2 * 2 * TILE * 5 * KB * 11 * KB * HD
    return pl.pallas_call(
        attend,
        out_shape=jax.ShapeDtypeStruct(x.shape, BF16),
        in_specs=[
            pl.BlockSpec(memory_space=pltpu.SMEM),
            pl.BlockSpec(memory_space=pltpu.VMEM),
        ]
        + [pl.BlockSpec(memory_space=pl.ANY)] * len(pieces),
        out_specs=pl.BlockSpec(memory_space=pltpu.VMEM),
        scratch_shapes=[
            pltpu.VMEM((SPANS * SPAN, WIDTH), BF16),
            pltpu.VMEM((BLOCKS, TILE, KB), F32),
            pltpu.VMEM((TILE, HD), F32),
            pltpu.VMEM((TILE, 10 * HD), F32),
            pltpu.SemaphoreType.DMA((SPANS,)),
        ],
        compiler_params=pltpu.CompilerParams(vmem_limit_bytes=30 * 2**20),
        cost_estimate=pl.CostEstimate(flops=flops, transcendentals=0, bytes_accessed=8 * 2**20),
        name="attend",
    )(meta, x, *pieces)


def gather_blocks(own):
    beside = lax.ppermute(own, "xh", [(0, 1), (1, 0)])
    here = jnp.concatenate([own, beside], axis=0)
    up = [(i, (i + 1) % 4) for i in range(4)]
    down = [(i, (i + 3) % 4) for i in range(4)]
    below = lax.ppermute(here, "z", up)
    above = lax.ppermute(here, "z", down)
    far_low = lax.ppermute(below[: 2 * SPAN], "z", up)
    far_high = lax.ppermute(above[2 * SPAN :], "z", down)
    mine = [here, below, above, far_low, far_high]
    return mine + [lax.ppermute(a, "core", [(0, 1), (1, 0)]) for a in mine]


def per_device(queries, query_tangents, keys, key_tangents, values, value_tangents, span_order):
    packed = jnp.concatenate(
        [
            keys.reshape(ROWS, KVH, HD),
            key_tangents.reshape(ROWS, KVH, P_SIZE * HD),
            values.reshape(ROWS, KVH, HD),
            value_tangents.reshape(ROWS, KVH, P_SIZE * HD),
        ],
        axis=2,
    )
    heads = ("y", "xl")
    head_kv = lax.all_to_all(packed.transpose(1, 0, 2), heads, 0, 0, tiled=True)
    pieces = gather_blocks(head_kv.reshape(ULY * ROWS, WIDTH))

    q = queries.reshape(ROWS, ULY, PARTS, HEADS, HD).transpose(2, 1, 0, 3, 4)
    qt = query_tangents.reshape(ROWS, ULY, PARTS, HEADS, P_SIZE, HD).transpose(2, 1, 4, 0, 3, 5)
    blk = lax.axis_index(("z", "xh", "core")).astype(jnp.int32)
    meta = jnp.concatenate([span_order, blk[None]])
    got = []
    for part in range(PARTS):
        x = jnp.concatenate(
            [
                q[part].reshape(ULY, 1, CHUNK, HD),
                qt[part].reshape(ULY, P_SIZE, CHUNK, HD),
            ],
            axis=1,
        )
        got.append(lax.all_to_all(x, heads, 0, 0, tiled=True))
    sent = []
    for part in range(PARTS):
        out = attention(meta, got[part], pieces)
        out = lax.all_to_all(out, heads, 0, 0, tiled=True)
        sent.append(out.reshape(ULY, 1 + P_SIZE, ROWS, HEADS, HD))
    attention_out = jnp.stack([o[:, 0] for o in sent], axis=1)
    attention_out = attention_out.transpose(2, 0, 1, 3, 4).reshape(ROWS, HQ, HD)
    tangent_out = jnp.stack([o[:, 1:] for o in sent], axis=1)
    tangent_out = tangent_out.transpose(3, 0, 1, 4, 2, 5).reshape(ROWS, HQ, P_SIZE, HD)
    return attention_out, tangent_out


def solution(mesh):
    grid = Mesh(mesh.devices.reshape(4, 2, 2, 4, 2), AXES)
    rows = P(AXES)
    return jax.shard_map(
        per_device,
        mesh=grid,
        in_specs=(rows,) * 6 + (P(),),
        out_specs=(rows, rows),
        check_vma=False,
    )
```

time: 175 us -> 136 us (0.78)
  blocking collectives: 51.7 us -> 13.4 us
  starting transfers between devices: 3.79 us -> 29.5 us
  waiting for transfers between devices: 58.6 us -> 35.1 us
  between operations: 14.1 us -> 0.86 us
  Pallas kernels: 32.1 us -> 38.5 us
  local copies, waits for them, and re-layouts: 12 us -> 14.4 us
  other arithmetic: 1.82 us -> 3.97 us
    all_to_all x2 -> x1, blocking collectives: 51.7 us -> 13.4 us  [per_device(): head_kv = lax.all_to_all(packed.transpose(1, 0, 2), heads, 0, 0, tiled=True)]
    all_gather x1 -> x0, waiting for transfers between devices: 23 us -> none  [per_device(): lax.all_gather(head_kv.reshape(ULY * ROWS, WIDTH), 'blk', axis=0, tiled=T...]
    all_to_all x1 -> x4, waiting for transfers between devices: 35.6 us -> 16.7 us  [the longest x2 16.1 us: per_device(): out = lax.all_to_all(out, heads, 0, 0, tiled=True)]
    ppermute x0 -> x10, waiting for transfers between devices: none -> 18.4 us  [the longest x1 7.64 us: gather_blocks(): below = lax.ppermute(here, 'z', up)]
    all_to_all x1 -> x4, starting transfers between devices: 3.76 us -> 18.6 us  [the longest x2 10.8 us: per_device(): out = lax.all_to_all(out, heads, 0, 0, tiled=True)]
    ppermute x0 -> x10, starting transfers between devices: none -> 10.9 us  [the longest x1 3.14 us: gather_blocks(): far_high = lax.ppermute(above[2 * SPAN:], 'z', down)]
    pallas_call x1 -> x2, Pallas kernels: 32.1 us -> 38.5 us  [attention(): pl.pallas_call(attend, out_shape=jax.ShapeDtypeStruct(x.shape, BF16), in_...]
    another operation x0 -> x4, local copies, waits for them, and re-layouts: none -> 2.53 us  [the longest x2 1.37 us: per_device(): tangent_out = jnp.stack([o[:, 1:] for o in sent], axis=1)]
  transfers between devices with their start and end apart: 2 -> 14, of which waited for: 2 -> 6; matrix products, arithmetic and copies ran while one was open for 1% -> 7% of each run, Pallas kernels for 0% -> 28%
where the time goes in v2:
time: 136 us
  Pallas kernels  38.5 us (28%)
  waiting for transfers between devices  35.1 us (26%)
  starting transfers between devices  29.5 us (22%)
  local copies, waits for them, and re-layouts  14.4 us (11%)
  blocking collectives  13.4 us (10%)
  other arithmetic  3.97 us (3%)
    pallas_call x2, Pallas kernels, attention(): pl.pallas_call(attend, out_shape=jax.ShapeDtypeStruct(x.shape, BF16), in_...  38.5 us
    all_to_all x2, waiting for transfers between devices, per_device(): out = lax.all_to_all(out, heads, 0, 0, tiled=True)  16.1 us
    all_to_all x1, blocking collectives, per_device(): head_kv = lax.all_to_all(packed.transpose(1, 0, 2), heads, 0, 0, tiled=True)  13.4 us
    all_to_all x2, starting transfers between devices, per_device(): out = lax.all_to_all(out, heads, 0, 0, tiled=True)  10.8 us
    all_to_all x2, starting transfers between devices, per_device(): got.append(lax.all_to_all(x, heads, 0, 0, tiled=True))  7.84 us
    ppermute x1, waiting for transfers between devices, gather_blocks(): below = lax.ppermute(here, 'z', up)  7.64 us
    ppermute x1, waiting for transfers between devices, gather_blocks(): far_low = lax.ppermute(below[:2 * SPAN], 'z', up)  4.53 us
    transpose x1, local copies, waits for them, and re-layouts, per_device(): tangent_out.transpose(3, 0, 1, 4, 2, 5).reshape(ROWS, HQ, P_SIZE, HD)  4.02 us
  transfers between devices with their start and end apart: 14, of which 6 were waited for; matrix products, arithmetic and copies ran while one was open for 7% of the time, Pallas kernels for 28%

profile of v2, /device:TPU:0, one launch (start us, length us, event | category | flops | bytes accessed | tf_op | source)
XLA Modules:
  0.0 135.7 jit_solution(4006699212301918438)
XLA Ops:
  0.6 1.0 reshape.34
  1.6 0.8 copy.13
  2.4 1.0 reshape.33
  3.4 0.8 copy.11
  4.2 13.4 %all_to_all.25 = bf16[8,16,1280]{2,1,0:T(8,128)(2,1)S(1)} all-to-all(bf16[8,16,1280]{2,1,0:T(8,128)(2,1)S(1)} %maximum_bitcast_fusion.2), channel_id=1, replica_groups=mesh['z'=4,'xh'=2,'core'=2,'y'=4,'xl'=2] {'y','xl'}, dimensions={0} | all-to-all | bytes 655360 | tf_op jit(solution)/shard_map/all_to_all | solution.py:194
  17.6 2.7 %collective-permute-start = (bf16[128,1280]{1,0:T(8,128)(2,1)S(1)}, bf16[128,1280]{1,0:T(8,128)(2,1)S(1)}, u32[]{:S(2)}, u32[]{:S(2)}) collective-permute-start(bf16[128,1280]{1,0:T(8,128)(2,1)S(1)} %bitcast.38), channel_id=1, source_target_pairs={{0,16},{16,0},{1,17},{17,1},{2,18},{18,2},{3,19},{19,3},{4,20},{20... | collective-permute-start | bytes 983048 | tf_op jit(solution)/shard_map/ppermute | solution.py:171
  20.4 2.2 %copy.19 = bf16[16,8,2,8,4,128]{5,3,0,4,1,2:T(8,128)(2,1)S(1)} copy(bf16[16,8,2,8,4,128]{5,4,3,2,1,0:T(4,128)(2,1)} %bitcast.35) | data formatting | bytes 4194304 | tf_op jit(solution)/shard_map/reshape | solution.py:198
  22.5 0.1 copy.20
  22.7 1.1 slice_bitcast_fusion.3
  23.8 3.5 %collective-permute-done = bf16[128,1280]{1,0:T(8,128)(2,1)S(1)} collective-permute-done((bf16[128,1280]{1,0:T(8,128)(2,1)S(1)}, bf16[128,1280]{1,0:T(8,128)(2,1)S(1)}, u32[]{:S(2)}, u32[]{:S(2)}) %collective-permute-start) | collective-permute-done | bytes 327712 | tf_op jit(solution)/shard_map/ppermute | solution.py:171
  27.4 2.0 %collective-permute-start.1 = (bf16[256,1280]{1,0:T(8,128)(2,1)S(1)}, bf16[256,1280]{1,0:T(8,128)(2,1)S(1)}, u32[]{:S(2)}, u32[]{:S(2)}) collective-permute-start(bf16[256,1280]{1,0:T(8,128)(2,1)S(1)} %pad_maximum_fusion.2.rest_0_), channel_id=1, source_target_pairs={{0,32},{32,64},{64,96},{96,0},{1,33},{33,65},{65,97},{97,1},{2,34}... | collective-permute-start | bytes 1966088 | tf_op jit(solution)/shard_map/ppermute | solution.py:175
  29.4 2.2 %collective-permute-start.2 = (bf16[256,1280]{1,0:T(8,128)(2,1)S(1)}, bf16[256,1280]{1,0:T(8,128)(2,1)S(1)}, u32[]{:S(2)}, u32[]{:S(2)}) collective-permute-start(bf16[256,1280]{1,0:T(8,128)(2,1)S(1)} %pad_maximum_fusion.2.rest_0_), channel_id=1, source_target_pairs={{0,96},{32,0},{64,32},{96,64},{1,97},{33,1},{65,33},{97,65},{2,98}... | collective-permute-start | bytes 1966088 | tf_op jit(solution)/shard_map/ppermute | solution.py:176
  31.6 1.2 pad_maximum_fusion.1
  32.8 3.6 %all-to-all-start.3 = ((bf16[8,5,128,128]{3,2,1,0:T(8,128)(2,1)}), bf16[8,5,128,128]{3,2,1,0:T(8,128)(2,1)S(1)}, u32[]{:S(2)}, u32[]{:S(2)}) async-start(bf16[8,5,128,128]{3,2,1,0:T(8,128)(2,1)} %pad_maximum_fusion.1), calls=%async_computation.3 | async-start | bytes 2621440 | tf_op jit(solution)/shard_map/all_to_all | solution.py:210
  36.4 0.0 copy-start.1
  36.4 0.1 collective-permute-start.5
  36.5 7.6 %collective-permute-done.1.rest_1_ = bf16[256,1280]{1,0:T(8,128)(2,1)S(1)} collective-permute-done((bf16[256,1280]{1,0:T(8,128)(2,1)S(1)}, bf16[256,1280]{1,0:T(8,128)(2,1)S(1)}, u32[]{:S(2)}, u32[]{:S(2)}) %collective-permute-start.1) | collective-permute-done | bytes 655392 | tf_op jit(solution)/shard_map/ppermute | solution.py:175
  44.1 0.1 collective-permute-start.3
  44.2 0.1 collective-permute-start.6
  44.3 0.0 collective-permute-done.2.rest_2_
  44.3 0.6 collective-permute-start.7
  44.9 3.1 %collective-permute-start.4 = (bf16[128,1280]{1,0:T(8,128)(2,1)S(1)}, bf16[128,1280]{1,0:T(8,128)(2,1)}, u32[]{:S(2)}, u32[]{:S(2)}) collective-permute-start(bf16[128,1280]{1,0:T(8,128)(2,1)S(1)} %slice.43), channel_id=1, source_target_pairs={{0,96},{32,0},{64,32},{96,64},{1,97},{33,1},{65,33},{97,65},{2,98}... | collective-permute-start | bytes 983048 | tf_op jit(solution)/shard_map/ppermute | solution.py:178
  48.1 4.5 %collective-permute-done.3.rest_3_ = bf16[128,1280]{1,0:T(8,128)(2,1)} collective-permute-done((bf16[128,1280]{1,0:T(8,128)(2,1)S(1)}, bf16[128,1280]{1,0:T(8,128)(2,1)}, u32[]{:S(2)}, u32[]{:S(2)}) %collective-permute-start.3) | collective-permute-done | bytes 327712 | tf_op jit(solution)/shard_map/ppermute | solution.py:177
  52.6 0.0 collective-permute-start.8
  52.6 2.7 %collective-permute-done.4.rest_4_ = bf16[128,1280]{1,0:T(8,128)(2,1)} collective-permute-done((bf16[128,1280]{1,0:T(8,128)(2,1)S(1)}, bf16[128,1280]{1,0:T(8,128)(2,1)}, u32[]{:S(2)}, u32[]{:S(2)}) %collective-permute-start.4) | collective-permute-done | bytes 327712 | tf_op jit(solution)/shard_map/ppermute | solution.py:178
  55.3 0.0 collective-permute-start.9
  55.3 0.1 pad_add_fusion.meta
  55.4 2.4 %pad_maximum_fusion = bf16[8,5,128,128]{3,2,1,0:T(8,128)(2,1)} fusion(bf16[8,4,128,128]{3,2,1,0:T(8,128)(2,1)} %get-tuple-element.2, bf16[8,1,128,128]{3,2,1,0:T(8,128)(2,1)S(1)} %get-tuple-element.4), kind=kLoop, calls=%fused_computation.2 | loop fusion | flops 655360 | bytes 2621440 | tf_op jit(solution)/shard_map/concatenate | solution.py:203
  57.7 0.0 all-to-all-done.3.x_ref
  57.8 4.3 %all-to-all-start = ((bf16[8,5,128,128]{3,2,1,0:T(8,128)(2,1)}), bf16[8,5,128,128]{3,2,1,0:T(8,128)(2,1)}, u32[]{:S(2)}, u32[]{:S(2)}) async-start(bf16[8,5,128,128]{3,2,1,0:T(8,128)(2,1)} %pad_maximum_fusion), calls=%async_computation | async-start | bytes 2621440 | tf_op jit(solution)/shard_map/all_to_all | solution.py:210
  62.0 0.0 collective-permute-done.5.rest_5_
  62.0 0.0 collective-permute-done.6.rest_6_
  62.0 0.0 collective-permute-done.7.rest_7_
  62.1 0.0 collective-permute-done.8.rest_8_
  62.1 18.9 %attend.3 = bf16[8,5,128,128]{3,2,1,0:T(8,128)(2,1)} custom-call(s32[33]{0:T(128)S(1)} %pad_add_fusion.meta, bf16[8,5,128,128]{3,2,1,0:T(8,128)(2,1)S(1)} %all-to-all-done.3.x_ref, bf16[256,1280]{1,0:T(8,128)(2,1)S(1)} %pad_maximum_fusion.2.rest_0_, bf16[256,1280]{1,0:T(8,128)(2,1)S(1)} %collective-permute-done.1.rest_1_, ...), custom_call_target="tpu_custom_call" | custom-call | flops 944892805120 | bytes 8388608 | tf_op jit(solution)/shard_map/attend/pallas_call | solution.py:148
  81.0 0.6 all-to-all-done.x_ref
  81.5 5.0 %all-to-all-start.4 = ((bf16[8,5,128,128]{3,2,1,0:T(8,128)(2,1)}), bf16[8,5,128,128]{3,2,1,0:T(8,128)(2,1)}, u32[]{:S(2)}, u32[]{:S(2)}) async-start(bf16[8,5,128,128]{3,2,1,0:T(8,128)(2,1)} %attend.3), calls=%async_computation.4 | async-start | bytes 2621440 | tf_op jit(solution)/shard_map/all_to_all | solution.py:214
  86.6 19.7 %attend.2 = bf16[8,5,128,128]{3,2,1,0:T(8,128)(2,1)} custom-call(s32[33]{0:T(128)S(1)} %pad_add_fusion.meta, bf16[8,5,128,128]{3,2,1,0:T(8,128)(2,1)} %all-to-all-done.x_ref, bf16[256,1280]{1,0:T(8,128)(2,1)S(1)} %pad_maximum_fusion.2.rest_0_, bf16[256,1280]{1,0:T(8,128)(2,1)S(1)} %collective-permute-done.1.rest_1_, ...), custom_call_target="tpu_custom_call" | custom-call | flops 944892805120 | bytes 8388608 | tf_op jit(solution)/shard_map/attend/pallas_call | solution.py:148
  106.3 0.0 all-to-all-done.4
  106.3 5.7 %all-to-all-start.2 = ((bf16[8,5,128,128]{3,2,1,0:T(8,128)(2,1)}), bf16[8,5,128,128]{3,2,1,0:T(8,128)(2,1)S(1)}, u32[]{:S(2)}, u32[]{:S(2)}) async-start(bf16[8,5,128,128]{3,2,1,0:T(8,128)(2,1)} %attend.2), calls=%async_computation.2 | async-start | bytes 2621440 | tf_op jit(solution)/shard_map/all_to_all | solution.py:214
  112.0 1.0 slice.47
  113.0 1.3 slice_bitcast_fusion
  114.3 16.1 %all-to-all-done.2 = bf16[8,5,128,128]{3,2,1,0:T(8,128)(2,1)S(1)} async-done(((bf16[8,5,128,128]{3,2,1,0:T(8,128)(2,1)}), bf16[8,5,128,128]{3,2,1,0:T(8,128)(2,1)S(1)}, u32[]{:S(2)}, u32[]{:S(2)}) %all-to-all-start.2) | async-done | bytes 1310752 | tf_op jit(solution)/shard_map/all_to_all | solution.py:214
  130.4 0.1 slice_bitcast_fusion.1
  130.5 0.1 maximum_bitcast_fusion.1
  130.5 0.9 copy.15
  131.4 0.2 maximum_bitcast_fusion
  131.6 4.0 %copy.16 = bf16[16,8,2,8,4,128]{5,4,3,2,1,0:T(4,128)(2,1)} copy(bf16[16,8,2,8,4,128]{5,3,0,4,1,2:T(8,128)(2,1)S(1)} %maximum_bitcast_fusion) | data formatting | bytes 4194304 | tf_op jit(solution)/shard_map/transpose | solution.py:219
  (12 shorter events, 0.3 us)
Async XLA Ops:
  17.6 9.7 %collective-permute-start = (bf16[128,1280]{1,0:T(8,128)(2,1)S(1)}, bf16[128,1280]{1,0:T(8,128)(2,1)S(1)}, u32[]{:S(2)}, u32[]{:S(2)}) collective-permute-start(bf16[128,1280]{1,0:T(8,128)(2,1)S(1)} %bitcast.38), channel_id=1, source_target_pairs={{0,16},{16,0},{1,17},{17,1},{2,18},{18,2},{3,19},{19,3},{4,20},{20... | collective-permute-start | bytes 983048 | tf_op jit(solution)/shard_map/ppermute | solution.py:171
  20.4 2.2 %copy-start = (bf16[16,128,128]{2,1,0:T(8,128)(2,1)S(1)}, bf16[16,128,128]{2,1,0:T(8,128)(2,1)}, u32[]{:S(2)}) copy-start(bf16[16,128,128]{2,1,0:T(8,128)(2,1)} %param.7) | copy-start | bytes 1572868
  27.4 16.7 %collective-permute-start.1 = (bf16[256,1280]{1,0:T(8,128)(2,1)S(1)}, bf16[256,1280]{1,0:T(8,128)(2,1)S(1)}, u32[]{:S(2)}, u32[]{:S(2)}) collective-permute-start(bf16[256,1280]{1,0:T(8,128)(2,1)S(1)} %pad_maximum_fusion.2.rest_0_), channel_id=1, source_target_pairs={{0,32},{32,64},{64,96},{96,0},{1,33},{33,65},{65,97},{97,1},{2,34}... | collective-permute-start | bytes 1966088 | tf_op jit(solution)/shard_map/ppermute | solution.py:175
  29.4 14.9 %collective-permute-start.2 = (bf16[256,1280]{1,0:T(8,128)(2,1)S(1)}, bf16[256,1280]{1,0:T(8,128)(2,1)S(1)}, u32[]{:S(2)}, u32[]{:S(2)}) collective-permute-start(bf16[256,1280]{1,0:T(8,128)(2,1)S(1)} %pad_maximum_fusion.2.rest_0_), channel_id=1, source_target_pairs={{0,96},{32,0},{64,32},{96,64},{1,97},{33,1},{65,33},{97,65},{2,98}... | collective-permute-start | bytes 1966088 | tf_op jit(solution)/shard_map/ppermute | solution.py:176
  32.8 25.0 %all-to-all-start.3 = ((bf16[8,5,128,128]{3,2,1,0:T(8,128)(2,1)}), bf16[8,5,128,128]{3,2,1,0:T(8,128)(2,1)S(1)}, u32[]{:S(2)}, u32[]{:S(2)}) async-start(bf16[8,5,128,128]{3,2,1,0:T(8,128)(2,1)} %pad_maximum_fusion.1), calls=%async_computation.3 | async-start | bytes 2621440 | tf_op jit(solution)/shard_map/all_to_all | solution.py:210
  36.4 18.9 %copy-start.1 = (s32[32]{0:T(128)S(1)}, s32[32]{0:T(128)}, u32[]{:S(2)}) copy-start(s32[32]{0:T(128)} %param.13) | copy-start | bytes 388
  36.4 25.7 %collective-permute-start.5 = (bf16[256,1280]{1,0:T(8,128)(2,1)S(1)}, bf16[256,1280]{1,0:T(8,128)(2,1)}, u32[]{:S(2)}, u32[]{:S(2)}) collective-permute-start(bf16[256,1280]{1,0:T(8,128)(2,1)S(1)} %pad_maximum_fusion.2.rest_0_), channel_id=1, source_target_pairs={{0,8},{8,0},{1,9},{9,1},{2,10},{10,2},{3,11},{11,3},{4,12},{12,4},... | collective-permute-start | bytes 1966088 | tf_op jit(solution)/shard_map/ppermute | solution.py:180
  44.1 8.5 %collective-permute-start.3 = (bf16[128,1280]{1,0:T(8,128)(2,1)S(1)}, bf16[128,1280]{1,0:T(8,128)(2,1)}, u32[]{:S(2)}, u32[]{:S(2)}) collective-permute-start(bf16[128,1280]{1,0:T(8,128)(2,1)S(1)} %slice.42), channel_id=1, source_target_pairs={{0,32},{32,64},{64,96},{96,0},{1,33},{33,65},{65,97},{97,1},{2,34}... | collective-permute-start | bytes 983048 | tf_op jit(solution)/shard_map/ppermute | solution.py:177
  44.2 17.8 %collective-permute-start.6 = (bf16[256,1280]{1,0:T(8,128)(2,1)S(1)}, bf16[256,1280]{1,0:T(8,128)(2,1)}, u32[]{:S(2)}, u32[]{:S(2)}) collective-permute-start(bf16[256,1280]{1,0:T(8,128)(2,1)S(1)} %collective-permute-done.1.rest_1_), channel_id=1, source_target_pairs={{0,8},{8,0},{1,9},{9,1},{2,10},{10,2},{3,11},{11,3},{4,12},{12,4},... | collective-permute-start | bytes 1966088 | tf_op jit(solution)/shard_map/ppermute | solution.py:180
  44.3 17.7 %collective-permute-start.7 = (bf16[256,1280]{1,0:T(8,128)(2,1)S(1)}, bf16[256,1280]{1,0:T(8,128)(2,1)}, u32[]{:S(2)}, u32[]{:S(2)}) collective-permute-start(bf16[256,1280]{1,0:T(8,128)(2,1)S(1)} %collective-permute-done.2.rest_2_), channel_id=1, source_target_pairs={{0,8},{8,0},{1,9},{9,1},{2,10},{10,2},{3,11},{11,3},{4,12},{12,4},... | collective-permute-start | bytes 1966088 | tf_op jit(solution)/shard_map/ppermute | solution.py:180
  44.9 10.4 %collective-permute-start.4 = (bf16[128,1280]{1,0:T(8,128)(2,1)S(1)}, bf16[128,1280]{1,0:T(8,128)(2,1)}, u32[]{:S(2)}, u32[]{:S(2)}) collective-permute-start(bf16[128,1280]{1,0:T(8,128)(2,1)S(1)} %slice.43), channel_id=1, source_target_pairs={{0,96},{32,0},{64,32},{96,64},{1,97},{33,1},{65,33},{97,65},{2,98}... | collective-permute-start | bytes 983048 | tf_op jit(solution)/shard_map/ppermute | solution.py:178
  52.6 9.5 %collective-permute-start.8 = (bf16[128,1280]{1,0:T(8,128)(2,1)}, bf16[128,1280]{1,0:T(8,128)(2,1)}, u32[]{:S(2)}, u32[]{:S(2)}) collective-permute-start(bf16[128,1280]{1,0:T(8,128)(2,1)} %collective-permute-done.3.rest_3_), channel_id=1, source_target_pairs={{0,8},{8,0},{1,9},{9,1},{2,10},{10,2},{3,11},{11,3},{4,12},{12,4},... | collective-permute-start | bytes 983048 | tf_op jit(solution)/shard_map/ppermute | solution.py:180
  55.3 6.8 %collective-permute-start.9 = (bf16[128,1280]{1,0:T(8,128)(2,1)}, bf16[128,1280]{1,0:T(8,128)(2,1)}, u32[]{:S(2)}, u32[]{:S(2)}) collective-permute-start(bf16[128,1280]{1,0:T(8,128)(2,1)} %collective-permute-done.4.rest_4_), channel_id=1, source_target_pairs={{0,8},{8,0},{1,9},{9,1},{2,10},{10,2},{3,11},{11,3},{4,12},{12,4},... | collective-permute-start | bytes 983048 | tf_op jit(solution)/shard_map/ppermute | solution.py:180
  57.8 23.8 %all-to-all-start = ((bf16[8,5,128,128]{3,2,1,0:T(8,128)(2,1)}), bf16[8,5,128,128]{3,2,1,0:T(8,128)(2,1)}, u32[]{:S(2)}, u32[]{:S(2)}) async-start(bf16[8,5,128,128]{3,2,1,0:T(8,128)(2,1)} %pad_maximum_fusion), calls=%async_computation | async-start | bytes 2621440 | tf_op jit(solution)/shard_map/all_to_all | solution.py:210
  81.5 24.7 %all-to-all-start.4 = ((bf16[8,5,128,128]{3,2,1,0:T(8,128)(2,1)}), bf16[8,5,128,128]{3,2,1,0:T(8,128)(2,1)}, u32[]{:S(2)}, u32[]{:S(2)}) async-start(bf16[8,5,128,128]{3,2,1,0:T(8,128)(2,1)} %attend.3), calls=%async_computation.4 | async-start | bytes 2621440 | tf_op jit(solution)/shard_map/all_to_all | solution.py:214
  106.3 24.1 %all-to-all-start.2 = ((bf16[8,5,128,128]{3,2,1,0:T(8,128)(2,1)}), bf16[8,5,128,128]{3,2,1,0:T(8,128)(2,1)S(1)}, u32[]{:S(2)}, u32[]{:S(2)}) async-start(bf16[8,5,128,128]{3,2,1,0:T(8,128)(2,1)} %attend.2), calls=%async_computation.2 | async-start | bytes 2621440 | tf_op jit(solution)/shard_map/all_to_all | solution.py:214

commit v3 on v2

--- a/solution.py
+++ b/solution.py
@@ -1,3 +1,4 @@
+import functools
 import math
 
 import jax
@@ -21,9 +22,10 @@
 PER_BLOCK = KB // SPAN
 BLOCKS = SPANS // PER_BLOCK
 PARTS = 2
-HEADS = GROUP // PARTS
-CHUNK = ROWS * HEADS
-TILE = SPAN * HEADS
+TOKENS = ROWS // PARTS
+CHUNK = TOKENS * GROUP
+TILE = 4 * CHUNK
+OUT = (ULY, TOKENS, 1 + P_SIZE, GROUP, HD)
 WIDTH = HD * (2 + 2 * P_SIZE)
 SCALE = HD**-0.5
 LOG2E = math.log2(math.e)
@@ -49,8 +51,8 @@
     return found
 
 
-def attend(meta, x_ref, *rest):
-    pieces, (out_ref, kv, scores, top, acc, sems) = rest[:10], rest[10:]
+def attend(part, meta, x_ref, *rest):
+    pieces, (out_ref, kv, scores, top, acc, woven, sems) = rest[:10], rest[10:]
     blk = meta[SPANS]
     first = 2 * blk
 
@@ -90,7 +92,8 @@
 
         lax.fori_loop(0, blocks - 1, first_pass, 0)
         last = blocks - 1
-        token = lax.broadcasted_iota(jnp.int32, (TILE, KB), 0) // HEADS
+        row = lax.broadcasted_iota(jnp.int32, (TILE, KB), 0)
+        token = row // CHUNK * ROWS + part * TOKENS + row % CHUNK // GROUP
         key = lax.broadcasted_iota(jnp.int32, (TILE, KB), 1)
         visible = key <= (pos - last * PER_BLOCK) * SPAN + token
         keep(last, jnp.where(visible, score(last), -1e30))
@@ -131,40 +134,72 @@
         inverse = 1.0 / acc[:, HD : 2 * HD]
         primal = acc[:, 0:HD] * inverse
 
-        def put(k, value):
-            out_ref[pl.ds(source, 4), k] = value.astype(BF16).reshape(4, CHUNK, HD)
-
-        put(0, primal)
+        out_ref[pl.ds(source, 4), :, 0] = primal.astype(BF16).reshape(4, TOKENS, GROUP, HD)
         for t in range(P_SIZE):
             c = 2 * (1 + t) * HD
-            put(1 + t, (acc[:, c : c + HD] - primal * acc[:, c + HD : c + 2 * HD]) * inverse)
+            value = (acc[:, c : c + HD] - primal * acc[:, c + HD : c + 2 * HD]) * inverse
+            woven[pl.ds(t, TILE, stride=P_SIZE), :] = value
+        for n in range(4):
+            rows = woven[n * P_SIZE * CHUNK : (n + 1) * P_SIZE * CHUNK, :]
+            out_ref[source + n, :, 1:] = rows.astype(BF16).reshape(TOKENS, P_SIZE, GROUP, HD)
         return unused
 
     lax.fori_loop(0, 2, tile, 0)
 
 
-def attention(meta, x, pieces):
+def attention(meta, x, pieces, part):
     flops = 2 * 2 * TILE * 5 * KB * 11 * KB * HD
     return pl.pallas_call(
-        attend,
-        out_shape=jax.ShapeDtypeStruct(x.shape, BF16),
+        functools.partial(attend, part),
+        grid=(1,),
+        out_shape=jax.ShapeDtypeStruct(OUT, BF16),
         in_specs=[
             pl.BlockSpec(memory_space=pltpu.SMEM),
-            pl.BlockSpec(memory_space=pltpu.VMEM),
+            pl.BlockSpec((ULY, 1 + P_SIZE, CHUNK, HD), lambda i: (0, 0, part, 0)),
         ]
         + [pl.BlockSpec(memory_space=pl.ANY)] * len(pieces),
-        out_specs=pl.BlockSpec(memory_space=pltpu.VMEM),
+        out_specs=pl.BlockSpec(OUT, lambda i: (0, 0, 0, 0, 0)),
         scratch_shapes=[
             pltpu.VMEM((SPANS * SPAN, WIDTH), BF16),
             pltpu.VMEM((BLOCKS, TILE, KB), F32),
             pltpu.VMEM((TILE, HD), F32),
             pltpu.VMEM((TILE, 10 * HD), F32),
+            pltpu.VMEM((P_SIZE * TILE, HD), F32),
             pltpu.SemaphoreType.DMA((SPANS,)),
         ],
-        compiler_params=pltpu.CompilerParams(vmem_limit_bytes=30 * 2**20),
+        compiler_params=pltpu.CompilerParams(vmem_limit_bytes=60 * 2**20),
         cost_estimate=pl.CostEstimate(flops=flops, transcendentals=0, bytes_accessed=8 * 2**20),
         name="attend",
     )(meta, x, *pieces)
+
+
+def place(*refs):
+    parts, (primal_ref, tangent_ref, sems) = refs[:PARTS], refs[PARTS:]
+    copies = []
+    for part in range(PARTS):
+        rows = pl.ds(part * TOKENS, TOKENS)
+        for g in range(ULY):
+            copies.append((parts[part].at[g, :, 1:], tangent_ref.at[rows, g]))
+            copies.append((parts[part].at[g, :, 0], primal_ref.at[rows, g]))
+    copies = [pltpu.make_async_copy(a, b, sems.at[n]) for n, (a, b) in enumerate(copies)]
+    for copy in copies:
+        copy.start()
+    for copy in copies:
+        copy.wait()
+
+
+def assemble(parts):
+    return pl.pallas_call(
+        place,
+        out_shape=(
+            jax.ShapeDtypeStruct((ROWS, ULY, GROUP, HD), BF16),
+            jax.ShapeDtypeStruct((ROWS, ULY, P_SIZE, GROUP, HD), BF16),
+        ),
+        in_specs=[pl.BlockSpec(memory_space=pl.ANY)] * PARTS,
+        out_specs=[pl.BlockSpec(memory_space=pl.ANY)] * 2,
+        scratch_shapes=[pltpu.SemaphoreType.DMA((2 * PARTS * ULY,))],
+        name="place",
+    )(*parts)
 
 
 def gather_blocks(own):
@@ -194,30 +229,24 @@
     head_kv = lax.all_to_all(packed.transpose(1, 0, 2), heads, 0, 0, tiled=True)
     pieces = gather_blocks(head_kv.reshape(ULY * ROWS, WIDTH))
 
-    q = queries.reshape(ROWS, ULY, PARTS, HEADS, HD).transpose(2, 1, 0, 3, 4)
-    qt = query_tangents.reshape(ROWS, ULY, PARTS, HEADS, P_SIZE, HD).transpose(2, 1, 4, 0, 3, 5)
+    q = queries.reshape(ROWS, ULY, GROUP, HD).transpose(1, 0, 2, 3)
+    qt = query_tangents.reshape(ROWS, ULY, GROUP, P_SIZE, HD).transpose(1, 3, 0, 2, 4)
     blk = lax.axis_index(("z", "xh", "core")).astype(jnp.int32)
     meta = jnp.concatenate([span_order, blk[None]])
-    got = []
-    for part in range(PARTS):
-        x = jnp.concatenate(
-            [
-                q[part].reshape(ULY, 1, CHUNK, HD),
-                qt[part].reshape(ULY, P_SIZE, CHUNK, HD),
-            ],
-            axis=1,
-        )
-        got.append(lax.all_to_all(x, heads, 0, 0, tiled=True))
+    x = jnp.concatenate(
+        [
+            q.reshape(ULY, 1, ROWS * GROUP, HD),
+            qt.reshape(ULY, P_SIZE, ROWS * GROUP, HD),
+        ],
+        axis=1,
+    )
+    x = lax.all_to_all(x, heads, 0, 0, tiled=True)
     sent = []
     for part in range(PARTS):
-        out = attention(meta, got[part], pieces)
-        out = lax.all_to_all(out, heads, 0, 0, tiled=True)
-        sent.append(out.reshape(ULY, 1 + P_SIZE, ROWS, HEADS, HD))
-    attention_out = jnp.stack([o[:, 0] for o in sent], axis=1)
-    attention_out = attention_out.transpose(2, 0, 1, 3, 4).reshape(ROWS, HQ, HD)
-    tangent_out = jnp.stack([o[:, 1:] for o in sent], axis=1)
-    tangent_out = tangent_out.transpose(3, 0, 1, 4, 2, 5).reshape(ROWS, HQ, P_SIZE, HD)
-    return attention_out, tangent_out
+        out = attention(meta, x, pieces, part)
+        sent.append(lax.all_to_all(out, heads, 0, 0, tiled=True))
+    primal, tangent = assemble(sent)
+    return primal.reshape(ROWS, HQ, HD), tangent.reshape(ROWS, HQ, P_SIZE, HD)
 
 
 def solution(mesh):

time: 136 us -> 240 us (1.76)
  Pallas kernels: 38.5 us -> 117 us
  waiting for transfers between devices: 35.1 us -> 63.4 us
  blocking collectives: 13.4 us -> 23 us
  local copies, waits for them, and re-layouts: 14.4 us -> 6.75 us
  starting transfers between devices: 29.5 us -> 25.2 us
    pallas_call x2 -> x3, Pallas kernels: 38.5 us -> 117 us  [the longest x1 80.8 us: assemble(): pl.pallas_call(place, out_shape=(jax.ShapeDtypeStruct((ROWS, ULY, GROUP,...]
    ppermute x1, waiting for transfers between devices: 3.52 us -> 35 us  [gather_blocks(): beside = lax.ppermute(own, 'xh', [(0, 1), (1, 0)])]
    ppermute x1, waiting for transfers between devices: 0.01 us -> 12.6 us  [gather_blocks(): above = lax.ppermute(here, 'z', down)]
    all_to_all x4 -> x3, waiting for transfers between devices: 16.7 us -> 6.74 us  [the longest x1 5.68 us: per_device(): head_kv = lax.all_to_all(packed.transpose(1, 0, 2), heads, 0, 0, tiled=True)]
    all_to_all x1, blocking collectives: 13.4 us -> 23 us  [per_device(): sent.append(lax.all_to_all(out, heads, 0, 0, tiled=True))]
    ppermute x1, waiting for transfers between devices: 7.64 us -> 0.01 us  [gather_blocks(): below = lax.ppermute(here, 'z', up)]
    transpose x2 -> x0, local copies, waits for them, and re-layouts: 4.95 us -> none  [the longest x1 4.02 us: per_device(): tangent_out.transpose(3, 0, 1, 4, 2, 5).reshape(ROWS, HQ, P_SIZE, HD)]
    all_to_all x4 -> x3, starting transfers between devices: 18.6 us -> 14 us  [the longest x1 5.51 us: per_device(): head_kv = lax.all_to_all(packed.transpose(1, 0, 2), heads, 0, 0, tiled=True)]
  transfers between devices with their start and end apart: 14 -> 13, of which waited for: 6 -> 7; matrix products, arithmetic and copies ran while one was open for 7% -> 2% of each run, Pallas kernels for 28% -> 7%
where the time goes in v3:
time: 240 us
  Pallas kernels  117 us (49%)
  waiting for transfers between devices  63.4 us (26%)
  starting transfers between devices  25.2 us (10%)
  blocking collectives  23 us (10%)
  local copies, waits for them, and re-layouts  6.75 us (3%)
  other arithmetic  4.04 us (2%)
    pallas_call x1, Pallas kernels, assemble(): pl.pallas_call(place, out_shape=(jax.ShapeDtypeStruct((ROWS, ULY, GROUP,...  80.8 us
    pallas_call x2, Pallas kernels, attention(): pl.pallas_call(functools.partial(attend, part), grid=(1,), out_shape=jax....  35.9 us
    ppermute x1, waiting for transfers between devices, gather_blocks(): beside = lax.ppermute(own, 'xh', [(0, 1), (1, 0)])  35 us
    all_to_all x1, blocking collectives, per_device(): sent.append(lax.all_to_all(out, heads, 0, 0, tiled=True))  23 us
    ppermute x1, waiting for transfers between devices, gather_blocks(): above = lax.ppermute(here, 'z', down)  12.6 us
    all_to_all x1, waiting for transfers between devices, per_device(): head_kv = lax.all_to_all(packed.transpose(1, 0, 2), heads, 0, 0, tiled=True)  5.68 us
    all_to_all x1, starting transfers between devices, per_device(): head_kv = lax.all_to_all(packed.transpose(1, 0, 2), heads, 0, 0, tiled=True)  5.51 us
    all_to_all x1, starting transfers between devices, per_device(): sent.append(lax.all_to_all(out, heads, 0, 0, tiled=True))  4.91 us
  transfers between devices with their start and end apart: 13, of which 7 were waited for; matrix products, arithmetic and copies ran while one was open for 2% of the time, Pallas kernels for 7%

profile of v3, /device:TPU:0, one launch (start us, length us, event | category | flops | bytes accessed | tf_op | source)
XLA Modules:
  0.0 239.9 jit_solution(3508202222661974087)
XLA Ops:
  0.6 0.0 copy-start.2
  0.6 0.0 copy-start.1
  0.6 0.9 copy.11
  1.6 0.8 copy.13
  2.3 1.0 reshape.35
  3.3 1.0 reshape.36
  4.4 0.8 maximum_bitcast_fusion
  5.1 5.5 %all-to-all-start.1 = ((bf16[8,16,1280]{2,1,0:T(8,128)(2,1)}), bf16[8,16,1280]{2,1,0:T(8,128)(2,1)S(1)}, u32[]{:S(2)}, u32[]{:S(2)}) async-start(bf16[8,16,1280]{2,1,0:T(8,128)(2,1)} %maximum_bitcast_fusion), calls=%async_computation.1 | async-start | bytes 655360 | tf_op jit(solution)/shard_map/all_to_all | solution.py:229
  10.6 0.0 copy-done.2
  10.7 0.0 copy-done.1
  10.7 0.5 copy.10
  11.2 1.7 pad_maximum_fusion
  12.9 5.7 %all-to-all-done.1 = bf16[8,16,1280]{2,1,0:T(8,128)(2,1)S(1)} async-done(((bf16[8,16,1280]{2,1,0:T(8,128)(2,1)}), bf16[8,16,1280]{2,1,0:T(8,128)(2,1)S(1)}, u32[]{:S(2)}, u32[]{:S(2)}) %all-to-all-start.1) | async-done | bytes 327712 | tf_op jit(solution)/shard_map/all_to_all | solution.py:229
  18.6 3.6 %all-to-all-start = ((bf16[8,5,256,128]{3,2,1,0:T(8,128)(2,1)}), bf16[8,5,256,128]{3,2,1,0:T(8,128)(2,1)S(1)}, u32[]{:S(2)}, u32[]{:S(2)}) async-start(bf16[8,5,256,128]{3,2,1,0:T(8,128)(2,1)} %pad_maximum_fusion), calls=%async_computation | async-start | bytes 5242880 | tf_op jit(solution)/shard_map/all_to_all | solution.py:243
  22.2 0.0 copy-start.4
  22.2 2.8 %collective-permute-start = (bf16[128,1280]{1,0:T(8,128)(2,1)S(1)}, bf16[128,1280]{1,0:T(8,128)(2,1)S(1)}, u32[]{:S(2)}, u32[]{:S(2)}) collective-permute-start(bf16[128,1280]{1,0:T(8,128)(2,1)S(1)} %bitcast.17), channel_id=1, source_target_pairs={{0,16},{16,0},{1,17},{17,1},{2,18},{18,2},{3,19},{19,3},{4,20},{20... | collective-permute-start | bytes 983048 | tf_op jit(solution)/shard_map/ppermute | solution.py:206
  25.1 35.0 %collective-permute-done = bf16[128,1280]{1,0:T(8,128)(2,1)S(1)} collective-permute-done((bf16[128,1280]{1,0:T(8,128)(2,1)S(1)}, bf16[128,1280]{1,0:T(8,128)(2,1)S(1)}, u32[]{:S(2)}, u32[]{:S(2)}) %collective-permute-start) | collective-permute-done | bytes 327712 | tf_op jit(solution)/shard_map/ppermute | solution.py:206
  60.0 0.9 pad_maximum_fusion.1.rest_0_
  60.9 4.0 %collective-permute-start.2 = (bf16[256,1280]{1,0:T(8,128)(2,1)}, bf16[256,1280]{1,0:T(8,128)(2,1)S(1)}, u32[]{:S(2)}, u32[]{:S(2)}) collective-permute-start(bf16[256,1280]{1,0:T(8,128)(2,1)} %pad_maximum_fusion.1.rest_0_), channel_id=1, source_target_pairs={{0,96},{32,0},{64,32},{96,64},{1,97},{33,1},{65,33},{97,65},{2,98}... | collective-permute-start | bytes 1966088 | tf_op jit(solution)/shard_map/ppermute | solution.py:211
  64.9 0.0 collective-permute-start.1
  65.0 0.0 collective-permute-start.5
  65.0 12.6 %collective-permute-done.2.rest_2_ = bf16[256,1280]{1,0:T(8,128)(2,1)S(1)} collective-permute-done((bf16[256,1280]{1,0:T(8,128)(2,1)}, bf16[256,1280]{1,0:T(8,128)(2,1)S(1)}, u32[]{:S(2)}, u32[]{:S(2)}) %collective-permute-start.2) | collective-permute-done | bytes 655392 | tf_op jit(solution)/shard_map/ppermute | solution.py:211
  77.6 3.7 %collective-permute-start.4 = (bf16[128,1280]{1,0:T(8,128)(2,1)S(1)}, bf16[128,1280]{1,0:T(8,128)(2,1)}, u32[]{:S(2)}, u32[]{:S(2)}) collective-permute-start(bf16[128,1280]{1,0:T(8,128)(2,1)S(1)} %slice.9), channel_id=1, source_target_pairs={{0,96},{32,0},{64,32},{96,64},{1,97},{33,1},{65,33},{97,65},{2,98}... | collective-permute-start | bytes 983048 | tf_op jit(solution)/shard_map/ppermute | solution.py:213
  81.3 0.0 collective-permute-done.1.rest_1_
  81.3 1.0 slice.8
  82.3 0.1 collective-permute-start.3
  82.3 0.1 collective-permute-start.7
  82.4 0.5 collective-permute-start.6
  82.9 2.9 %collective-permute-done.4.rest_4_ = bf16[128,1280]{1,0:T(8,128)(2,1)} collective-permute-done((bf16[128,1280]{1,0:T(8,128)(2,1)S(1)}, bf16[128,1280]{1,0:T(8,128)(2,1)}, u32[]{:S(2)}, u32[]{:S(2)}) %collective-permute-start.4) | collective-permute-done | bytes 327712 | tf_op jit(solution)/shard_map/ppermute | solution.py:213
  85.8 0.0 collective-permute-start.9
  85.9 4.9 %collective-permute-done.3.rest_3_ = bf16[128,1280]{1,0:T(8,128)(2,1)} collective-permute-done((bf16[128,1280]{1,0:T(8,128)(2,1)S(1)}, bf16[128,1280]{1,0:T(8,128)(2,1)}, u32[]{:S(2)}, u32[]{:S(2)}) %collective-permute-start.3) | collective-permute-done | bytes 327712 | tf_op jit(solution)/shard_map/ppermute | solution.py:212
  90.7 0.0 collective-permute-start.8
  90.7 0.0 copy-done.4
  90.7 0.7 pad_add_fusion.meta
  91.4 0.0 collective-permute-done.5.rest_5_
  91.4 0.0 collective-permute-done.9.rest_9_
  91.4 0.0 collective-permute-done.7.rest_7_
  91.4 1.3 collective-permute-done.8.rest_8_
  92.7 0.0 collective-permute-done.6.rest_6_
  92.7 0.0 all-to-all-done.x_ref
  92.7 0.0 copy-done.3
  92.7 1.5 copy-done
  94.2 17.9 %attend.2 = bf16[8,8,5,16,128]{4,3,2,1,0:T(8,128)(2,1)} custom-call(s32[33]{0:T(128)} %pad_add_fusion.meta, bf16[8,5,256,128]{3,2,1,0:T(8,128)(2,1)} %copy-done, bf16[256,1280]{1,0:T(8,128)(2,1)} %pad_maximum_fusion.1.rest_0_, bf16[256,1280]{1,0:T(8,128)(2,1)} %collective-permute-done.1.rest_1_, bf16[256,1280]{1,0:T(8,128)(2,1)} %copy-done.3, ...), custom_call_target="tpu_custom_call" | custom-call | flops 944892805120 | bytes 8388608 | tf_op jit(solution)/shard_map/attend/pallas_call | solution.py:152
  112.1 4.9 %all-to-all-start.2 = ((bf16[8,8,5,16,128]{4,3,2,1,0:T(8,128)(2,1)}), bf16[8,8,5,16,128]{4,3,2,1,0:T(8,128)(2,1)}, u32[]{:S(2)}, u32[]{:S(2)}) async-start(bf16[8,8,5,16,128]{4,3,2,1,0:T(8,128)(2,1)} %attend.2), calls=%async_computation.2 | async-start | bytes 2621440 | tf_op jit(solution)/shard_map/all_to_all | solution.py:247
  117.1 17.9 %attend.3 = bf16[8,8,5,16,128]{4,3,2,1,0:T(8,128)(2,1)} custom-call(s32[33]{0:T(128)} %pad_add_fusion.meta, bf16[8,5,256,128]{3,2,1,0:T(8,128)(2,1)} %copy-done, bf16[256,1280]{1,0:T(8,128)(2,1)} %pad_maximum_fusion.1.rest_0_, bf16[256,1280]{1,0:T(8,128)(2,1)} %collective-permute-done.1.rest_1_, bf16[256,1280]{1,0:T(8,128)(2,1)} %copy-done.3, ...), custom_call_target="tpu_custom_call" | custom-call | flops 944892805120 | bytes 8388608 | tf_op jit(solution)/shard_map/attend/pallas_call | solution.py:152
  135.0 1.1 all-to-all-done.2.refs_0_
  136.0 23.0 %all_to_all.20.refs_1_ = bf16[8,8,5,16,128]{4,3,2,1,0:T(8,128)(2,1)} all-to-all(bf16[8,8,5,16,128]{4,3,2,1,0:T(8,128)(2,1)} %attend.3), channel_id=1, replica_groups=mesh['z'=4,'xh'=2,'core'=2,'y'=4,'xl'=2] {'y','xl'}, dimensions={0} | all-to-all | bytes 2621440 | tf_op jit(solution)/shard_map/all_to_all | solution.py:247
  159.1 80.8 %place.1 = (bf16[16,8,16,128]{3,2,1,0:T(8,128)(2,1)}, bf16[16,8,4,16,128]{4,3,2,1,0:T(8,128)(2,1)}) custom-call(bf16[8,8,5,16,128]{4,3,2,1,0:T(8,128)(2,1)} %all-to-all-done.2.refs_0_, bf16[8,8,5,16,128]{4,3,2,1,0:T(8,128)(2,1)} %all_to_all.20.refs_1_), custom_call_target="tpu_custom_call" | custom-call | tf_op jit(solution)/shard_map/place/pallas_call | solution.py:192
  (6 shorter events, 0.1 us)
Async XLA Ops:
  0.6 10.0 %copy-start.2 = (bf16[16,128,128]{2,1,0:T(8,128)(2,1)S(1)}, bf16[16,128,128]{2,1,0:T(8,128)(2,1)}, u32[]{:S(2)}) copy-start(bf16[16,128,128]{2,1,0:T(8,128)(2,1)} %param.7) | copy-start | bytes 1572868
  0.6 10.0 %copy-start.1 = (bf16[16,128,4,128]{3,2,1,0:T(4,128)(2,1)S(1)}, bf16[16,128,4,128]{3,2,1,0:T(4,128)(2,1)}, u32[]{:S(2)}) copy-start(bf16[16,128,4,128]{3,2,1,0:T(4,128)(2,1)} %param.8) | copy-start | bytes 6291460
  5.1 13.5 %all-to-all-start.1 = ((bf16[8,16,1280]{2,1,0:T(8,128)(2,1)}), bf16[8,16,1280]{2,1,0:T(8,128)(2,1)S(1)}, u32[]{:S(2)}, u32[]{:S(2)}) async-start(bf16[8,16,1280]{2,1,0:T(8,128)(2,1)} %maximum_bitcast_fusion), calls=%async_computation.1 | async-start | bytes 655360 | tf_op jit(solution)/shard_map/all_to_all | solution.py:229
  18.6 74.1 %all-to-all-start = ((bf16[8,5,256,128]{3,2,1,0:T(8,128)(2,1)}), bf16[8,5,256,128]{3,2,1,0:T(8,128)(2,1)S(1)}, u32[]{:S(2)}, u32[]{:S(2)}) async-start(bf16[8,5,256,128]{3,2,1,0:T(8,128)(2,1)} %pad_maximum_fusion), calls=%async_computation | async-start | bytes 5242880 | tf_op jit(solution)/shard_map/all_to_all | solution.py:243
  22.2 68.5 %copy-start.4 = (s32[32]{0:T(128)S(1)}, s32[32]{0:T(128)}, u32[]{:S(2)}) copy-start(s32[32]{0:T(128)} %param.13) | copy-start | bytes 388
  22.2 37.8 %collective-permute-start = (bf16[128,1280]{1,0:T(8,128)(2,1)S(1)}, bf16[128,1280]{1,0:T(8,128)(2,1)S(1)}, u32[]{:S(2)}, u32[]{:S(2)}) collective-permute-start(bf16[128,1280]{1,0:T(8,128)(2,1)S(1)} %bitcast.17), channel_id=1, source_target_pairs={{0,16},{16,0},{1,17},{17,1},{2,18},{18,2},{3,19},{19,3},{4,20},{20... | collective-permute-start | bytes 983048 | tf_op jit(solution)/shard_map/ppermute | solution.py:206
  60.9 16.7 %collective-permute-start.2 = (bf16[256,1280]{1,0:T(8,128)(2,1)}, bf16[256,1280]{1,0:T(8,128)(2,1)S(1)}, u32[]{:S(2)}, u32[]{:S(2)}) collective-permute-start(bf16[256,1280]{1,0:T(8,128)(2,1)} %pad_maximum_fusion.1.rest_0_), channel_id=1, source_target_pairs={{0,96},{32,0},{64,32},{96,64},{1,97},{33,1},{65,33},{97,65},{2,98}... | collective-permute-start | bytes 1966088 | tf_op jit(solution)/shard_map/ppermute | solution.py:211
  64.9 16.3 %collective-permute-start.1 = (bf16[256,1280]{1,0:T(8,128)(2,1)}, bf16[256,1280]{1,0:T(8,128)(2,1)}, u32[]{:S(2)}, u32[]{:S(2)}) collective-permute-start(bf16[256,1280]{1,0:T(8,128)(2,1)} %pad_maximum_fusion.1.rest_0_), channel_id=1, source_target_pairs={{0,32},{32,64},{64,96},{96,0},{1,33},{33,65},{65,97},{97,1},{2,34}... | collective-permute-start | bytes 1966088 | tf_op jit(solution)/shard_map/ppermute | solution.py:210
  65.0 26.4 %collective-permute-start.5 = (bf16[256,1280]{1,0:T(8,128)(2,1)}, bf16[256,1280]{1,0:T(8,128)(2,1)}, u32[]{:S(2)}, u32[]{:S(2)}) collective-permute-start(bf16[256,1280]{1,0:T(8,128)(2,1)} %pad_maximum_fusion.1.rest_0_), channel_id=1, source_target_pairs={{0,8},{8,0},{1,9},{9,1},{2,10},{10,2},{3,11},{11,3},{4,12},{12,4},... | collective-permute-start | bytes 1966088 | tf_op jit(solution)/shard_map/ppermute | solution.py:215
  77.6 15.1 %copy-start.3 = (bf16[256,1280]{1,0:T(8,128)(2,1)}, bf16[256,1280]{1,0:T(8,128)(2,1)S(1)}, u32[]{:S(2)}) copy-start(bf16[256,1280]{1,0:T(8,128)(2,1)S(1)} %collective-permute-done.2.rest_2_) | copy-start | bytes 1966084
  77.6 8.2 %collective-permute-start.4 = (bf16[128,1280]{1,0:T(8,128)(2,1)S(1)}, bf16[128,1280]{1,0:T(8,128)(2,1)}, u32[]{:S(2)}, u32[]{:S(2)}) collective-permute-start(bf16[128,1280]{1,0:T(8,128)(2,1)S(1)} %slice.9), channel_id=1, source_target_pairs={{0,96},{32,0},{64,32},{96,64},{1,97},{33,1},{65,33},{97,65},{2,98}... | collective-permute-start | bytes 983048 | tf_op jit(solution)/shard_map/ppermute | solution.py:213
  82.3 8.5 %collective-permute-start.3 = (bf16[128,1280]{1,0:T(8,128)(2,1)S(1)}, bf16[128,1280]{1,0:T(8,128)(2,1)}, u32[]{:S(2)}, u32[]{:S(2)}) collective-permute-start(bf16[128,1280]{1,0:T(8,128)(2,1)S(1)} %slice.8), channel_id=1, source_target_pairs={{0,32},{32,64},{64,96},{96,0},{1,33},{33,65},{65,97},{97,1},{2,34}... | collective-permute-start | bytes 983048 | tf_op jit(solution)/shard_map/ppermute | solution.py:212
  82.3 9.1 %collective-permute-start.7 = (bf16[256,1280]{1,0:T(8,128)(2,1)S(1)}, bf16[256,1280]{1,0:T(8,128)(2,1)}, u32[]{:S(2)}, u32[]{:S(2)}) collective-permute-start(bf16[256,1280]{1,0:T(8,128)(2,1)S(1)} %collective-permute-done.2.rest_2_), channel_id=1, source_target_pairs={{0,8},{8,0},{1,9},{9,1},{2,10},{10,2},{3,11},{11,3},{4,12},{12,4},... | collective-permute-start | bytes 1966088 | tf_op jit(solution)/shard_map/ppermute | solution.py:215
  82.4 10.3 %collective-permute-start.6 = (bf16[256,1280]{1,0:T(8,128)(2,1)}, bf16[256,1280]{1,0:T(8,128)(2,1)}, u32[]{:S(2)}, u32[]{:S(2)}) collective-permute-start(bf16[256,1280]{1,0:T(8,128)(2,1)} %collective-permute-done.1.rest_1_), channel_id=1, source_target_pairs={{0,8},{8,0},{1,9},{9,1},{2,10},{10,2},{3,11},{11,3},{4,12},{12,4},... | collective-permute-start | bytes 1966088 | tf_op jit(solution)/shard_map/ppermute | solution.py:215
  85.8 5.5 %collective-permute-start.9 = (bf16[128,1280]{1,0:T(8,128)(2,1)}, bf16[128,1280]{1,0:T(8,128)(2,1)}, u32[]{:S(2)}, u32[]{:S(2)}) collective-permute-start(bf16[128,1280]{1,0:T(8,128)(2,1)} %collective-permute-done.4.rest_4_), channel_id=1, source_target_pairs={{0,8},{8,0},{1,9},{9,1},{2,10},{10,2},{3,11},{11,3},{4,12},{12,4},... | collective-permute-start | bytes 983048 | tf_op jit(solution)/shard_map/ppermute | solution.py:215
  90.7 2.0 collective-permute-start.8
  92.7 1.5 copy-start
  112.1 23.9 %all-to-all-start.2 = ((bf16[8,8,5,16,128]{4,3,2,1,0:T(8,128)(2,1)}), bf16[8,8,5,16,128]{4,3,2,1,0:T(8,128)(2,1)}, u32[]{:S(2)}, u32[]{:S(2)}) async-start(bf16[8,8,5,16,128]{4,3,2,1,0:T(8,128)(2,1)} %attend.2), calls=%async_computation.2 | async-start | bytes 2621440 | tf_op jit(solution)/shard_map/all_to_all | solution.py:247

commit v4 on v3

--- a/solution.py
+++ b/solution.py
@@ -38,14 +38,14 @@
     return lax.dot_general(a, b, (((1,), (1,)), ((), ())), preferred_element_type=F32)
 
 
-def pieces_of(z, xh, core):
+def pieces_of(z, core):
     found = []
     for other_core in range(2):
         at = 5 * other_core
         c = core ^ other_core
         for operand, step, halves in ((0, 0, (0, 1)), (1, 3, (0, 1)), (2, 1, (0, 1)), (3, 2, (0,)), (4, 2, (1,))):
             for place, h in enumerate(halves):
-                block = (((z + step) % 4) * 2 + (xh ^ h)) * 2 + c
+                block = (((z + step) % 4) * 2 + h) * 2 + c
                 for s in range(2):
                     found.append((at + operand, place * 2 * SPAN + s * SPAN, 2 * block + s))
     return found
@@ -56,7 +56,7 @@
     blk = meta[SPANS]
     first = 2 * blk
 
-    for n, (operand, row, stored) in enumerate(pieces_of(blk // 4, (blk // 2) % 2, blk % 2)):
+    for n, (operand, row, stored) in enumerate(pieces_of(blk // 4, blk % 2)):
         at = pl.multiple_of(meta[stored] * SPAN, SPAN)
         pltpu.make_async_copy(
             pieces[operand].at[pl.ds(row, SPAN), :], kv.at[pl.ds(at, SPAN), :], sems.at[n]
@@ -173,38 +173,40 @@
     )(meta, x, *pieces)
 
 
-def place(*refs):
-    parts, (primal_ref, tangent_ref, sems) = refs[:PARTS], refs[PARTS:]
-    copies = []
-    for part in range(PARTS):
-        rows = pl.ds(part * TOKENS, TOKENS)
-        for g in range(ULY):
-            copies.append((parts[part].at[g, :, 1:], tangent_ref.at[rows, g]))
-            copies.append((parts[part].at[g, :, 0], primal_ref.at[rows, g]))
-    copies = [pltpu.make_async_copy(a, b, sems.at[n]) for n, (a, b) in enumerate(copies)]
-    for copy in copies:
-        copy.start()
-    for copy in copies:
-        copy.wait()
+def place(part_ref, *refs):
+    primal_ref, tangent_ref = refs[-2:]
+    for g in range(ULY):
+        primal_ref[:, g] = part_ref[g, :, 0]
+        tangent_ref[:, g] = part_ref[g, :, 1:]
 
 
 def assemble(parts):
-    return pl.pallas_call(
-        place,
-        out_shape=(
-            jax.ShapeDtypeStruct((ROWS, ULY, GROUP, HD), BF16),
-            jax.ShapeDtypeStruct((ROWS, ULY, P_SIZE, GROUP, HD), BF16),
-        ),
-        in_specs=[pl.BlockSpec(memory_space=pl.ANY)] * PARTS,
-        out_specs=[pl.BlockSpec(memory_space=pl.ANY)] * 2,
-        scratch_shapes=[pltpu.SemaphoreType.DMA((2 * PARTS * ULY,))],
-        name="place",
-    )(*parts)
-
-
-def gather_blocks(own):
-    beside = lax.ppermute(own, "xh", [(0, 1), (1, 0)])
-    here = jnp.concatenate([own, beside], axis=0)
+    step = 2
+    steps = TOKENS // step
+    placed = ()
+    for n, part in enumerate(parts):
+        placed = pl.pallas_call(
+            place,
+            grid=(steps,),
+            out_shape=(
+                jax.ShapeDtypeStruct((ROWS, ULY, GROUP, HD), BF16),
+                jax.ShapeDtypeStruct((ROWS, ULY, P_SIZE, GROUP, HD), BF16),
+            ),
+            in_specs=[pl.BlockSpec((ULY, step, 1 + P_SIZE, GROUP, HD), lambda i: (0, i, 0, 0, 0))]
+            + [pl.BlockSpec(memory_space=pl.ANY)] * len(placed),
+            out_specs=(
+                pl.BlockSpec((step, ULY, GROUP, HD), lambda i, n=n: (n * steps + i, 0, 0, 0)),
+                pl.BlockSpec(
+                    (step, ULY, P_SIZE, GROUP, HD), lambda i, n=n: (n * steps + i, 0, 0, 0, 0)
+                ),
+            ),
+            input_output_aliases={1 + k: k for k in range(len(placed))},
+            name="place",
+        )(part, *placed)
+    return placed
+
+
+def gather_blocks(here):
     up = [(i, (i + 1) % 4) for i in range(4)]
     down = [(i, (i + 3) % 4) for i in range(4)]
     below = lax.ppermute(here, "z", up)
@@ -226,8 +228,10 @@
         axis=2,
     )
     heads = ("y", "xl")
-    head_kv = lax.all_to_all(packed.transpose(1, 0, 2), heads, 0, 0, tiled=True)
-    pieces = gather_blocks(head_kv.reshape(ULY * ROWS, WIDTH))
+    packed = packed.transpose(1, 0, 2)
+    packed = jnp.concatenate([packed, packed], axis=0)
+    head_kv = lax.all_to_all(packed, ("xh",) + heads, 0, 0, tiled=True)
+    pieces = gather_blocks(head_kv.reshape(2 * ULY * ROWS, WIDTH))
 
     q = queries.reshape(ROWS, ULY, GROUP, HD).transpose(1, 0, 2, 3)
     qt = query_tangents.reshape(ROWS, ULY, GROUP, P_SIZE, HD).transpose(1, 3, 0, 2, 4)

time: 240 us -> 134 us (0.56)
  Pallas kernels: 117 us -> 42.8 us
  blocking collectives: 23 us -> 0 us
  waiting for transfers between devices: 63.4 us -> 48.1 us
  starting transfers between devices: 25.2 us -> 29.6 us
    pallas_call x1 -> x2, Pallas kernels: 80.8 us -> 6.93 us  [assemble(): pl.pallas_call(place, grid=(steps,), out_shape=(jax.ShapeDtypeStruct((ROW...]
    ppermute x1 -> x0, waiting for transfers between devices: 35 us -> none  [gather_blocks(): beside = lax.ppermute(own, 'xh', [(0, 1), (1, 0)])]
    all_to_all x1 -> x0, blocking collectives: 23 us -> none  [per_device(): sent.append(lax.all_to_all(out, heads, 0, 0, tiled=True))]
    all_to_all x1 -> x2, waiting for transfers between devices: 1.05 us -> 15.8 us  [per_device(): sent.append(lax.all_to_all(out, heads, 0, 0, tiled=True))]
    all_to_all x1 -> x2, starting transfers between devices: 4.91 us -> 10 us  [per_device(): sent.append(lax.all_to_all(out, heads, 0, 0, tiled=True))]
    all_to_all x1, waiting for transfers between devices: 5.68 us -> 10.6 us  [per_device(): head_kv = lax.all_to_all(packed, ('xh',) + heads, 0, 0, tiled=True)]
    ppermute x1 -> x0, starting transfers between devices: 2.81 us -> none  [gather_blocks(): beside = lax.ppermute(own, 'xh', [(0, 1), (1, 0)])]
  transfers between devices with their start and end apart: 13 -> 13, of which waited for: 7 -> 7; matrix products, arithmetic and copies ran while one was open for 2% -> 4% of each run, Pallas kernels for 7% -> 16%
where the time goes in v4:
time: 134 us; the launch traced here: 133 us
  waiting for transfers between devices  48.1 us (36%)
  Pallas kernels  42.8 us (32%)
  starting transfers between devices  29.6 us (22%)
  local copies, waits for them, and re-layouts  8.65 us (6%)
  other arithmetic  3.26 us (2%)
    pallas_call x2, Pallas kernels, attention(): pl.pallas_call(functools.partial(attend, part), grid=(1,), out_shape=jax....  35.9 us
    all_to_all x2, waiting for transfers between devices, per_device(): sent.append(lax.all_to_all(out, heads, 0, 0, tiled=True))  15.8 us
    ppermute x1, waiting for transfers between devices, gather_blocks(): above = lax.ppermute(here, 'z', down)  12.6 us
    all_to_all x1, waiting for transfers between devices, per_device(): head_kv = lax.all_to_all(packed, ('xh',) + heads, 0, 0, tiled=True)  10.6 us
    all_to_all x2, starting transfers between devices, per_device(): sent.append(lax.all_to_all(out, heads, 0, 0, tiled=True))  10 us
    all_to_all x1, starting transfers between devices, per_device(): head_kv = lax.all_to_all(packed, ('xh',) + heads, 0, 0, tiled=True)  7.28 us
    pallas_call x2, Pallas kernels, assemble(): pl.pallas_call(place, grid=(steps,), out_shape=(jax.ShapeDtypeStruct((ROW...  6.93 us
    ppermute x1, waiting for transfers between devices, gather_blocks(): far_low = lax.ppermute(below[:2 * SPAN], 'z', up)  4.73 us
  transfers between devices with their start and end apart: 13, of which 7 were waited for; matrix products, arithmetic and copies ran while one was open for 4% of the time, Pallas kernels for 16%

profile of v4, /device:TPU:0, one launch (start us, length us, event | category | flops | bytes accessed | tf_op | source)
XLA Modules:
  0.0 133.2 jit_solution(8908998941066395200)
XLA Ops:
  0.6 0.8 copy.13
  1.4 0.8 copy.15
  2.2 1.0 reshape.35
  3.2 1.0 reshape.36
  4.1 0.0 copy-start.2
  4.2 0.0 copy-start.4
  4.3 0.9 pad_maximum_fusion.1
  5.1 7.3 %all-to-all-start.1 = ((bf16[16,16,1280]{2,1,0:T(8,128)(2,1)}), bf16[16,16,1280]{2,1,0:T(8,128)(2,1)S(1)}, u32[]{:S(2)}, u32[]{:S(2)}) async-start(bf16[16,16,1280]{2,1,0:T(8,128)(2,1)} %pad_maximum_fusion.1), calls=%async_computation.1 | async-start | bytes 1310720 | tf_op jit(solution)/shard_map/all_to_all | solution.py:233
  12.4 0.0 copy-done.4
  12.5 0.0 copy-done.2
  12.5 0.5 copy.12
  13.0 1.7 %pad_maximum_fusion = bf16[8,5,256,128]{3,2,1,0:T(8,128)(2,1)} fusion(bf16[8,4,256,128]{3,2,1,0:T(8,128)(2,1)S(1)} %bitcast.14, bf16[8,1,256,128]{3,2,1,0:T(8,128)(2,1)S(1)} %bitcast.15), kind=kLoop, calls=%fused_computation | loop fusion | flops 1310720 | bytes 5242880 | tf_op jit(solution)/shard_map/concatenate | solution.py:240
  14.7 10.6 %all-to-all-done.1 = bf16[16,16,1280]{2,1,0:T(8,128)(2,1)S(1)} async-done(((bf16[16,16,1280]{2,1,0:T(8,128)(2,1)}), bf16[16,16,1280]{2,1,0:T(8,128)(2,1)S(1)}, u32[]{:S(2)}, u32[]{:S(2)}) %all-to-all-start.1) | async-done | bytes 655392 | tf_op jit(solution)/shard_map/all_to_all | solution.py:233
  25.4 3.6 %all-to-all-start = ((bf16[8,5,256,128]{3,2,1,0:T(8,128)(2,1)}), bf16[8,5,256,128]{3,2,1,0:T(8,128)(2,1)S(1)}, u32[]{:S(2)}, u32[]{:S(2)}) async-start(bf16[8,5,256,128]{3,2,1,0:T(8,128)(2,1)} %pad_maximum_fusion), calls=%async_computation | async-start | bytes 5242880 | tf_op jit(solution)/shard_map/all_to_all | solution.py:247
  29.0 4.1 %collective-permute-start.1 = (bf16[256,1280]{1,0:T(8,128)(2,1)S(1)}, bf16[256,1280]{1,0:T(8,128)(2,1)}, u32[]{:S(2)}, u32[]{:S(2)}) collective-permute-start(bf16[256,1280]{1,0:T(8,128)(2,1)S(1)} %bitcast.18), channel_id=1, source_target_pairs={{0,96},{32,0},{64,32},{96,64},{1,97},{33,1},{65,33},{97,65},{2,98}... | collective-permute-start | bytes 1966088 | tf_op jit(solution)/shard_map/ppermute | solution.py:213
  33.1 0.0 collective-permute-start
  33.1 0.0 copy-done.3
  33.1 0.0 collective-permute-start.4
  33.1 12.6 %collective-permute-done.1.rest_2_ = bf16[256,1280]{1,0:T(8,128)(2,1)} collective-permute-done((bf16[256,1280]{1,0:T(8,128)(2,1)S(1)}, bf16[256,1280]{1,0:T(8,128)(2,1)}, u32[]{:S(2)}, u32[]{:S(2)}) %collective-permute-start.1) | collective-permute-done | bytes 655392 | tf_op jit(solution)/shard_map/ppermute | solution.py:213
  45.7 1.0 slice.9
  46.7 3.9 %collective-permute-start.3 = (bf16[128,1280]{1,0:T(8,128)(2,1)S(1)}, bf16[128,1280]{1,0:T(8,128)(2,1)}, u32[]{:S(2)}, u32[]{:S(2)}) collective-permute-start(bf16[128,1280]{1,0:T(8,128)(2,1)S(1)} %slice.9), channel_id=1, source_target_pairs={{0,96},{32,0},{64,32},{96,64},{1,97},{33,1},{65,33},{97,65},{2,98}... | collective-permute-start | bytes 983048 | tf_op jit(solution)/shard_map/ppermute | solution.py:215
  50.6 0.0 collective-permute-done.rest_1_
  50.6 1.0 slice.8
  51.6 0.1 collective-permute-start.2
  51.7 0.1 collective-permute-start.6
  51.7 0.5 collective-permute-start.5
  52.2 3.0 %collective-permute-done.3.rest_4_ = bf16[128,1280]{1,0:T(8,128)(2,1)} collective-permute-done((bf16[128,1280]{1,0:T(8,128)(2,1)S(1)}, bf16[128,1280]{1,0:T(8,128)(2,1)}, u32[]{:S(2)}, u32[]{:S(2)}) %collective-permute-start.3) | collective-permute-done | bytes 327712 | tf_op jit(solution)/shard_map/ppermute | solution.py:215
  55.3 0.0 collective-permute-start.8
  55.3 4.7 %collective-permute-done.2.rest_3_ = bf16[128,1280]{1,0:T(8,128)(2,1)} collective-permute-done((bf16[128,1280]{1,0:T(8,128)(2,1)S(1)}, bf16[128,1280]{1,0:T(8,128)(2,1)}, u32[]{:S(2)}, u32[]{:S(2)}) %collective-permute-start.2) | collective-permute-done | bytes 327712 | tf_op jit(solution)/shard_map/ppermute | solution.py:214
  60.0 0.0 collective-permute-start.7
  60.0 0.0 copy-done.5
  60.0 0.6 pad_add_fusion.meta
  60.6 0.0 collective-permute-done.4.rest_5_
  60.6 0.0 collective-permute-done.8.rest_9_
  60.7 0.0 collective-permute-done.6.rest_7_
  60.7 1.3 %collective-permute-done.7.rest_8_ = bf16[128,1280]{1,0:T(8,128)(2,1)} collective-permute-done((bf16[128,1280]{1,0:T(8,128)(2,1)}, bf16[128,1280]{1,0:T(8,128)(2,1)}, u32[]{:S(2)}, u32[]{:S(2)}) %collective-permute-start.7) | collective-permute-done | bytes 327712 | tf_op jit(solution)/shard_map/ppermute | solution.py:217
  62.0 0.0 collective-permute-done.5.rest_6_
  62.0 0.0 all-to-all-done.x_ref
  62.0 1.5 %copy-done.1 = bf16[8,5,256,128]{3,2,1,0:T(8,128)(2,1)} copy-done((bf16[8,5,256,128]{3,2,1,0:T(8,128)(2,1)}, bf16[8,5,256,128]{3,2,1,0:T(8,128)(2,1)S(1)}, u32[]{:S(2)}) %copy-start.1) | copy-done | bytes 2621464
  63.5 17.9 %attend.3 = bf16[8,8,5,16,128]{4,3,2,1,0:T(8,128)(2,1)} custom-call(s32[33]{0:T(128)} %pad_add_fusion.meta, bf16[8,5,256,128]{3,2,1,0:T(8,128)(2,1)} %copy-done.1, bf16[256,1280]{1,0:T(8,128)(2,1)} %bitcast.21, bf16[256,1280]{1,0:T(8,128)(2,1)} %collective-permute-done.rest_1_, bf16[256,1280]{1,0:T(8,128)(2,1)} %collective-permute-done.1.rest_2_, ...), custom_call_target="tpu_custom_call" | custom-call | flops 944892805120 | bytes 8388608 | tf_op jit(solution)/shard_map/attend/pallas_call | solution.py:152
  81.4 5.3 %all-to-all-start.3 = ((bf16[8,8,5,16,128]{4,3,2,1,0:T(8,128)(2,1)}), bf16[8,8,5,16,128]{4,3,2,1,0:T(8,128)(2,1)}, u32[]{:S(2)}, u32[]{:S(2)}) async-start(bf16[8,8,5,16,128]{4,3,2,1,0:T(8,128)(2,1)} %attend.3), calls=%async_computation.3 | async-start | bytes 2621440 | tf_op jit(solution)/shard_map/all_to_all | solution.py:251
  86.7 18.0 %attend.2 = bf16[8,8,5,16,128]{4,3,2,1,0:T(8,128)(2,1)} custom-call(s32[33]{0:T(128)} %pad_add_fusion.meta, bf16[8,5,256,128]{3,2,1,0:T(8,128)(2,1)} %copy-done.1, bf16[256,1280]{1,0:T(8,128)(2,1)} %bitcast.22, bf16[256,1280]{1,0:T(8,128)(2,1)} %collective-permute-done.rest_1_, bf16[256,1280]{1,0:T(8,128)(2,1)} %collective-permute-done.1.rest_2_, ...), custom_call_target="tpu_custom_call" | custom-call | flops 944892805120 | bytes 8388608 | tf_op jit(solution)/shard_map/attend/pallas_call | solution.py:152
  104.7 1.0 all-to-all-done.3.part_ref
  105.7 4.7 %all-to-all-start.2 = ((bf16[8,8,5,16,128]{4,3,2,1,0:T(8,128)(2,1)}), bf16[8,8,5,16,128]{4,3,2,1,0:T(8,128)(2,1)S(1)}, u32[]{:S(2)}, u32[]{:S(2)}) async-start(bf16[8,8,5,16,128]{4,3,2,1,0:T(8,128)(2,1)} %attend.2), calls=%async_computation.2 | async-start | bytes 2621440 | tf_op jit(solution)/shard_map/all_to_all | solution.py:251
  110.4 3.5 %place.2 = (bf16[16,8,16,128]{3,2,1,0:T(8,128)(2,1)}, bf16[16,8,4,16,128]{4,3,2,1,0:T(8,128)(2,1)}) custom-call(bf16[8,8,5,16,128]{4,3,2,1,0:T(8,128)(2,1)} %all-to-all-done.3.part_ref), custom_call_target="tpu_custom_call" | custom-call | tf_op jit(solution)/shard_map/place/pallas_call | solution.py:188
  113.9 14.8 %all-to-all-done.2.part_ref = bf16[8,8,5,16,128]{4,3,2,1,0:T(8,128)(2,1)S(1)} async-done(((bf16[8,8,5,16,128]{4,3,2,1,0:T(8,128)(2,1)}), bf16[8,8,5,16,128]{4,3,2,1,0:T(8,128)(2,1)S(1)}, u32[]{:S(2)}, u32[]{:S(2)}) %all-to-all-start.2) | async-done | bytes 1310752 | tf_op jit(solution)/shard_map/all_to_all | solution.py:251
  128.7 1.1 copy-done
  129.8 3.5 %place.3 = (bf16[16,8,16,128]{3,2,1,0:T(8,128)(2,1)}, bf16[16,8,4,16,128]{4,3,2,1,0:T(8,128)(2,1)}) custom-call(bf16[8,8,5,16,128]{4,3,2,1,0:T(8,128)(2,1)} %copy-done, bf16[16,8,16,128]{3,2,1,0:T(8,128)(2,1)} %get-tuple-element.6.refs_0_, bf16[16,8,4,16,128]{4,3,2,1,0:T(8,128)(2,1)} %get-tuple-element.7.refs_1_), custom_call_target="tpu_custom_call", output_to_operand_aliasing={{0}: (1, {}), {1}: (2, {})} | custom-call | tf_op jit(solution)/shard_map/place/pallas_call | solution.py:188
  (8 shorter events, 0.2 us)
Async XLA Ops:
  4.1 8.3 %copy-start.2 = (bf16[16,128,4,128]{3,2,1,0:T(4,128)(2,1)S(1)}, bf16[16,128,4,128]{3,2,1,0:T(4,128)(2,1)}, u32[]{:S(2)}) copy-start(bf16[16,128,4,128]{3,2,1,0:T(4,128)(2,1)} %param.8) | copy-start | bytes 6291460
  4.2 8.2 %copy-start.4 = (bf16[16,128,128]{2,1,0:T(8,128)(2,1)S(1)}, bf16[16,128,128]{2,1,0:T(8,128)(2,1)}, u32[]{:S(2)}) copy-start(bf16[16,128,128]{2,1,0:T(8,128)(2,1)} %param.7) | copy-start | bytes 1572868
  5.1 20.2 %all-to-all-start.1 = ((bf16[16,16,1280]{2,1,0:T(8,128)(2,1)}), bf16[16,16,1280]{2,1,0:T(8,128)(2,1)S(1)}, u32[]{:S(2)}, u32[]{:S(2)}) async-start(bf16[16,16,1280]{2,1,0:T(8,128)(2,1)} %pad_maximum_fusion.1), calls=%async_computation.1 | async-start | bytes 1310720 | tf_op jit(solution)/shard_map/all_to_all | solution.py:233
  14.7 45.3 %copy-start.5 = (s32[32]{0:T(128)S(1)}, s32[32]{0:T(128)}, u32[]{:S(2)}) copy-start(s32[32]{0:T(128)} %param.13) | copy-start | bytes 388
  25.4 7.7 %copy-start.3 = (bf16[16,16,1280]{2,1,0:T(8,128)(2,1)}, bf16[16,16,1280]{2,1,0:T(8,128)(2,1)S(1)}, u32[]{:S(2)}) copy-start(bf16[16,16,1280]{2,1,0:T(8,128)(2,1)S(1)} %all-to-all-done.1) | copy-start | bytes 1966084
  25.4 36.6 %all-to-all-start = ((bf16[8,5,256,128]{3,2,1,0:T(8,128)(2,1)}), bf16[8,5,256,128]{3,2,1,0:T(8,128)(2,1)S(1)}, u32[]{:S(2)}, u32[]{:S(2)}) async-start(bf16[8,5,256,128]{3,2,1,0:T(8,128)(2,1)} %pad_maximum_fusion), calls=%async_computation | async-start | bytes 5242880 | tf_op jit(solution)/shard_map/all_to_all | solution.py:247
  29.0 16.7 %collective-permute-start.1 = (bf16[256,1280]{1,0:T(8,128)(2,1)S(1)}, bf16[256,1280]{1,0:T(8,128)(2,1)}, u32[]{:S(2)}, u32[]{:S(2)}) collective-permute-start(bf16[256,1280]{1,0:T(8,128)(2,1)S(1)} %bitcast.18), channel_id=1, source_target_pairs={{0,96},{32,0},{64,32},{96,64},{1,97},{33,1},{65,33},{97,65},{2,98}... | collective-permute-start | bytes 1966088 | tf_op jit(solution)/shard_map/ppermute | solution.py:213
  33.1 17.5 %collective-permute-start = (bf16[256,1280]{1,0:T(8,128)(2,1)S(1)}, bf16[256,1280]{1,0:T(8,128)(2,1)}, u32[]{:S(2)}, u32[]{:S(2)}) collective-permute-start(bf16[256,1280]{1,0:T(8,128)(2,1)S(1)} %bitcast.19), channel_id=1, source_target_pairs={{0,32},{32,64},{64,96},{96,0},{1,33},{33,65},{65,97},{97,1},{2,34}... | collective-permute-start | bytes 1966088 | tf_op jit(solution)/shard_map/ppermute | solution.py:212
  33.1 27.5 %collective-permute-start.4 = (bf16[256,1280]{1,0:T(8,128)(2,1)S(1)}, bf16[256,1280]{1,0:T(8,128)(2,1)}, u32[]{:S(2)}, u32[]{:S(2)}) collective-permute-start(bf16[256,1280]{1,0:T(8,128)(2,1)S(1)} %bitcast.20), channel_id=1, source_target_pairs={{0,8},{8,0},{1,9},{9,1},{2,10},{10,2},{3,11},{11,3},{4,12},{12,4},... | collective-permute-start | bytes 1966088 | tf_op jit(solution)/shard_map/ppermute | solution.py:217
  46.7 8.6 %collective-permute-start.3 = (bf16[128,1280]{1,0:T(8,128)(2,1)S(1)}, bf16[128,1280]{1,0:T(8,128)(2,1)}, u32[]{:S(2)}, u32[]{:S(2)}) collective-permute-start(bf16[128,1280]{1,0:T(8,128)(2,1)S(1)} %slice.9), channel_id=1, source_target_pairs={{0,96},{32,0},{64,32},{96,64},{1,97},{33,1},{65,33},{97,65},{2,98}... | collective-permute-start | bytes 983048 | tf_op jit(solution)/shard_map/ppermute | solution.py:215
  51.6 8.5 %collective-permute-start.2 = (bf16[128,1280]{1,0:T(8,128)(2,1)S(1)}, bf16[128,1280]{1,0:T(8,128)(2,1)}, u32[]{:S(2)}, u32[]{:S(2)}) collective-permute-start(bf16[128,1280]{1,0:T(8,128)(2,1)S(1)} %slice.8), channel_id=1, source_target_pairs={{0,32},{32,64},{64,96},{96,0},{1,33},{33,65},{65,97},{97,1},{2,34}... | collective-permute-start | bytes 983048 | tf_op jit(solution)/shard_map/ppermute | solution.py:214
  51.7 9.0 %collective-permute-start.6 = (bf16[256,1280]{1,0:T(8,128)(2,1)}, bf16[256,1280]{1,0:T(8,128)(2,1)}, u32[]{:S(2)}, u32[]{:S(2)}) collective-permute-start(bf16[256,1280]{1,0:T(8,128)(2,1)} %collective-permute-done.1.rest_2_), channel_id=1, source_target_pairs={{0,8},{8,0},{1,9},{9,1},{2,10},{10,2},{3,11},{11,3},{4,12},{12,4},... | collective-permute-start | bytes 1966088 | tf_op jit(solution)/shard_map/ppermute | solution.py:217
  51.7 10.3 %collective-permute-start.5 = (bf16[256,1280]{1,0:T(8,128)(2,1)}, bf16[256,1280]{1,0:T(8,128)(2,1)}, u32[]{:S(2)}, u32[]{:S(2)}) collective-permute-start(bf16[256,1280]{1,0:T(8,128)(2,1)} %collective-permute-done.rest_1_), channel_id=1, source_target_pairs={{0,8},{8,0},{1,9},{9,1},{2,10},{10,2},{3,11},{11,3},{4,12},{12,4},... | collective-permute-start | bytes 1966088 | tf_op jit(solution)/shard_map/ppermute | solution.py:217
  55.3 5.4 %collective-permute-start.8 = (bf16[128,1280]{1,0:T(8,128)(2,1)}, bf16[128,1280]{1,0:T(8,128)(2,1)}, u32[]{:S(2)}, u32[]{:S(2)}) collective-permute-start(bf16[128,1280]{1,0:T(8,128)(2,1)} %collective-permute-done.3.rest_4_), channel_id=1, source_target_pairs={{0,8},{8,0},{1,9},{9,1},{2,10},{10,2},{3,11},{11,3},{4,12},{12,4},... | collective-permute-start | bytes 983048 | tf_op jit(solution)/shard_map/ppermute | solution.py:217
  60.0 2.0 %collective-permute-start.7 = (bf16[128,1280]{1,0:T(8,128)(2,1)}, bf16[128,1280]{1,0:T(8,128)(2,1)}, u32[]{:S(2)}, u32[]{:S(2)}) collective-permute-start(bf16[128,1280]{1,0:T(8,128)(2,1)} %collective-permute-done.2.rest_3_), channel_id=1, source_target_pairs={{0,8},{8,0},{1,9},{9,1},{2,10},{10,2},{3,11},{11,3},{4,12},{12,4},... | collective-permute-start | bytes 983048 | tf_op jit(solution)/shard_map/ppermute | solution.py:217
  62.0 1.5 %copy-start.1 = (bf16[8,5,256,128]{3,2,1,0:T(8,128)(2,1)}, bf16[8,5,256,128]{3,2,1,0:T(8,128)(2,1)S(1)}, u32[]{:S(2)}) copy-start(bf16[8,5,256,128]{3,2,1,0:T(8,128)(2,1)S(1)} %all-to-all-done.x_ref) | copy-start | bytes 7864324
  81.4 24.2 %all-to-all-start.3 = ((bf16[8,8,5,16,128]{4,3,2,1,0:T(8,128)(2,1)}), bf16[8,8,5,16,128]{4,3,2,1,0:T(8,128)(2,1)}, u32[]{:S(2)}, u32[]{:S(2)}) async-start(bf16[8,8,5,16,128]{4,3,2,1,0:T(8,128)(2,1)} %attend.3), calls=%async_computation.3 | async-start | bytes 2621440 | tf_op jit(solution)/shard_map/all_to_all | solution.py:251
  105.7 23.0 %all-to-all-start.2 = ((bf16[8,8,5,16,128]{4,3,2,1,0:T(8,128)(2,1)}), bf16[8,8,5,16,128]{4,3,2,1,0:T(8,128)(2,1)S(1)}, u32[]{:S(2)}, u32[]{:S(2)}) async-start(bf16[8,8,5,16,128]{4,3,2,1,0:T(8,128)(2,1)} %attend.2), calls=%async_computation.2 | async-start | bytes 2621440 | tf_op jit(solution)/shard_map/all_to_all | solution.py:251
  128.7 1.1 copy-start

commit v5 on v4

--- a/solution.py
+++ b/solution.py
@@ -28,6 +28,7 @@
 OUT = (ULY, TOKENS, 1 + P_SIZE, GROUP, HD)
 WIDTH = HD * (2 + 2 * P_SIZE)
 SCALE = HD**-0.5
+LIMIT = 34
 LOG2E = math.log2(math.e)
 F32 = jnp.float32
 BF16 = jnp.bfloat16
@@ -52,19 +53,24 @@
 
 
 def attend(part, meta, x_ref, *rest):
-    pieces, (out_ref, kv, scores, top, acc, woven, sems) = rest[:10], rest[10:]
+    pieces, (out_hbm, kv, scores, top, acc, woven, out_ref, sems, out_sems) = rest[:10], rest[10:]
     blk = meta[SPANS]
     first = 2 * blk
 
-    for n, (operand, row, stored) in enumerate(pieces_of(blk // 4, blk % 2)):
-        at = pl.multiple_of(meta[stored] * SPAN, SPAN)
-        pltpu.make_async_copy(
-            pieces[operand].at[pl.ds(row, SPAN), :], kv.at[pl.ds(at, SPAN), :], sems.at[n]
-        ).start()
+    def fetch(columns, sem, operand=0, row=0, at=0):
+        rows = pl.ds(at, SPAN)
+        return pltpu.make_async_copy(
+            pieces[operand].at[pl.ds(row, SPAN), columns], kv.at[rows, columns], sem
+        )
+
+    only_keys, others = slice(0, HD), slice(HD, WIDTH)
+    spans = pieces_of(blk // 4, blk % 2)
+    for columns, group in ((only_keys, 0), (others, 1)):
+        for n, (operand, row, stored) in enumerate(spans):
+            at = pl.multiple_of(meta[stored] * SPAN, SPAN)
+            fetch(columns, sems.at[group, n], operand, row, at).start()
     for n in range(SPANS):
-        pltpu.make_async_copy(
-            pieces[0].at[pl.ds(0, SPAN), :], kv.at[pl.ds(0, SPAN), :], sems.at[n]
-        ).wait()
+        fetch(only_keys, sems.at[0, n]).wait()
 
     ones = jnp.ones((KB, HD), BF16)
 
@@ -74,7 +80,8 @@
         source = half * 4
 
         def rows_of(k):
-            return x_ref[pl.ds(source, 4), k].reshape(TILE, HD)
+            rows = slice(part * CHUNK, (part + 1) * CHUNK)
+            return x_ref[pl.ds(source, 4), k, rows].reshape(TILE, HD)
 
         def score(b):
             at = pl.multiple_of(b * KB, KB)
@@ -99,6 +106,11 @@
         keep(last, jnp.where(visible, score(last), -1e30))
         top[...] = jnp.broadcast_to(jnp.max(top[...], axis=1, keepdims=True), (TILE, HD))
         acc[...] = jnp.zeros_like(acc)
+
+        @pl.when(half == 0)
+        def _():
+            for n in range(SPANS):
+                fetch(others, sems.at[1, n]).wait()
 
         def second_pass(b, carry):
             at = pl.multiple_of(b * KB, KB)
@@ -142,65 +154,74 @@
         for n in range(4):
             rows = woven[n * P_SIZE * CHUNK : (n + 1) * P_SIZE * CHUNK, :]
             out_ref[source + n, :, 1:] = rows.astype(BF16).reshape(TOKENS, P_SIZE, GROUP, HD)
+        send(half).start()
         return unused
 
+    def send(half):
+        rows = pl.ds(half * 4, 4)
+        return pltpu.make_async_copy(out_ref.at[rows], out_hbm.at[rows], out_sems.at[half])
+
     lax.fori_loop(0, 2, tile, 0)
+    for half in range(2):
+        send(half).wait()
 
 
 def attention(meta, x, pieces, part):
     flops = 2 * 2 * TILE * 5 * KB * 11 * KB * HD
     return pl.pallas_call(
         functools.partial(attend, part),
-        grid=(1,),
-        out_shape=jax.ShapeDtypeStruct(OUT, BF16),
+        out_shape=pltpu.HBM(OUT, BF16),
         in_specs=[
             pl.BlockSpec(memory_space=pltpu.SMEM),
-            pl.BlockSpec((ULY, 1 + P_SIZE, CHUNK, HD), lambda i: (0, 0, part, 0)),
+            pl.BlockSpec(memory_space=pltpu.VMEM),
         ]
-        + [pl.BlockSpec(memory_space=pl.ANY)] * len(pieces),
-        out_specs=pl.BlockSpec(OUT, lambda i: (0, 0, 0, 0, 0)),
+        + [pl.BlockSpec(memory_space=pltpu.HBM)] * len(pieces),
+        out_specs=pl.BlockSpec(memory_space=pltpu.HBM),
         scratch_shapes=[
             pltpu.VMEM((SPANS * SPAN, WIDTH), BF16),
             pltpu.VMEM((BLOCKS, TILE, KB), F32),
             pltpu.VMEM((TILE, HD), F32),
             pltpu.VMEM((TILE, 10 * HD), F32),
             pltpu.VMEM((P_SIZE * TILE, HD), F32),
-            pltpu.SemaphoreType.DMA((SPANS,)),
+            pltpu.VMEM(OUT, BF16),
+            pltpu.SemaphoreType.DMA((2, SPANS)),
+            pltpu.SemaphoreType.DMA((2,)),
         ],
-        compiler_params=pltpu.CompilerParams(vmem_limit_bytes=60 * 2**20),
+        compiler_params=pltpu.CompilerParams(vmem_limit_bytes=LIMIT * 2**20),
         cost_estimate=pl.CostEstimate(flops=flops, transcendentals=0, bytes_accessed=8 * 2**20),
         name="attend",
     )(meta, x, *pieces)
 
 
-def place(part_ref, *refs):
-    primal_ref, tangent_ref = refs[-2:]
+def place(part, part_ref, *refs):
+    primal_ref, tangent_ref, sems = refs[-3:]
+    rows = pl.ds(part * TOKENS, TOKENS)
+    copies = []
     for g in range(ULY):
-        primal_ref[:, g] = part_ref[g, :, 0]
-        tangent_ref[:, g] = part_ref[g, :, 1:]
+        copies.append((part_ref.at[g, :, 1:], tangent_ref.at[rows, g]))
+        copies.append((part_ref.at[g, :, 0], primal_ref.at[rows, g]))
+    copies = [pltpu.make_async_copy(a, b, sems.at[n]) for n, (a, b) in enumerate(copies)]
+    for copy in copies:
+        copy.start()
+    for copy in copies:
+        copy.wait()
 
 
 def assemble(parts):
-    step = 2
-    steps = TOKENS // step
     placed = ()
     for n, part in enumerate(parts):
         placed = pl.pallas_call(
-            place,
-            grid=(steps,),
+            functools.partial(place, n),
             out_shape=(
                 jax.ShapeDtypeStruct((ROWS, ULY, GROUP, HD), BF16),
                 jax.ShapeDtypeStruct((ROWS, ULY, P_SIZE, GROUP, HD), BF16),
             ),
-            in_specs=[pl.BlockSpec((ULY, step, 1 + P_SIZE, GROUP, HD), lambda i: (0, i, 0, 0, 0))]
-            + [pl.BlockSpec(memory_space=pl.ANY)] * len(placed),
-            out_specs=(
-                pl.BlockSpec((step, ULY, GROUP, HD), lambda i, n=n: (n * steps + i, 0, 0, 0)),
-                pl.BlockSpec(
-                    (step, ULY, P_SIZE, GROUP, HD), lambda i, n=n: (n * steps + i, 0, 0, 0, 0)
-                ),
-            ),
+            in_specs=[pl.BlockSpec(memory_space=pltpu.VMEM)]
+            + [pl.BlockSpec(memory_space=pltpu.HBM)] * len(placed),
+            out_specs=(pl.BlockSpec(memory_space=pltpu.HBM),) * 2,
+            scratch_shapes=[pltpu.SemaphoreType.DMA((2 * ULY,))],
             input_output_aliases={1 + k: k for k in range(len(placed))},
+            compiler_params=pltpu.CompilerParams(vmem_limit_bytes=8 * 2**20),
             name="place",
         )(part, *placed)
     return placed

time: 134 us -> 125 us (0.933)
  Pallas kernels: 42.8 us -> 35.7 us
    pallas_call x4, Pallas kernels: 42.8 us -> 35.7 us  [the longest x2 32 us: attention(): pl.pallas_call(functools.partial(attend, part), out_shape=pltpu.HBM(OUT,...]
    unnamed x14 -> x6, local copies, waits for them, and re-layouts: 4.12 us -> 1.59 us
    all_to_all x2, waiting for transfers between devices: 15.8 us -> 18 us  [per_device(): sent.append(lax.all_to_all(out, heads, 0, 0, tiled=True))]
    reshape x1, local copies, waits for them, and re-layouts: 0.5 us -> 2.1 us  [per_device(): query_tangents.reshape(ROWS, ULY, GROUP, P_SIZE, HD)]
    all_to_all x1, waiting for transfers between devices: 10.6 us -> 9.05 us  [per_device(): head_kv = lax.all_to_all(packed, ('xh',) + heads, 0, 0, tiled=True)]
  transfers between devices with their start and end apart: 13 -> 13, of which waited for: 7 -> 7; matrix products, arithmetic and copies ran while one was open for 4% -> 5% of each run, Pallas kernels for 16% -> 15%
where the time goes in v5:
time: 125 us
  waiting for transfers between devices  49.3 us (39%)
  Pallas kernels  35.7 us (29%)
  starting transfers between devices  28.3 us (23%)
  local copies, waits for them, and re-layouts  7.72 us (6%)
  other arithmetic  2.71 us (2%)
    pallas_call x2, Pallas kernels, attention(): pl.pallas_call(functools.partial(attend, part), out_shape=pltpu.HBM(OUT,...  32 us
    all_to_all x2, waiting for transfers between devices, per_device(): sent.append(lax.all_to_all(out, heads, 0, 0, tiled=True))  18 us
    ppermute x1, waiting for transfers between devices, gather_blocks(): above = lax.ppermute(here, 'z', down)  12.6 us
    all_to_all x1, waiting for transfers between devices, per_device(): head_kv = lax.all_to_all(packed, ('xh',) + heads, 0, 0, tiled=True)  9.05 us
    all_to_all x2, starting transfers between devices, per_device(): sent.append(lax.all_to_all(out, heads, 0, 0, tiled=True))  8.88 us
    all_to_all x1, starting transfers between devices, per_device(): head_kv = lax.all_to_all(packed, ('xh',) + heads, 0, 0, tiled=True)  7.15 us
    ppermute x1, waiting for transfers between devices, gather_blocks(): far_low = lax.ppermute(below[:2 * SPAN], 'z', up)  4.73 us
    ppermute x1, starting transfers between devices, gather_blocks(): above = lax.ppermute(here, 'z', down)  4.11 us
  transfers between devices with their start and end apart: 13, of which 7 were waited for; matrix products, arithmetic and copies ran while one was open for 5% of the time, Pallas kernels for 15%

profile of v5, /device:TPU:0, one launch (start us, length us, event | category | flops | bytes accessed | tf_op | source)
XLA Modules:
  0.0 124.5 jit_solution(6392051397105309282)
XLA Ops:
  0.6 0.0 copy-start
  0.6 0.8 copy.13
  1.5 0.8 copy.15
  2.2 1.0 reshape.35
  3.2 1.0 reshape.36
  4.3 0.9 pad_maximum_fusion.1
  5.2 7.1 %all-to-all-start.1 = ((bf16[16,16,1280]{2,1,0:T(8,128)(2,1)}), bf16[16,16,1280]{2,1,0:T(8,128)(2,1)S(1)}, u32[]{:S(2)}, u32[]{:S(2)}) async-start(bf16[16,16,1280]{2,1,0:T(8,128)(2,1)} %pad_maximum_fusion.1), calls=%async_computation.1 | async-start | bytes 1310720 | tf_op jit(solution)/shard_map/all_to_all | solution.py:254
  12.3 0.0 copy-done
  12.4 2.1 %copy.12 = bf16[16,8,16,4,128]{4,2,0,3,1:T(8,128)(2,1)S(1)} copy(bf16[16,8,16,4,128]{4,3,2,1,0:T(4,128)(2,1)} %bitcast.21) | data formatting | bytes 4194304 | tf_op jit(solution)/shard_map/reshape | solution.py:258
  14.5 1.7 %pad_maximum_fusion = bf16[8,5,256,128]{3,2,1,0:T(8,128)(2,1)} fusion(bf16[8,4,256,128]{3,2,1,0:T(8,128)(2,1)S(1)} %bitcast.19, bf16[8,1,256,128]{3,2,1,0:T(8,128)(2,1)S(1)} %bitcast.20), kind=kLoop, calls=%fused_computation | loop fusion | flops 1310720 | bytes 5242880 | tf_op jit(solution)/shard_map/concatenate | solution.py:261
  16.2 0.0 copy-start.1
  16.2 9.1 %all-to-all-done.1 = bf16[16,16,1280]{2,1,0:T(8,128)(2,1)S(1)} async-done(((bf16[16,16,1280]{2,1,0:T(8,128)(2,1)}), bf16[16,16,1280]{2,1,0:T(8,128)(2,1)S(1)}, u32[]{:S(2)}, u32[]{:S(2)}) %all-to-all-start.1) | async-done | bytes 655392 | tf_op jit(solution)/shard_map/all_to_all | solution.py:254
  25.3 3.6 %all-to-all-start = ((bf16[8,5,256,128]{3,2,1,0:T(8,128)(2,1)}), bf16[8,5,256,128]{3,2,1,0:T(8,128)(2,1)S(1)}, u32[]{:S(2)}, u32[]{:S(2)}) async-start(bf16[8,5,256,128]{3,2,1,0:T(8,128)(2,1)} %pad_maximum_fusion), calls=%async_computation | async-start | bytes 5242880 | tf_op jit(solution)/shard_map/all_to_all | solution.py:268
  28.9 4.1 %collective-permute-start.1 = (bf16[256,1280]{1,0:T(8,128)(2,1)S(1)}, bf16[256,1280]{1,0:T(8,128)(2,1)}, u32[]{:S(2)}, u32[]{:S(2)}) collective-permute-start(bf16[256,1280]{1,0:T(8,128)(2,1)S(1)} %bitcast.14), channel_id=1, source_target_pairs={{0,96},{32,0},{64,32},{96,64},{1,97},{33,1},{65,33},{97,65},{2,98}... | collective-permute-start | bytes 1966088 | tf_op jit(solution)/shard_map/ppermute | solution.py:234
  33.0 0.0 collective-permute-start
  33.0 0.0 collective-permute-start.4
  33.0 12.6 %collective-permute-done.1.rest_2_ = bf16[256,1280]{1,0:T(8,128)(2,1)} collective-permute-done((bf16[256,1280]{1,0:T(8,128)(2,1)S(1)}, bf16[256,1280]{1,0:T(8,128)(2,1)}, u32[]{:S(2)}, u32[]{:S(2)}) %collective-permute-start.1) | collective-permute-done | bytes 655392 | tf_op jit(solution)/shard_map/ppermute | solution.py:234
  45.6 1.0 slice.9
  46.6 3.9 %collective-permute-start.3 = (bf16[128,1280]{1,0:T(8,128)(2,1)S(1)}, bf16[128,1280]{1,0:T(8,128)(2,1)}, u32[]{:S(2)}, u32[]{:S(2)}) collective-permute-start(bf16[128,1280]{1,0:T(8,128)(2,1)S(1)} %slice.9), channel_id=1, source_target_pairs={{0,96},{32,0},{64,32},{96,64},{1,97},{33,1},{65,33},{97,65},{2,98}... | collective-permute-start | bytes 983048 | tf_op jit(solution)/shard_map/ppermute | solution.py:236
  50.5 0.0 collective-permute-done.rest_1_
  50.5 1.0 slice.8
  51.5 0.1 collective-permute-start.2
  51.6 0.1 collective-permute-start.6
  51.7 0.5 collective-permute-start.5
  52.2 3.0 %collective-permute-done.3.rest_4_ = bf16[128,1280]{1,0:T(8,128)(2,1)} collective-permute-done((bf16[128,1280]{1,0:T(8,128)(2,1)S(1)}, bf16[128,1280]{1,0:T(8,128)(2,1)}, u32[]{:S(2)}, u32[]{:S(2)}) %collective-permute-start.3) | collective-permute-done | bytes 327712 | tf_op jit(solution)/shard_map/ppermute | solution.py:236
  55.2 0.0 collective-permute-start.8
  55.2 4.7 %collective-permute-done.2.rest_3_ = bf16[128,1280]{1,0:T(8,128)(2,1)} collective-permute-done((bf16[128,1280]{1,0:T(8,128)(2,1)S(1)}, bf16[128,1280]{1,0:T(8,128)(2,1)}, u32[]{:S(2)}, u32[]{:S(2)}) %collective-permute-start.2) | collective-permute-done | bytes 327712 | tf_op jit(solution)/shard_map/ppermute | solution.py:235
  59.9 0.0 collective-permute-start.7
  59.9 0.0 copy-done.1
  59.9 0.1 pad_add_fusion.meta
  60.0 0.0 collective-permute-done.4.rest_5_
  60.0 0.0 collective-permute-done.8.rest_9_
  60.0 0.0 collective-permute-done.6.rest_7_
  60.0 1.9 %collective-permute-done.7.rest_8_ = bf16[128,1280]{1,0:T(8,128)(2,1)} collective-permute-done((bf16[128,1280]{1,0:T(8,128)(2,1)}, bf16[128,1280]{1,0:T(8,128)(2,1)}, u32[]{:S(2)}, u32[]{:S(2)}) %collective-permute-start.7) | collective-permute-done | bytes 327712 | tf_op jit(solution)/shard_map/ppermute | solution.py:238
  61.9 0.0 collective-permute-done.5.rest_6_
  61.9 0.0 all-to-all-done.x_ref
  61.9 16.0 %attend.3 = bf16[8,8,5,16,128]{4,3,2,1,0:T(8,128)(2,1)} custom-call(s32[33]{0:T(128)S(1)} %pad_add_fusion.meta, bf16[8,5,256,128]{3,2,1,0:T(8,128)(2,1)S(1)} %all-to-all-done.x_ref, bf16[256,1280]{1,0:T(8,128)(2,1)S(1)} %bitcast.17, bf16[256,1280]{1,0:T(8,128)(2,1)} %collective-permute-done.rest_1_, bf16[256,1280]{1,0:T(8,128)(2,1)} %collective-permute-done.1.rest_2_, ...), custom_call_target="tpu_custom_call" | custom-call | flops 944892805120 | bytes 8388608 | tf_op jit(solution)/shard_map/attend/pallas_call | solution.py:171
  77.9 5.3 %all-to-all-start.3 = ((bf16[8,8,5,16,128]{4,3,2,1,0:T(8,128)(2,1)}), bf16[8,8,5,16,128]{4,3,2,1,0:T(8,128)(2,1)}, u32[]{:S(2)}, u32[]{:S(2)}) async-start(bf16[8,8,5,16,128]{4,3,2,1,0:T(8,128)(2,1)} %attend.3), calls=%async_computation.3 | async-start | bytes 2621440 | tf_op jit(solution)/shard_map/all_to_all | solution.py:272
  83.2 16.0 %attend.2 = bf16[8,8,5,16,128]{4,3,2,1,0:T(8,128)(2,1)} custom-call(s32[33]{0:T(128)S(1)} %pad_add_fusion.meta, bf16[8,5,256,128]{3,2,1,0:T(8,128)(2,1)S(1)} %all-to-all-done.x_ref, bf16[256,1280]{1,0:T(8,128)(2,1)S(1)} %bitcast.18, bf16[256,1280]{1,0:T(8,128)(2,1)} %collective-permute-done.rest_1_, bf16[256,1280]{1,0:T(8,128)(2,1)} %collective-permute-done.1.rest_2_, ...), custom_call_target="tpu_custom_call" | custom-call | flops 944892805120 | bytes 8388608 | tf_op jit(solution)/shard_map/attend/pallas_call | solution.py:171
  99.2 2.7 %all-to-all-done.3.part_ref = bf16[8,8,5,16,128]{4,3,2,1,0:T(8,128)(2,1)} async-done(((bf16[8,8,5,16,128]{4,3,2,1,0:T(8,128)(2,1)}), bf16[8,8,5,16,128]{4,3,2,1,0:T(8,128)(2,1)}, u32[]{:S(2)}, u32[]{:S(2)}) %all-to-all-start.3) | async-done | bytes 1310752 | tf_op jit(solution)/shard_map/all_to_all | solution.py:272
  101.9 3.6 %all-to-all-start.2 = ((bf16[8,8,5,16,128]{4,3,2,1,0:T(8,128)(2,1)}), bf16[8,8,5,16,128]{4,3,2,1,0:T(8,128)(2,1)S(1)}, u32[]{:S(2)}, u32[]{:S(2)}) async-start(bf16[8,8,5,16,128]{4,3,2,1,0:T(8,128)(2,1)} %attend.2), calls=%async_computation.2 | async-start | bytes 2621440 | tf_op jit(solution)/shard_map/all_to_all | solution.py:272
  105.5 2.5 %place.2 = (bf16[16,8,16,128]{3,2,1,0:T(8,128)(2,1)}, bf16[16,8,4,16,128]{4,3,2,1,0:T(8,128)(2,1)}) custom-call(bf16[8,8,5,16,128]{4,3,2,1,0:T(8,128)(2,1)} %all-to-all-done.3.part_ref), custom_call_target="tpu_custom_call" | custom-call | tf_op jit(solution)/shard_map/place/pallas_call | solution.py:213
  108.0 15.3 %all-to-all-done.2.part_ref = bf16[8,8,5,16,128]{4,3,2,1,0:T(8,128)(2,1)S(1)} async-done(((bf16[8,8,5,16,128]{4,3,2,1,0:T(8,128)(2,1)}), bf16[8,8,5,16,128]{4,3,2,1,0:T(8,128)(2,1)S(1)}, u32[]{:S(2)}, u32[]{:S(2)}) %all-to-all-start.2) | async-done | bytes 1310752 | tf_op jit(solution)/shard_map/all_to_all | solution.py:272
  123.3 1.2 place.3
  (4 shorter events, 0.2 us)
Async XLA Ops:
  0.6 11.7 %copy-start = (bf16[16,128,128]{2,1,0:T(8,128)(2,1)S(1)}, bf16[16,128,128]{2,1,0:T(8,128)(2,1)}, u32[]{:S(2)}) copy-start(bf16[16,128,128]{2,1,0:T(8,128)(2,1)} %param.7) | copy-start | bytes 1572868
  5.2 20.1 %all-to-all-start.1 = ((bf16[16,16,1280]{2,1,0:T(8,128)(2,1)}), bf16[16,16,1280]{2,1,0:T(8,128)(2,1)S(1)}, u32[]{:S(2)}, u32[]{:S(2)}) async-start(bf16[16,16,1280]{2,1,0:T(8,128)(2,1)} %pad_maximum_fusion.1), calls=%async_computation.1 | async-start | bytes 1310720 | tf_op jit(solution)/shard_map/all_to_all | solution.py:254
  16.2 43.7 %copy-start.1 = (s32[32]{0:T(128)S(1)}, s32[32]{0:T(128)}, u32[]{:S(2)}) copy-start(s32[32]{0:T(128)} %param.13) | copy-start | bytes 388
  25.3 36.6 %all-to-all-start = ((bf16[8,5,256,128]{3,2,1,0:T(8,128)(2,1)}), bf16[8,5,256,128]{3,2,1,0:T(8,128)(2,1)S(1)}, u32[]{:S(2)}, u32[]{:S(2)}) async-start(bf16[8,5,256,128]{3,2,1,0:T(8,128)(2,1)} %pad_maximum_fusion), calls=%async_computation | async-start | bytes 5242880 | tf_op jit(solution)/shard_map/all_to_all | solution.py:268
  28.9 16.7 %collective-permute-start.1 = (bf16[256,1280]{1,0:T(8,128)(2,1)S(1)}, bf16[256,1280]{1,0:T(8,128)(2,1)}, u32[]{:S(2)}, u32[]{:S(2)}) collective-permute-start(bf16[256,1280]{1,0:T(8,128)(2,1)S(1)} %bitcast.14), channel_id=1, source_target_pairs={{0,96},{32,0},{64,32},{96,64},{1,97},{33,1},{65,33},{97,65},{2,98}... | collective-permute-start | bytes 1966088 | tf_op jit(solution)/shard_map/ppermute | solution.py:234
  33.0 17.5 %collective-permute-start = (bf16[256,1280]{1,0:T(8,128)(2,1)S(1)}, bf16[256,1280]{1,0:T(8,128)(2,1)}, u32[]{:S(2)}, u32[]{:S(2)}) collective-permute-start(bf16[256,1280]{1,0:T(8,128)(2,1)S(1)} %bitcast.15), channel_id=1, source_target_pairs={{0,32},{32,64},{64,96},{96,0},{1,33},{33,65},{65,97},{97,1},{2,34}... | collective-permute-start | bytes 1966088 | tf_op jit(solution)/shard_map/ppermute | solution.py:233
  33.0 27.0 %collective-permute-start.4 = (bf16[256,1280]{1,0:T(8,128)(2,1)S(1)}, bf16[256,1280]{1,0:T(8,128)(2,1)}, u32[]{:S(2)}, u32[]{:S(2)}) collective-permute-start(bf16[256,1280]{1,0:T(8,128)(2,1)S(1)} %bitcast.16), channel_id=1, source_target_pairs={{0,8},{8,0},{1,9},{9,1},{2,10},{10,2},{3,11},{11,3},{4,12},{12,4},... | collective-permute-start | bytes 1966088 | tf_op jit(solution)/shard_map/ppermute | solution.py:238
  46.6 8.6 %collective-permute-start.3 = (bf16[128,1280]{1,0:T(8,128)(2,1)S(1)}, bf16[128,1280]{1,0:T(8,128)(2,1)}, u32[]{:S(2)}, u32[]{:S(2)}) collective-permute-start(bf16[128,1280]{1,0:T(8,128)(2,1)S(1)} %slice.9), channel_id=1, source_target_pairs={{0,96},{32,0},{64,32},{96,64},{1,97},{33,1},{65,33},{97,65},{2,98}... | collective-permute-start | bytes 983048 | tf_op jit(solution)/shard_map/ppermute | solution.py:236
  51.5 8.5 %collective-permute-start.2 = (bf16[128,1280]{1,0:T(8,128)(2,1)S(1)}, bf16[128,1280]{1,0:T(8,128)(2,1)}, u32[]{:S(2)}, u32[]{:S(2)}) collective-permute-start(bf16[128,1280]{1,0:T(8,128)(2,1)S(1)} %slice.8), channel_id=1, source_target_pairs={{0,32},{32,64},{64,96},{96,0},{1,33},{33,65},{65,97},{97,1},{2,34}... | collective-permute-start | bytes 983048 | tf_op jit(solution)/shard_map/ppermute | solution.py:235
  51.6 8.5 %collective-permute-start.6 = (bf16[256,1280]{1,0:T(8,128)(2,1)}, bf16[256,1280]{1,0:T(8,128)(2,1)}, u32[]{:S(2)}, u32[]{:S(2)}) collective-permute-start(bf16[256,1280]{1,0:T(8,128)(2,1)} %collective-permute-done.1.rest_2_), channel_id=1, source_target_pairs={{0,8},{8,0},{1,9},{9,1},{2,10},{10,2},{3,11},{11,3},{4,12},{12,4},... | collective-permute-start | bytes 1966088 | tf_op jit(solution)/shard_map/ppermute | solution.py:238
  51.7 10.3 %collective-permute-start.5 = (bf16[256,1280]{1,0:T(8,128)(2,1)}, bf16[256,1280]{1,0:T(8,128)(2,1)}, u32[]{:S(2)}, u32[]{:S(2)}) collective-permute-start(bf16[256,1280]{1,0:T(8,128)(2,1)} %collective-permute-done.rest_1_), channel_id=1, source_target_pairs={{0,8},{8,0},{1,9},{9,1},{2,10},{10,2},{3,11},{11,3},{4,12},{12,4},... | collective-permute-start | bytes 1966088 | tf_op jit(solution)/shard_map/ppermute | solution.py:238
  55.2 4.8 %collective-permute-start.8 = (bf16[128,1280]{1,0:T(8,128)(2,1)}, bf16[128,1280]{1,0:T(8,128)(2,1)}, u32[]{:S(2)}, u32[]{:S(2)}) collective-permute-start(bf16[128,1280]{1,0:T(8,128)(2,1)} %collective-permute-done.3.rest_4_), channel_id=1, source_target_pairs={{0,8},{8,0},{1,9},{9,1},{2,10},{10,2},{3,11},{11,3},{4,12},{12,4},... | collective-permute-start | bytes 983048 | tf_op jit(solution)/shard_map/ppermute | solution.py:238
  59.9 2.0 %collective-permute-start.7 = (bf16[128,1280]{1,0:T(8,128)(2,1)}, bf16[128,1280]{1,0:T(8,128)(2,1)}, u32[]{:S(2)}, u32[]{:S(2)}) collective-permute-start(bf16[128,1280]{1,0:T(8,128)(2,1)} %collective-permute-done.2.rest_3_), channel_id=1, source_target_pairs={{0,8},{8,0},{1,9},{9,1},{2,10},{10,2},{3,11},{11,3},{4,12},{12,4},... | collective-permute-start | bytes 983048 | tf_op jit(solution)/shard_map/ppermute | solution.py:238
  77.9 24.0 %all-to-all-start.3 = ((bf16[8,8,5,16,128]{4,3,2,1,0:T(8,128)(2,1)}), bf16[8,8,5,16,128]{4,3,2,1,0:T(8,128)(2,1)}, u32[]{:S(2)}, u32[]{:S(2)}) async-start(bf16[8,8,5,16,128]{4,3,2,1,0:T(8,128)(2,1)} %attend.3), calls=%async_computation.3 | async-start | bytes 2621440 | tf_op jit(solution)/shard_map/all_to_all | solution.py:272
  101.9 21.4 %all-to-all-start.2 = ((bf16[8,8,5,16,128]{4,3,2,1,0:T(8,128)(2,1)}), bf16[8,8,5,16,128]{4,3,2,1,0:T(8,128)(2,1)S(1)}, u32[]{:S(2)}, u32[]{:S(2)}) async-start(bf16[8,8,5,16,128]{4,3,2,1,0:T(8,128)(2,1)} %attend.2), calls=%async_computation.2 | async-start | bytes 2621440 | tf_op jit(solution)/shard_map/all_to_all | solution.py:272

commit v6 on v5

--- a/solution.py
+++ b/solution.py
@@ -249,8 +249,8 @@
         axis=2,
     )
     heads = ("y", "xl")
-    packed = packed.transpose(1, 0, 2)
-    packed = jnp.concatenate([packed, packed], axis=0)
+    packed = jnp.broadcast_to(packed[:, None], (ROWS, 2, KVH, WIDTH))
+    packed = packed.reshape(ROWS, 2 * KVH, WIDTH).transpose(1, 0, 2)
     head_kv = lax.all_to_all(packed, ("xh",) + heads, 0, 0, tiled=True)
     pieces = gather_blocks(head_kv.reshape(2 * ULY * ROWS, WIDTH))
 

time: 125 us -> 125 us (level)
  waiting for transfers between devices: 49.3 us -> 46.8 us
  Pallas kernels: 35.7 us -> 37.1 us
    all_to_all x2, waiting for transfers between devices: 18 us -> 15.5 us  [per_device(): sent.append(lax.all_to_all(out, heads, 0, 0, tiled=True))]
    unnamed x6 -> x4, local copies, waits for them, and re-layouts: 1.59 us -> 0.01 us
    pallas_call x2, Pallas kernels: 32 us -> 33.4 us  [attention(): pl.pallas_call(functools.partial(attend, part), out_shape=pltpu.HBM(OUT,...]
  transfers between devices with their start and end apart: 13 -> 13, of which waited for: 7 -> 7; matrix products, arithmetic and copies ran while one was open for 5% -> 5% of each run, Pallas kernels for 15% -> 16%
where the time goes in v6:
time: 125 us; the launch traced here: 124 us
  waiting for transfers between devices  46.8 us (37%)
  Pallas kernels  37.1 us (30%)
  starting transfers between devices  29.2 us (23%)
  local copies, waits for them, and re-layouts  7.05 us (6%)
  other arithmetic  2.6 us (2%)
    pallas_call x2, Pallas kernels, attention(): pl.pallas_call(functools.partial(attend, part), out_shape=pltpu.HBM(OUT,...  33.4 us
    all_to_all x2, waiting for transfers between devices, per_device(): sent.append(lax.all_to_all(out, heads, 0, 0, tiled=True))  15.5 us
    ppermute x1, waiting for transfers between devices, gather_blocks(): above = lax.ppermute(here, 'z', down)  12.6 us
    all_to_all x2, starting transfers between devices, per_device(): sent.append(lax.all_to_all(out, heads, 0, 0, tiled=True))  9.81 us
    all_to_all x1, waiting for transfers between devices, per_device(): head_kv = lax.all_to_all(packed, ('xh',) + heads, 0, 0, tiled=True)  9.05 us
    all_to_all x1, starting transfers between devices, per_device(): head_kv = lax.all_to_all(packed, ('xh',) + heads, 0, 0, tiled=True)  7.15 us
    ppermute x1, waiting for transfers between devices, gather_blocks(): far_low = lax.ppermute(below[:2 * SPAN], 'z', up)  4.73 us
    ppermute x1, starting transfers between devices, gather_blocks(): above = lax.ppermute(here, 'z', down)  4.11 us
  transfers between devices with their start and end apart: 13, of which 7 were waited for; matrix products, arithmetic and copies ran while one was open for 5% of the time, Pallas kernels for 16%

profile of v6, /device:TPU:0, one launch (start us, length us, event | category | flops | bytes accessed | tf_op | source)
XLA Modules:
  0.0 123.5 jit_solution(15262915906162371961)
XLA Ops:
  0.6 0.0 copy-start
  0.6 1.0 reshape.39
  1.7 1.0 reshape.40
  2.6 0.8 pad_maximum_fusion.1
  3.4 0.1 copy.13
  3.5 0.9 broadcast_in_dim.10
  4.4 7.1 %all-to-all-start.1 = ((bf16[16,16,1280]{2,1,0:T(8,128)(2,1)}), bf16[16,16,1280]{2,1,0:T(8,128)(2,1)S(1)}, u32[]{:S(2)}, u32[]{:S(2)}) async-start(bf16[16,16,1280]{2,1,0:T(8,128)(2,1)} %bitcast.8), calls=%async_computation.1 | async-start | bytes 1310720 | tf_op jit(solution)/shard_map/all_to_all | solution.py:254
  11.5 0.0 copy-done
  11.6 2.1 %copy.12 = bf16[16,8,16,4,128]{4,2,0,3,1:T(8,128)(2,1)S(1)} copy(bf16[16,8,16,4,128]{4,3,2,1,0:T(4,128)(2,1)} %bitcast.22) | data formatting | bytes 4194304 | tf_op jit(solution)/shard_map/reshape | solution.py:258
  13.7 1.7 %pad_maximum_fusion = bf16[8,5,256,128]{3,2,1,0:T(8,128)(2,1)} fusion(bf16[8,4,256,128]{3,2,1,0:T(8,128)(2,1)S(1)} %bitcast.20, bf16[8,1,256,128]{3,2,1,0:T(8,128)(2,1)S(1)} %bitcast.21), kind=kLoop, calls=%fused_computation | loop fusion | flops 1310720 | bytes 5242880 | tf_op jit(solution)/shard_map/concatenate | solution.py:261
  15.4 0.0 copy-start.1
  15.4 9.1 %all-to-all-done.1 = bf16[16,16,1280]{2,1,0:T(8,128)(2,1)S(1)} async-done(((bf16[16,16,1280]{2,1,0:T(8,128)(2,1)}), bf16[16,16,1280]{2,1,0:T(8,128)(2,1)S(1)}, u32[]{:S(2)}, u32[]{:S(2)}) %all-to-all-start.1) | async-done | bytes 655392 | tf_op jit(solution)/shard_map/all_to_all | solution.py:254
  24.5 3.6 %all-to-all-start = ((bf16[8,5,256,128]{3,2,1,0:T(8,128)(2,1)}), bf16[8,5,256,128]{3,2,1,0:T(8,128)(2,1)S(1)}, u32[]{:S(2)}, u32[]{:S(2)}) async-start(bf16[8,5,256,128]{3,2,1,0:T(8,128)(2,1)} %pad_maximum_fusion), calls=%async_computation | async-start | bytes 5242880 | tf_op jit(solution)/shard_map/all_to_all | solution.py:268
  28.1 4.1 %collective-permute-start.1 = (bf16[256,1280]{1,0:T(8,128)(2,1)S(1)}, bf16[256,1280]{1,0:T(8,128)(2,1)}, u32[]{:S(2)}, u32[]{:S(2)}) collective-permute-start(bf16[256,1280]{1,0:T(8,128)(2,1)S(1)} %bitcast.15), channel_id=1, source_target_pairs={{0,96},{32,0},{64,32},{96,64},{1,97},{33,1},{65,33},{97,65},{2,98}... | collective-permute-start | bytes 1966088 | tf_op jit(solution)/shard_map/ppermute | solution.py:234
  32.2 0.0 collective-permute-start
  32.2 0.0 collective-permute-start.4
  32.2 12.6 %collective-permute-done.1.rest_2_ = bf16[256,1280]{1,0:T(8,128)(2,1)} collective-permute-done((bf16[256,1280]{1,0:T(8,128)(2,1)S(1)}, bf16[256,1280]{1,0:T(8,128)(2,1)}, u32[]{:S(2)}, u32[]{:S(2)}) %collective-permute-start.1) | collective-permute-done | bytes 655392 | tf_op jit(solution)/shard_map/ppermute | solution.py:234
  44.8 1.0 slice.9
  45.8 3.9 %collective-permute-start.3 = (bf16[128,1280]{1,0:T(8,128)(2,1)S(1)}, bf16[128,1280]{1,0:T(8,128)(2,1)}, u32[]{:S(2)}, u32[]{:S(2)}) collective-permute-start(bf16[128,1280]{1,0:T(8,128)(2,1)S(1)} %slice.9), channel_id=1, source_target_pairs={{0,96},{32,0},{64,32},{96,64},{1,97},{33,1},{65,33},{97,65},{2,98}... | collective-permute-start | bytes 983048 | tf_op jit(solution)/shard_map/ppermute | solution.py:236
  49.7 0.0 collective-permute-done.rest_1_
  49.7 1.0 slice.8
  50.7 0.1 collective-permute-start.2
  50.8 0.1 collective-permute-start.6
  50.9 0.5 collective-permute-start.5
  51.4 3.0 %collective-permute-done.3.rest_4_ = bf16[128,1280]{1,0:T(8,128)(2,1)} collective-permute-done((bf16[128,1280]{1,0:T(8,128)(2,1)S(1)}, bf16[128,1280]{1,0:T(8,128)(2,1)}, u32[]{:S(2)}, u32[]{:S(2)}) %collective-permute-start.3) | collective-permute-done | bytes 327712 | tf_op jit(solution)/shard_map/ppermute | solution.py:236
  54.4 0.0 collective-permute-start.8
  54.4 4.7 %collective-permute-done.2.rest_3_ = bf16[128,1280]{1,0:T(8,128)(2,1)} collective-permute-done((bf16[128,1280]{1,0:T(8,128)(2,1)S(1)}, bf16[128,1280]{1,0:T(8,128)(2,1)}, u32[]{:S(2)}, u32[]{:S(2)}) %collective-permute-start.2) | collective-permute-done | bytes 327712 | tf_op jit(solution)/shard_map/ppermute | solution.py:235
  59.1 0.0 collective-permute-start.7
  59.1 0.0 copy-done.1
  59.1 0.1 pad_add_fusion.meta
  59.2 0.0 collective-permute-done.4.rest_5_
  59.2 0.0 collective-permute-done.8.rest_9_
  59.2 0.0 collective-permute-done.6.rest_7_
  59.2 1.9 %collective-permute-done.7.rest_8_ = bf16[128,1280]{1,0:T(8,128)(2,1)} collective-permute-done((bf16[128,1280]{1,0:T(8,128)(2,1)}, bf16[128,1280]{1,0:T(8,128)(2,1)}, u32[]{:S(2)}, u32[]{:S(2)}) %collective-permute-start.7) | collective-permute-done | bytes 327712 | tf_op jit(solution)/shard_map/ppermute | solution.py:238
  61.1 0.0 collective-permute-done.5.rest_6_
  61.1 0.0 all-to-all-done.x_ref
  61.1 16.7 %attend.3 = bf16[8,8,5,16,128]{4,3,2,1,0:T(8,128)(2,1)} custom-call(s32[33]{0:T(128)S(1)} %pad_add_fusion.meta, bf16[8,5,256,128]{3,2,1,0:T(8,128)(2,1)S(1)} %all-to-all-done.x_ref, bf16[256,1280]{1,0:T(8,128)(2,1)S(1)} %bitcast.18, bf16[256,1280]{1,0:T(8,128)(2,1)} %collective-permute-done.rest_1_, bf16[256,1280]{1,0:T(8,128)(2,1)} %collective-permute-done.1.rest_2_, ...), custom_call_target="tpu_custom_call" | custom-call | flops 944892805120 | bytes 8388608 | tf_op jit(solution)/shard_map/attend/pallas_call | solution.py:171
  77.9 5.3 %all-to-all-start.3 = ((bf16[8,8,5,16,128]{4,3,2,1,0:T(8,128)(2,1)}), bf16[8,8,5,16,128]{4,3,2,1,0:T(8,128)(2,1)}, u32[]{:S(2)}, u32[]{:S(2)}) async-start(bf16[8,8,5,16,128]{4,3,2,1,0:T(8,128)(2,1)} %attend.3), calls=%async_computation.3 | async-start | bytes 2621440 | tf_op jit(solution)/shard_map/all_to_all | solution.py:272
  83.1 16.7 %attend.2 = bf16[8,8,5,16,128]{4,3,2,1,0:T(8,128)(2,1)} custom-call(s32[33]{0:T(128)S(1)} %pad_add_fusion.meta, bf16[8,5,256,128]{3,2,1,0:T(8,128)(2,1)S(1)} %all-to-all-done.x_ref, bf16[256,1280]{1,0:T(8,128)(2,1)S(1)} %bitcast.19, bf16[256,1280]{1,0:T(8,128)(2,1)} %collective-permute-done.rest_1_, bf16[256,1280]{1,0:T(8,128)(2,1)} %collective-permute-done.1.rest_2_, ...), custom_call_target="tpu_custom_call" | custom-call | flops 944892805120 | bytes 8388608 | tf_op jit(solution)/shard_map/attend/pallas_call | solution.py:171
  99.9 1.2 all-to-all-done.3.part_ref
  101.1 4.5 %all-to-all-start.2 = ((bf16[8,8,5,16,128]{4,3,2,1,0:T(8,128)(2,1)}), bf16[8,8,5,16,128]{4,3,2,1,0:T(8,128)(2,1)S(1)}, u32[]{:S(2)}, u32[]{:S(2)}) async-start(bf16[8,8,5,16,128]{4,3,2,1,0:T(8,128)(2,1)} %attend.2), calls=%async_computation.2 | async-start | bytes 2621440 | tf_op jit(solution)/shard_map/all_to_all | solution.py:272
  105.6 2.5 %place.2 = (bf16[16,8,16,128]{3,2,1,0:T(8,128)(2,1)}, bf16[16,8,4,16,128]{4,3,2,1,0:T(8,128)(2,1)}) custom-call(bf16[8,8,5,16,128]{4,3,2,1,0:T(8,128)(2,1)} %all-to-all-done.3.part_ref), custom_call_target="tpu_custom_call" | custom-call | tf_op jit(solution)/shard_map/place/pallas_call | solution.py:213
  108.1 14.2 %all-to-all-done.2.part_ref = bf16[8,8,5,16,128]{4,3,2,1,0:T(8,128)(2,1)S(1)} async-done(((bf16[8,8,5,16,128]{4,3,2,1,0:T(8,128)(2,1)}), bf16[8,8,5,16,128]{4,3,2,1,0:T(8,128)(2,1)S(1)}, u32[]{:S(2)}, u32[]{:S(2)}) %all-to-all-start.2) | async-done | bytes 1310752 | tf_op jit(solution)/shard_map/all_to_all | solution.py:272
  122.3 1.2 place.3
  (1 shorter events, 0.0 us)
Async XLA Ops:
  0.6 10.9 %copy-start = (bf16[16,128,128]{2,1,0:T(8,128)(2,1)S(1)}, bf16[16,128,128]{2,1,0:T(8,128)(2,1)}, u32[]{:S(2)}) copy-start(bf16[16,128,128]{2,1,0:T(8,128)(2,1)} %param.7) | copy-start | bytes 1572868
  4.4 20.1 %all-to-all-start.1 = ((bf16[16,16,1280]{2,1,0:T(8,128)(2,1)}), bf16[16,16,1280]{2,1,0:T(8,128)(2,1)S(1)}, u32[]{:S(2)}, u32[]{:S(2)}) async-start(bf16[16,16,1280]{2,1,0:T(8,128)(2,1)} %bitcast.8), calls=%async_computation.1 | async-start | bytes 1310720 | tf_op jit(solution)/shard_map/all_to_all | solution.py:254
  15.4 43.7 %copy-start.1 = (s32[32]{0:T(128)S(1)}, s32[32]{0:T(128)}, u32[]{:S(2)}) copy-start(s32[32]{0:T(128)} %param.13) | copy-start | bytes 388
  24.5 36.6 %all-to-all-start = ((bf16[8,5,256,128]{3,2,1,0:T(8,128)(2,1)}), bf16[8,5,256,128]{3,2,1,0:T(8,128)(2,1)S(1)}, u32[]{:S(2)}, u32[]{:S(2)}) async-start(bf16[8,5,256,128]{3,2,1,0:T(8,128)(2,1)} %pad_maximum_fusion), calls=%async_computation | async-start | bytes 5242880 | tf_op jit(solution)/shard_map/all_to_all | solution.py:268
  28.1 16.7 %collective-permute-start.1 = (bf16[256,1280]{1,0:T(8,128)(2,1)S(1)}, bf16[256,1280]{1,0:T(8,128)(2,1)}, u32[]{:S(2)}, u32[]{:S(2)}) collective-permute-start(bf16[256,1280]{1,0:T(8,128)(2,1)S(1)} %bitcast.15), channel_id=1, source_target_pairs={{0,96},{32,0},{64,32},{96,64},{1,97},{33,1},{65,33},{97,65},{2,98}... | collective-permute-start | bytes 1966088 | tf_op jit(solution)/shard_map/ppermute | solution.py:234
  32.2 17.5 %collective-permute-start = (bf16[256,1280]{1,0:T(8,128)(2,1)S(1)}, bf16[256,1280]{1,0:T(8,128)(2,1)}, u32[]{:S(2)}, u32[]{:S(2)}) collective-permute-start(bf16[256,1280]{1,0:T(8,128)(2,1)S(1)} %bitcast.16), channel_id=1, source_target_pairs={{0,32},{32,64},{64,96},{96,0},{1,33},{33,65},{65,97},{97,1},{2,34}... | collective-permute-start | bytes 1966088 | tf_op jit(solution)/shard_map/ppermute | solution.py:233
  32.2 27.0 %collective-permute-start.4 = (bf16[256,1280]{1,0:T(8,128)(2,1)S(1)}, bf16[256,1280]{1,0:T(8,128)(2,1)}, u32[]{:S(2)}, u32[]{:S(2)}) collective-permute-start(bf16[256,1280]{1,0:T(8,128)(2,1)S(1)} %bitcast.17), channel_id=1, source_target_pairs={{0,8},{8,0},{1,9},{9,1},{2,10},{10,2},{3,11},{11,3},{4,12},{12,4},... | collective-permute-start | bytes 1966088 | tf_op jit(solution)/shard_map/ppermute | solution.py:238
  45.8 8.6 %collective-permute-start.3 = (bf16[128,1280]{1,0:T(8,128)(2,1)S(1)}, bf16[128,1280]{1,0:T(8,128)(2,1)}, u32[]{:S(2)}, u32[]{:S(2)}) collective-permute-start(bf16[128,1280]{1,0:T(8,128)(2,1)S(1)} %slice.9), channel_id=1, source_target_pairs={{0,96},{32,0},{64,32},{96,64},{1,97},{33,1},{65,33},{97,65},{2,98}... | collective-permute-start | bytes 983048 | tf_op jit(solution)/shard_map/ppermute | solution.py:236
  50.7 8.5 %collective-permute-start.2 = (bf16[128,1280]{1,0:T(8,128)(2,1)S(1)}, bf16[128,1280]{1,0:T(8,128)(2,1)}, u32[]{:S(2)}, u32[]{:S(2)}) collective-permute-start(bf16[128,1280]{1,0:T(8,128)(2,1)S(1)} %slice.8), channel_id=1, source_target_pairs={{0,32},{32,64},{64,96},{96,0},{1,33},{33,65},{65,97},{97,1},{2,34}... | collective-permute-start | bytes 983048 | tf_op jit(solution)/shard_map/ppermute | solution.py:235
  50.8 8.5 %collective-permute-start.6 = (bf16[256,1280]{1,0:T(8,128)(2,1)}, bf16[256,1280]{1,0:T(8,128)(2,1)}, u32[]{:S(2)}, u32[]{:S(2)}) collective-permute-start(bf16[256,1280]{1,0:T(8,128)(2,1)} %collective-permute-done.1.rest_2_), channel_id=1, source_target_pairs={{0,8},{8,0},{1,9},{9,1},{2,10},{10,2},{3,11},{11,3},{4,12},{12,4},... | collective-permute-start | bytes 1966088 | tf_op jit(solution)/shard_map/ppermute | solution.py:238
  50.9 10.3 %collective-permute-start.5 = (bf16[256,1280]{1,0:T(8,128)(2,1)}, bf16[256,1280]{1,0:T(8,128)(2,1)}, u32[]{:S(2)}, u32[]{:S(2)}) collective-permute-start(bf16[256,1280]{1,0:T(8,128)(2,1)} %collective-permute-done.rest_1_), channel_id=1, source_target_pairs={{0,8},{8,0},{1,9},{9,1},{2,10},{10,2},{3,11},{11,3},{4,12},{12,4},... | collective-permute-start | bytes 1966088 | tf_op jit(solution)/shard_map/ppermute | solution.py:238
  54.4 4.8 %collective-permute-start.8 = (bf16[128,1280]{1,0:T(8,128)(2,1)}, bf16[128,1280]{1,0:T(8,128)(2,1)}, u32[]{:S(2)}, u32[]{:S(2)}) collective-permute-start(bf16[128,1280]{1,0:T(8,128)(2,1)} %collective-permute-done.3.rest_4_), channel_id=1, source_target_pairs={{0,8},{8,0},{1,9},{9,1},{2,10},{10,2},{3,11},{11,3},{4,12},{12,4},... | collective-permute-start | bytes 983048 | tf_op jit(solution)/shard_map/ppermute | solution.py:238
  59.1 2.0 %collective-permute-start.7 = (bf16[128,1280]{1,0:T(8,128)(2,1)}, bf16[128,1280]{1,0:T(8,128)(2,1)}, u32[]{:S(2)}, u32[]{:S(2)}) collective-permute-start(bf16[128,1280]{1,0:T(8,128)(2,1)} %collective-permute-done.2.rest_3_), channel_id=1, source_target_pairs={{0,8},{8,0},{1,9},{9,1},{2,10},{10,2},{3,11},{11,3},{4,12},{12,4},... | collective-permute-start | bytes 983048 | tf_op jit(solution)/shard_map/ppermute | solution.py:238
  77.9 23.2 %all-to-all-start.3 = ((bf16[8,8,5,16,128]{4,3,2,1,0:T(8,128)(2,1)}), bf16[8,8,5,16,128]{4,3,2,1,0:T(8,128)(2,1)}, u32[]{:S(2)}, u32[]{:S(2)}) async-start(bf16[8,8,5,16,128]{4,3,2,1,0:T(8,128)(2,1)} %attend.3), calls=%async_computation.3 | async-start | bytes 2621440 | tf_op jit(solution)/shard_map/all_to_all | solution.py:272
  101.1 21.2 %all-to-all-start.2 = ((bf16[8,8,5,16,128]{4,3,2,1,0:T(8,128)(2,1)}), bf16[8,8,5,16,128]{4,3,2,1,0:T(8,128)(2,1)S(1)}, u32[]{:S(2)}, u32[]{:S(2)}) async-start(bf16[8,8,5,16,128]{4,3,2,1,0:T(8,128)(2,1)} %attend.2), calls=%async_computation.2 | async-start | bytes 2621440 | tf_op jit(solution)/shard_map/all_to_all | solution.py:272
